TPU v7x, 32 devices: a whole 2x2x4 slice. The times are simulated.
32 devices in a mesh: graph: 32 (over z, y, x, core).
Axes of the slice: x: 2, y: 2, z: 4, core: 2. Of those that a mesh axis runs over, the one named last changes fastest.
Arguments:
- node_feats: bfloat16 [65536, 500], P('graph')
- w_one: float32 [500, 256], replicated
- w_two: float32 [256, 7], replicated
- send_idx: int32 [64, 1024], P('graph')
- edge_src: int32 [262144], P('graph')
- edge_dst: int32 [262144], P('graph')
- edge_w: float32 [262144], P('graph')
- labels: int32 [65536], P('graph')
- label_mask: int32 [65536], P('graph')
Outputs:
- output 1: float32 [], replicated
- output 2: float32 [500, 256], replicated
- output 3: float32 [256, 7], replicated
All inputs are finite; a program needn't handle non-finite values.
Results may differ from a plain program's by a relative error of at most 0.001.
Values are sent between devices in bfloat16 or wider.
A program may use at most 1 GiB of HBM per device.

v0:
```python
import jax
import jax.numpy as jnp
from jax import lax
from jax.sharding import PartitionSpec as P

GRAPH_AXIS = "graph"
CONTRACT_ROWS = (((0,), (0,)), ((), ()))
CONTRACT_COLS = (((1,), (1,)), ((), ()))


def solution(mesh):
    num_dev = mesh.shape[GRAPH_AXIS]
    to_next = [(dev_id, (dev_id + 1) % num_dev) for dev_id in range(num_dev)]
    to_prev = [(dev_id, (dev_id - 1) % num_dev) for dev_id in range(num_dev)]

    def halo_extend(node_table, send_rows):
        from_prev = lax.ppermute(node_table[send_rows[1]], GRAPH_AXIS, to_next)
        from_next = lax.ppermute(node_table[send_rows[0]], GRAPH_AXIS, to_prev)
        return jnp.concatenate([node_table, from_prev, from_next], axis=0)

    def aggregate(ext_table, edge_src, edge_dst, edge_w, rows_loc):
        return jax.ops.segment_sum(edge_w[:, None] * ext_table[edge_src], edge_dst, num_segments=rows_loc)

    def scatter_back(grad_rows, send_rows, edge_src, edge_dst, edge_w):
        rows_loc = grad_rows.shape[0]
        halo_rows = send_rows.shape[1]
        ext_grad = jax.ops.segment_sum(edge_w[:, None] * grad_rows[edge_dst], edge_src, num_segments=rows_loc + 2 * halo_rows)
        back_prev = lax.ppermute(ext_grad[rows_loc:rows_loc + halo_rows], GRAPH_AXIS, to_prev)
        back_next = lax.ppermute(ext_grad[rows_loc + halo_rows:], GRAPH_AXIS, to_next)
        row_ids = jnp.concatenate([send_rows[1], send_rows[0]])
        return ext_grad[:rows_loc].at[row_ids].add(jnp.concatenate([back_prev, back_next], axis=0))

    def device_step(node_feats, w_one, w_two, send_rows, edge_src, edge_dst, edge_w, labels, label_mask):
        rows_loc = node_feats.shape[0]
        w_one_b = w_one.astype(jnp.bfloat16)
        w_two_b = w_two.astype(jnp.bfloat16)
        tab_one = jnp.dot(node_feats, w_one_b, preferred_element_type=jnp.float32).astype(jnp.bfloat16)
        pre_one = aggregate(halo_extend(tab_one, send_rows), edge_src, edge_dst, edge_w, rows_loc)
        hidden = jnp.maximum(pre_one, 0.0).astype(jnp.bfloat16)
        tab_two = jnp.dot(hidden, w_two_b, preferred_element_type=jnp.float32).astype(jnp.bfloat16)
        logits = aggregate(halo_extend(tab_two, send_rows), edge_src, edge_dst, edge_w, rows_loc)
        mask_f = label_mask.astype(jnp.float32)
        label_count = jnp.maximum(lax.psum(jnp.sum(mask_f), GRAPH_AXIS), 1.0)
        log_norm = jax.nn.logsumexp(logits, axis=1)
        one_hot = (labels[:, None] == jnp.arange(logits.shape[1])[None, :]).astype(jnp.float32)
        picked = jnp.sum(logits * one_hot, axis=1)
        mean_loss = lax.psum(jnp.sum(mask_f * (log_norm - picked)), GRAPH_AXIS) / label_count
        d_logits = (jnp.exp(logits - log_norm[:, None]) - one_hot) * (mask_f / label_count)[:, None]
        d_tab_two = scatter_back(d_logits, send_rows, edge_src, edge_dst, edge_w).astype(jnp.bfloat16)
        grad_two = lax.psum(lax.dot_general(hidden, d_tab_two, CONTRACT_ROWS, preferred_element_type=jnp.float32), GRAPH_AXIS)
        d_hidden = lax.dot_general(d_tab_two, w_two_b, CONTRACT_COLS, preferred_element_type=jnp.float32)
        d_pre = jnp.where(pre_one > 0.0, d_hidden, 0.0)
        d_tab_one = scatter_back(d_pre, send_rows, edge_src, edge_dst, edge_w).astype(jnp.bfloat16)
        grad_one = lax.psum(lax.dot_general(node_feats, d_tab_one, CONTRACT_ROWS, preferred_element_type=jnp.float32), GRAPH_AXIS)
        return mean_loss, grad_one, grad_two

    row_spec = P(GRAPH_AXIS)
    return jax.shard_map(device_step, mesh=mesh, in_specs=(row_spec, P(), P(), row_spec, row_spec, row_spec, row_spec, row_spec, row_spec), out_specs=(P(), P(), P()), check_vma=False)
```

profile of v0, /device:TPU:0, one launch (start us, length us, event | category | flops | bytes accessed | tf_op | source)
XLA Modules:
  0.0 704.3 jit_solution(12854137965560059576)
XLA Ops:
  7.2 0.9 compare_select_fusion.5
  8.1 0.7 copy-done
  8.8 1.9 convolution_convert_fusion
  10.7 4.9 gather_fusion
  15.6 0.5 collective-permute-start
  16.1 5.0 gather_fusion.1
  21.1 5.9 collective-permute-start.1
  27.1 1.8 collective-permute-done
  28.9 4.8 collective-permute-done.1
  33.7 2.5 pad_maximum_fusion
  36.2 100.8 %scatter_custom_fusion = f32[2048,256]{1,0:T(8,128)} fusion(s32[8192]{0:T(1024)S(1)} %copy-done.7, f32[8192]{0:T(1024)S(1)} %copy-done.2, f32[]{:T(128)} %constant.6.clone.1, bf16[4096,256]{1,0:T(8,128)(2,1)} %pad_maximum_fusion, s32[8192]{0:T(1024)S(1)} %fusion.34), kind=kCustom, calls=%fused_computation.16 | custom fusion | flops 6291456 | bytes 4259844 | tf_op jit(solution)/shard_map/scatter-add | solution.py:22
  137.0 2.0 convolution_convert_fusion.1
  139.0 0.3 copy.35
  139.3 3.2 gather_fusion.3
  142.5 3.2 gather_fusion.2
  145.8 0.1 copy.36
  145.9 0.1 copy.38
  146.0 5.6 collective-permute-start.3
  151.7 1.4 collective-permute-done.3
  153.1 5.3 collective-permute-done.2
  158.5 1.4 copy.39
  159.9 93.7 %scatter_custom_fusion.1 = f32[2048,7]{1,0:T(8,128)S(1)} fusion(s32[8192]{0:T(1024)S(1)} %copy-done.7, f32[8192]{0:T(1024)S(1)} %copy-done.2, f32[]{:T(128)} %constant.6.clone.1, bf16[4096,7]{1,0:T(8,128)(2,1)} %copy.39, s32[8192]{0:T(1024)S(1)} %fusion.34), kind=kCustom, calls=%fused_computation.21 | custom fusion | flops 172032 | bytes 180228 | tf_op jit(solution)/shard_map/scatter-add | solution.py:22
  253.5 0.3 reduce_max.9
  253.9 1.3 select_reduce_fusion
  255.2 0.6 convert_reduce_fusion
  255.8 37.0 %psum.29 = f32[]{:T(128)} all-reduce(f32[]{:T(128)} %get-tuple-element.5), channel_id=1, replica_groups=mesh['graph'=32] {'graph'}, use_global_device_ids=true, to_apply=%region_8.0 | all-reduce | flops 1 | bytes 8 | tf_op jit(solution)/shard_map/psum | solution.py:43
  293.5 2.5 subtract_multiply_fusion
  295.9 95.5 %scatter_custom_fusion.2 = f32[4096,7]{1,0:T(8,128)} fusion(s32[8192]{0:T(1024)S(1)} %copy-done.8, f32[8192]{0:T(1024)S(1)} %copy-done.2, f32[]{:T(128)} %constant.6.clone.1, f32[2048,7]{1,0:T(8,128)} %subtract_multiply_fusion, s32[8192]{0:T(1024)S(1)} %fusion.35), kind=kCustom, calls=%fused_computation.19 | custom fusion | flops 114688 | bytes 237572 | tf_op jit(solution)/shard_map/scatter-add | solution.py:27
  391.4 1.4 fusion.45
  392.8 2.8 collective-permute-start.4
  395.6 6.7 collective-permute-done.4
  402.3 5.5 collective-permute-done.5
  407.8 0.8 copy-done.4
  408.6 12.8 %scatter_custom_fusion.3 = f32[2048,7]{1,0:T(8,128)S(1)} fusion(f32[2048,7]{1,0:T(8,128)S(1)} %slice-done, s32[2048]{0:T(1024)S(1)} %bitcast.17, f32[1024,7]{1,0:T(8,128)} %copy-done.4, f32[]{:T(128)} %constant.10.clone.1, f32[1024,7]{1,0:T(8,128)} %copy-done.3), kind=kCustom, calls=%fused_computation.39 | custom fusion | flops 28672 | bytes 114692 | tf_op jit(solution)/shard_map/scatter-add | solution.py:31
  421.4 3.3 compare_select_fusion
  424.7 95.0 %scatter_custom_fusion.4 = f32[4096,256]{1,0:T(8,128)} fusion(s32[8192]{0:T(1024)S(1)} %copy-done.8, f32[8192]{0:T(1024)S(1)} %copy-done.2, f32[]{:T(128)} %constant.6.clone.1, f32[2048,256]{1,0:T(8,128)} %compare_select_fusion, s32[8192]{0:T(1024)S(1)} %fusion.35), kind=kCustom, calls=%fused_computation.14 | custom fusion | flops 4194304 | bytes 6356996 | tf_op jit(solution)/shard_map/scatter-add | solution.py:27
  519.8 1.8 fusion.44
  521.6 0.9 collective-permute-start.6
  522.5 0.1 copy-done.1
  522.6 1.5 slice.57
  524.1 10.8 %collective-permute-done.6 = f32[1024,256]{1,0:T(8,128)} collective-permute-done((f32[1024,256]{1,0:T(8,128)S(1)}, f32[1024,256]{1,0:T(8,128)}, u32[]{:S(2)}, u32[]{:S(2)}) %collective-permute-start.6) | collective-permute-done | bytes 1048608 | tf_op jit(solution)/shard_map/ppermute | solution.py:28
  534.9 5.5 collective-permute-done.7
  540.4 15.2 %scatter_custom_fusion.5 = f32[2048,256]{1,0:T(8,128)} fusion(f32[2048,256]{1,0:T(8,128)} %slice.57, s32[2048]{0:T(1024)S(1)} %bitcast.18, f32[1024,256]{1,0:T(8,128)} %collective-permute-done.7, f32[]{:T(128)} %constant.10.clone.1, f32[1024,256]{1,0:T(8,128)} %collective-permute-done.6), kind=kCustom, calls=%fused_computation.29 | custom fusion | flops 1048576 | bytes 4194816 | tf_op jit(solution)/shard_map/scatter-add | solution.py:31
  555.6 3.1 convolution_bitcast_fusion
  558.7 1.9 fusion.27
  560.6 47.6 %all-reduce = (f32[]{:T(128)}, f32[256,7]{0,1:T(8,128)}) all-reduce(f32[]{:T(128)} %get-tuple-element.6, f32[256,7]{0,1:T(8,128)S(1)} %fusion.27), channel_id=1, replica_groups=mesh['graph'=32] {'graph'}, use_global_device_ids=true, to_apply=%region_6.0 | all-reduce | flops 1793 | bytes 14344 | tf_op jit(solution)/shard_map/psum | solution.py:47
  608.8 85.6 %all-reduce.3.cloned.1.call-done = f32[500,256]{1,0:T(8,128)} async-done(((f32[500,256]{1,0:T(8,128)}), f32[500,256]{1,0:T(8,128)}) %all-reduce.3.cloned.1.call-update) | async-done | bytes 512016 | tf_op jit(solution)/shard_map/psum | solution.py:54
  694.4 1.9 copy.43
  (35 shorter events, 0.2 us)
Async XLA Ops:
  7.2 1.6 copy-start
  7.2 687.3 %all-reduce.3.cloned.1.call-start = ((), (), s32[]{:S(2)}) async-start(), calls=%async_computation | async-start | bytes 1032192 | tf_op jit(solution)/shard_map/psum | solution.py:54
  15.6 13.3 %collective-permute-start = (bf16[1024,256]{1,0:T(8,128)(2,1)}, bf16[1024,256]{1,0:T(8,128)(2,1)}, u32[]{:S(2)}, u32[]{:S(2)}) collective-permute-start(bf16[1024,256]{1,0:T(8,128)(2,1)} %gather_fusion), channel_id=1, source_target_pairs={{0,1},{1,2},{2,3},{3,4},{4,5},{5,6},{6,7},{7,8},{8,9},{9,10},{10,1... | collective-permute-start | bytes 1572872 | tf_op jit(solution)/shard_map/ppermute | solution.py:17
  16.1 10.9 %copy-start.8 = (s32[8192]{0:T(1024)S(1)}, s32[8192]{0:T(1024)}, u32[]{:S(2)}) copy-start(s32[8192]{0:T(1024)} %param.13) | copy-start | bytes 98308
  16.1 10.9 %copy-start.7 = (s32[8192]{0:T(1024)S(1)}, s32[8192]{0:T(1024)}, u32[]{:S(2)}) copy-start(s32[8192]{0:T(1024)} %param.14) | copy-start | bytes 98308
  21.1 12.6 %collective-permute-start.1 = (bf16[1024,256]{1,0:T(8,128)(2,1)}, bf16[1024,256]{1,0:T(8,128)(2,1)S(1)}, u32[]{:S(2)}, u32[]{:S(2)}) collective-permute-start(bf16[1024,256]{1,0:T(8,128)(2,1)} %gather_fusion.1), channel_id=1, source_target_pairs={{0,31},{1,0},{2,1},{3,2},{4,3},{5,4},{6,5},{7,6},{8,7},{9,8},{10,9... | collective-permute-start | bytes 1572872 | tf_op jit(solution)/shard_map/ppermute | solution.py:18
  27.1 9.2 %copy-start.2 = (f32[8192]{0:T(1024)S(1)}, f32[8192]{0:T(1024)}, u32[]{:S(2)}) copy-start(f32[8192]{0:T(1024)} %param.15) | copy-start | bytes 98308
  36.2 100.8 %copy-start.6 = (f32[256,7]{0,1:T(8,128)S(1)}, f32[256,7]{0,1:T(8,128)}, u32[]{:S(2)}) copy-start(f32[256,7]{0,1:T(8,128)} %param.11) | copy-start | bytes 21508
  139.3 12.3 %copy-start.9 = (s32[2,1024]{1,0:T(2,128)S(1)}, s32[2,1024]{1,0:T(2,128)}, u32[]{:S(2)}) copy-start(s32[2,1024]{1,0:T(2,128)} %param.12) | copy-start | bytes 24580
  146.0 7.1 %collective-permute-start.3 = (bf16[1024,7]{0,1:T(8,128)(2,1)S(1)}, bf16[1024,7]{0,1:T(8,128)(2,1)S(1)}, u32[]{:S(2)}, u32[]{:S(2)}) collective-permute-start(bf16[1024,7]{0,1:T(8,128)(2,1)S(1)} %copy.38), channel_id=1, source_target_pairs={{0,31},{1,0},{2,1},{3,2},{4,3},{5,4},{6,5},{7,6},{8,7},{9,8},{10,9... | collective-permute-start | bytes 43016 | tf_op jit(solution)/shard_map/ppermute | solution.py:18
  151.7 6.8 collective-permute-start.2
  158.4 95.4 %copy-start.5 = (s32[2048]{0:T(1024)S(1)}, s32[2048]{0:T(1024)}, u32[]{:S(2)}) copy-start(s32[2048]{0:T(1024)} %param.16) | copy-start | bytes 24580
  159.9 95.3 %copy-start.10 = (s32[2048]{0:T(1024)S(1)}, s32[2048]{0:T(1024)}, u32[]{:S(2)}) copy-start(s32[2048]{0:T(1024)} %param.17) | copy-start | bytes 24580
  391.4 17.2 %slice-start = ((f32[4096,7]{1,0:T(8,128)}), f32[2048,7]{1,0:T(8,128)S(1)}, s32[]{:S(2)}) async-start(f32[4096,7]{1,0:T(8,128)} %scatter_custom_fusion.2), calls=%async_computation.1 | async-start | bytes 2097152 | tf_op jit(solution)/shard_map/slice | solution.py:31
  392.8 9.5 %collective-permute-start.4 = (f32[1024,7]{1,0:T(8,128)S(1)}, f32[1024,7]{1,0:T(8,128)S(1)}, u32[]{:S(2)}, u32[]{:S(2)}) collective-permute-start(f32[1024,7]{1,0:T(8,128)S(1)} %get-tuple-element.12), channel_id=1, source_target_pairs={{0,31},{1,0},{2,1},{3,2},{4,3},{5,4},{6,5},{7,6},{8,7},{9,8},{10,9... | collective-permute-start | bytes 86024 | tf_op jit(solution)/shard_map/ppermute | solution.py:28
  395.6 12.2 %collective-permute-start.5 = (f32[1024,7]{1,0:T(8,128)S(1)}, f32[1024,7]{1,0:T(8,128)S(1)}, u32[]{:S(2)}, u32[]{:S(2)}) collective-permute-start(f32[1024,7]{1,0:T(8,128)S(1)} %get-tuple-element.13), channel_id=1, source_target_pairs={{0,1},{1,2},{2,3},{3,4},{4,5},{5,6},{6,7},{7,8},{8,9},{9,10},{10,1... | collective-permute-start | bytes 86024 | tf_op jit(solution)/shard_map/ppermute | solution.py:29
  402.3 5.5 copy-start.3
  407.8 0.8 copy-start.4
  519.8 2.8 copy-start.1
  521.6 13.3 %collective-permute-start.6 = (f32[1024,256]{1,0:T(8,128)S(1)}, f32[1024,256]{1,0:T(8,128)}, u32[]{:S(2)}, u32[]{:S(2)}) collective-permute-start(f32[1024,256]{1,0:T(8,128)S(1)} %get-tuple-element.10), channel_id=1, source_target_pairs={{0,31},{1,0},{2,1},{3,2},{4,3},{5,4},{6,5},{7,6},{8,7},{9,8},{10,9... | collective-permute-start | bytes 3145736 | tf_op jit(solution)/shard_map/ppermute | solution.py:28
  522.5 17.9 %collective-permute-start.7 = (f32[1024,256]{1,0:T(8,128)S(1)}, f32[1024,256]{1,0:T(8,128)}, u32[]{:S(2)}, u32[]{:S(2)}) collective-permute-start(f32[1024,256]{1,0:T(8,128)S(1)} %get-tuple-element.11), channel_id=1, source_target_pairs={{0,1},{1,2},{2,3},{3,4},{4,5},{5,6},{6,7},{7,8},{8,9},{9,10},{10,1... | collective-permute-start | bytes 3145736 | tf_op jit(solution)/shard_map/ppermute | solution.py:29
Sparse Core Ops, SparseCore 0:
  558.8 135.5 all-reduce.2
where the time goes:
time: 706 us; the launch traced here: 704 us
  other arithmetic  421 us (60%)
  waiting for transfers between devices  127 us (18%)
  blocking collectives  84.6 us (12%)
  local copies, waits for them, and re-layouts  26.5 us (4%)
  between operations  16.7 us (2%)
  starting transfers between devices  15.9 us (2%)
  matrix products  12.1 us (2%)
    scatter-add x2, other arithmetic, aggregate(): jax.ops.segment_sum(edge_w[:, None] * ext_table[edge_src], edge_dst, num_...  194 us
    scatter-add x2, other arithmetic, scatter_back(): jax.ops.segment_sum(edge_w[:, None] * grad_rows[edge_dst], edge_src, num_...  190 us
    psum x1, waiting for transfers between devices, device_step(): lax.psum(lax.dot_general(node_feats, d_tab_one, CONTRACT_ROWS, preferred_...  85.6 us
    psum x1, blocking collectives, device_step(): lax.psum(jnp.sum(mask_f * (log_norm - picked)), GRAPH_AXIS) / label_count  47.6 us
    psum x1, blocking collectives, device_step(): label_count = jnp.maximum(lax.psum(jnp.sum(mask_f), GRAPH_AXIS), 1.0)  37 us
    scatter-add x2, other arithmetic, scatter_back(): ext_grad[:rows_loc].at[row_ids]  28 us
    ppermute x2, waiting for transfers between devices, scatter_back(): lax.ppermute(ext_grad[rows_loc:rows_loc + halo_rows], GRAPH_AXIS, to_prev)  17.5 us
  transfers between devices with their start and end apart: 9, of which 9 were waited for; matrix products, arithmetic and copies ran while one was open for 1% of the time, Pallas kernels for 0%

commit v1 on v0

v1 whole, which is shorter than its diff:
```python
import functools

import jax
import jax.numpy as jnp
from jax import lax
from jax.experimental import pallas as pl
from jax.experimental.pallas import tpu as pltpu
from jax.sharding import PartitionSpec as P

GRAPH_AXIS = "graph"
MESH = pl.DeviceIdType.MESH
LANES = 128
CLASS_ROWS = 8
VMEM_BYTES = 60 * 2**20
F32 = jnp.float32
BF16 = jnp.bfloat16
NT = (((1,), (1,)), ((), ()))


def vmem():
    return pl.BlockSpec(memory_space=pltpu.VMEM)


def smem():
    return pl.BlockSpec(memory_space=pltpu.SMEM)


def flip(me, bit):
    return me + bit * (1 - 2 * ((me // bit) % 2))


def meet(partners):
    barrier = pltpu.get_barrier_semaphore()
    for dev in partners:
        pl.semaphore_signal(barrier, inc=1, device_id=(dev,), device_id_type=MESH)
    pl.semaphore_wait(barrier, len(partners))


def remote(src, dst, sems, slot, dev):
    return pltpu.make_async_remote_copy(
        src_ref=src, dst_ref=dst, send_sem=sems.at[0, slot], recv_sem=sems.at[1, slot],
        device_id=(dev,), device_id_type=MESH)


def three_pieces(val):
    top = val.astype(BF16).astype(F32)
    rest = val - top
    mid = rest.astype(BF16).astype(F32)
    return top, mid, rest - mid


def k1_body(num_dev, bits, x_ref, w_ref, send_ref, mask_ref, own_ref, halo_ref, cnt_ref,
            stage, cnt_send, cnt_recv, sems, cnt_sems):
    me = lax.axis_index(GRAPH_AXIS)
    nxt, prv = (me + 1) % num_dev, (me + num_dev - 1) % num_dev
    partners = [flip(me, b) for b in bits]
    meet([nxt, prv] + partners)
    rows = own_ref.shape[0]
    halo = send_ref.shape[1]
    own_ref[...] = jnp.dot(x_ref[...], w_ref[...].astype(BF16), preferred_element_type=F32).astype(BF16)

    blocks = halo // LANES
    ids = jnp.concatenate([send_ref[r:r + 1, b * LANES:(b + 1) * LANES] for r in range(2) for b in range(blocks)], axis=0)
    ids_col = jnp.transpose(ids)
    node = lax.broadcasted_iota(jnp.int32, (LANES, rows), 1)
    copies = []
    half = halo // 2
    for part in range(2):
        for r in (1, 0):
            for b in range(part * blocks // 2, (part + 1) * blocks // 2):
                col = ids_col[:, r * blocks + b:r * blocks + b + 1]
                pick = (node == col).astype(F32).astype(BF16)
                stage[pl.ds(r * halo + b * LANES, LANES), :] = jnp.dot(
                    pick, own_ref[...], preferred_element_type=F32).astype(BF16)
            dst_row = (1 - r) * halo + part * half
            copy = remote(stage.at[pl.ds(r * halo + part * half, half), :], halo_ref.at[pl.ds(dst_row, half), :],
                          sems, 2 * part + r, nxt if r == 1 else prv)
            copy.start()
            copies.append(copy)

    total = jnp.sum(jnp.sum(mask_ref[...].astype(F32), axis=1, keepdims=True), axis=0, keepdims=True)
    total = jnp.broadcast_to(total, cnt_ref.shape)
    for i, dev in enumerate(partners):
        cnt_send[i] = total
        copy = remote(cnt_send.at[i], cnt_recv.at[i], cnt_sems, i, dev)
        copy.start()
        copy.wait()
        total = total + cnt_recv[i]
    cnt_ref[...] = jnp.maximum(total, 1.0)
    for copy in copies:
        copy.wait()


def spread_weights(w_ref, wide):
    wt = jnp.transpose(w_ref[...])
    for b in range(w_ref.shape[0]):
        wide[pl.ds(b * LANES, LANES), :] = jnp.broadcast_to(wt[:, b:b + 1], (LANES, LANES))


def row_loop(pair_ref, wide, table, bufs, swap, unroll):
    def clear(i, carry):
        for buf in bufs:
            buf[pl.ds(i * 64, 64), :] = jnp.zeros((64, LANES), F32)
        return carry

    lax.fori_loop(0, bufs[0].shape[0] // 64, clear, 0)
    num = len(bufs)

    def step(i, carry):
        base = i * unroll
        for first in range(0, unroll, num):
            pairs = [pair_ref[base + first + j] for j in range(num)]
            low = [pl.multiple_of(p & 0xFFFF, 2) for p in pairs]
            high = [pl.multiple_of(lax.shift_right_logical(p, 16), 2) for p in pairs]
            take, put = (high, low) if swap else (low, high)
            vals = [wide[pl.ds(base + first + j, 1), :] * table[pl.ds(take[j], 2), :] for j in range(num)]
            old = [bufs[j][pl.ds(put[j], 2), :] for j in range(num)]
            for j in range(num):
                bufs[j][pl.ds(put[j], 2), :] = old[j] + vals[j]
        return carry

    lax.fori_loop(0, wide.shape[0] // unroll, step, 0)


def to_rows(src_ref, table, first_row):
    def body(i, carry):
        blk = src_ref[pl.ds(pl.multiple_of(i * LANES, LANES), LANES), :].astype(F32)
        for h in range(2):
            table[pl.ds(2 * first_row + 2 * i * LANES + h, LANES, stride=2), :] = blk[:, h * LANES:(h + 1) * LANES]
        return carry

    lax.fori_loop(0, src_ref.shape[0] // LANES, body, 0)


def sum_rows(bufs, blk):
    halves = []
    for h in range(2):
        parts = [buf[pl.ds(2 * blk * LANES + h, LANES, stride=2), :] for buf in bufs]
        while len(parts) > 1:
            parts = [a + b for a, b in zip(parts[::2], parts[1::2])]
        halves.append(parts[0])
    return jnp.concatenate(halves, axis=1)


def k2_body(unroll, own_ref, halo_ref, pair_ref, w_ref, w2t_ref, hid_ref, pos_ref, tab_ref, table, wide, *bufs):
    spread_weights(w_ref, wide)
    to_rows(own_ref, table, 0)
    to_rows(halo_ref, table, own_ref.shape[0])
    row_loop(pair_ref, wide, table, bufs, False, unroll)

    def finish(i, carry):
        pre = sum_rows(bufs, i)
        hid = jnp.maximum(pre, 0.0).astype(BF16)
        at = pl.ds(pl.multiple_of(i * LANES, LANES), LANES)
        hid_ref[at, :] = hid
        pos_ref[at, :] = (pre > 0.0).astype(F32).astype(BF16)
        t2 = lax.dot_general(w2t_ref[...], hid, NT, preferred_element_type=F32)
        tab_ref[pl.ds(pl.multiple_of(i * CLASS_ROWS, CLASS_ROWS), CLASS_ROWS), :] = t2.astype(BF16).astype(F32)
        return carry

    lax.fori_loop(0, hid_ref.shape[0] // LANES, finish, 0)


def k4_body(unroll, dy_ref, pair_ref, w_ref, ext_ref, table, wide, *bufs):
    spread_weights(w_ref, wide)
    to_rows(dy_ref, table, 0)
    row_loop(pair_ref, wide, table, bufs, True, unroll)

    def finish(i, carry):
        ext_ref[pl.ds(pl.multiple_of(i * LANES, LANES), LANES), :] = sum_rows(bufs, i)
        return carry

    lax.fori_loop(0, ext_ref.shape[0] // LANES, finish, 0)


def wide_row(ref, first):
    blk = ref[pl.ds(first, 8), :]
    return jnp.concatenate([blk[j:j + 1, :] for j in range(8)], axis=1)


def lo_hot(idx):
    lo = idx & (LANES - 1)
    node = lax.broadcasted_iota(jnp.int32, (LANES, idx.shape[1]), 0)
    return (node == lo).astype(F32).astype(BF16)


def hi_of(idx):
    return jnp.broadcast_to(lax.shift_right_logical(idx, 7), (CLASS_ROWS, idx.shape[1]))


def pick_cols(table_b, pieces, idx, hot):
    cols = jnp.dot(table_b, hot, preferred_element_type=F32)
    rows = table_b.shape[0] // pieces
    hi = hi_of(idx)
    out = jnp.zeros(hi.shape, F32)
    for h in range(rows // CLASS_ROWS):
        part = cols[h * CLASS_ROWS:(h + 1) * CLASS_ROWS]
        for p in range(1, pieces):
            part = part + cols[p * rows + h * CLASS_ROWS:p * rows + (h + 1) * CLASS_ROWS]
        out = out + jnp.where(hi == h, part, 0.0)
    return out


def add_cols(val, idx, hot, num_hi):
    hi = hi_of(idx)
    pieces = three_pieces(val)
    rows = []
    for h in range(0, num_hi, 2):
        both = [jnp.where(hi == h + k, p, 0.0) for k in range(2) for p in pieces]
        rows.append(jnp.concatenate(both, axis=0).astype(BF16))
    return lax.dot_general(jnp.concatenate(rows, axis=0), hot, NT, preferred_element_type=F32)


def join_pieces(acc, num_hi):
    out = []
    for h in range(num_hi):
        a = acc[h * 24:h * 24 + 24, :]
        out.append(a[0:8] + a[8:16] + a[16:24])
    return out


def stack_pieces(val):
    return jnp.concatenate(three_pieces(val), axis=0).astype(BF16)


def k3_body(num_dev, tab_ref, send_ref, src_ref, dst_ref, w_ref, lab_ref, mask_ref, cnt_ref, hid_ref, pos_ref, w2t_ref,
            dy_ref, misc_ref, ext_b, fwd_send, fwd_recv, bwd_send, bwd_recv, acc_z, acc_s, acc_r, dz_b, sems):
    me = lax.axis_index(GRAPH_AXIS)
    nxt, prv = (me + 1) % num_dev, (me + num_dev - 1) % num_dev
    meet([nxt, prv])
    own_hi = tab_ref.shape[0] // CLASS_ROWS
    halo = send_ref.shape[1]
    halo_hi = halo // LANES
    all_hi = own_hi + 2 * halo_hi
    own_b = tab_ref[...].astype(BF16)
    ext_b[pl.ds(0, own_hi * CLASS_ROWS), :] = own_b
    hot_send = [lo_hot(send_ref[r:r + 1, :]) for r in range(2)]
    copies = []
    for r in (1, 0):
        val = pick_cols(own_b, 1, send_ref[r:r + 1, :], hot_send[r])
        fwd_send[r] = jnp.concatenate([val, jnp.zeros_like(val)], axis=0).astype(BF16)
        copy = remote(fwd_send.at[r], fwd_recv.at[1 - r], sems, r, nxt if r == 1 else prv)
        copy.start()
        copies.append(copy)
    acc_z[...] = jnp.zeros_like(acc_z)
    acc_s[...] = jnp.zeros_like(acc_s)
    for copy in copies:
        copy.wait()
    for r in range(2):
        got = fwd_recv[r].astype(F32)
        for j in range(0, halo_hi, 2):
            two = jnp.concatenate([got[0:8, (j + k) * LANES:(j + k + 1) * LANES] for k in range(2)], axis=0)
            ext_b[pl.ds((own_hi + r * halo_hi + j) * CLASS_ROWS, 16), :] = two.astype(BF16)

    steps = src_ref.shape[0] // 8

    def forward(i, carry):
        first = pl.multiple_of(i * 8, 8)
        src, dst = wide_row(src_ref, first), wide_row(dst_ref, first)
        val = pick_cols(ext_b[...], 1, src, lo_hot(src)) * wide_row(w_ref, first)
        acc_z[...] += add_cols(val, dst, lo_hot(dst), own_hi)
        return carry

    lax.fori_loop(0, steps, forward, 0)

    logits = join_pieces(acc_z[...], own_hi)
    cls = lax.broadcasted_iota(jnp.int32, (CLASS_ROWS, LANES), 0)
    count = cnt_ref[0:1, :]
    loss = jnp.zeros((1, LANES), F32)
    d_log = []
    for h in range(own_hi):
        z = jnp.where(cls < 7, logits[h], -jnp.inf)
        top = jnp.max(z, axis=0, keepdims=True)
        norm = jnp.log(jnp.sum(jnp.exp(z - top), axis=0, keepdims=True)) + top
        hot = cls == lab_ref[h:h + 1, :]
        mask = mask_ref[h:h + 1, :].astype(F32)
        picked = jnp.sum(jnp.where(hot, logits[h], 0.0), axis=0, keepdims=True)
        loss = loss + mask * (norm - picked)
        d_log.append((jnp.exp(z - norm) - hot.astype(F32)) * (mask / count))
    dz_b[...] = stack_pieces(jnp.concatenate(d_log, axis=0))

    def backward(i, carry):
        first = pl.multiple_of(i * 8, 8)
        src, dst = wide_row(src_ref, first), wide_row(dst_ref, first)
        val = pick_cols(dz_b[...], 3, dst, lo_hot(dst)) * wide_row(w_ref, first)
        acc_s[...] += add_cols(val, src, lo_hot(src), all_hi)
        return carry

    lax.fori_loop(0, steps, backward, 0)

    d_ext = join_pieces(acc_s[...], all_hi)
    copies = []
    for r in range(2):
        for j in range(halo_hi):
            bwd_send[r, :, j * LANES:(j + 1) * LANES] = d_ext[own_hi + r * halo_hi + j]
        copy = remote(bwd_send.at[r], bwd_recv.at[1 - r], sems, 2 + r, prv if r == 0 else nxt)
        copy.start()
        copies.append(copy)
    for copy in copies:
        copy.wait()
    for r in range(2):
        part = add_cols(bwd_recv[r], send_ref[r:r + 1, :], hot_send[r], own_hi)
        acc_r[...] = part if r == 0 else acc_r[...] + part
    back = join_pieces(acc_r[...], own_hi)
    grad = jnp.zeros((CLASS_ROWS, hid_ref.shape[1]), F32)
    for h in range(own_hi):
        d_tab = d_ext[h] + back[h]
        d_tab_b = d_tab.astype(BF16)
        at = pl.ds(h * LANES, LANES)
        grad = grad + jnp.dot(d_tab_b, hid_ref[at, :], preferred_element_type=F32)
        d_hid = jnp.dot(jnp.transpose(d_tab).astype(BF16), w2t_ref[...], preferred_element_type=F32)
        dy_ref[at, :] = jnp.where(pos_ref[at, :].astype(F32) > 0.0, d_hid, 0.0)
    misc_ref[0:8, :] = grad
    total = jnp.sum(loss, axis=1, keepdims=True) / count[:, 0:1]
    misc_ref[8:16, :] = jnp.broadcast_to(total, (8, misc_ref.shape[1]))


def k5_body(num_dev, bits, x_ref, ext_ref, send_ref, misc_ref, grad_ref, tail_ref,
            xt, hot, recv, back, part, full, *rest):
    landing, (sems, sum_sems) = rest[:len(bits)], rest[len(bits):]
    me = lax.axis_index(GRAPH_AXIS)
    nxt, prv = (me + 1) % num_dev, (me + num_dev - 1) % num_dev
    partners = [flip(me, b) for b in bits]
    meet([nxt, prv] + partners)
    rows, feats = x_ref.shape
    halo = send_ref.shape[1]
    chunks = 4
    size = halo // chunks
    copies = []
    for q in range(chunks):
        for r in range(2):
            copy = remote(ext_ref.at[pl.ds(rows + r * halo + q * size, size), :],
                          recv.at[pl.ds((1 - r) * halo + q * size, size), :], sems, 2 * q + r, prv if r == 0 else nxt)
            copy.start()
            copies.append(copy)
    node = lax.broadcasted_iota(jnp.int32, (rows, size), 0)
    for r in range(2):
        for q in range(chunks):
            ids = send_ref[r:r + 1, q * size:(q + 1) * size]
            hot[:, r * halo + q * size:r * halo + (q + 1) * size] = (node == ids).astype(F32).astype(BF16)
    for b in range(4):
        lo, hi = b * LANES, min((b + 1) * LANES, feats)
        blk = x_ref[:, lo:hi].astype(F32)
        if hi - lo < LANES:
            blk = jnp.concatenate([blk, jnp.zeros((rows, LANES - (hi - lo)), F32)], axis=1)
        xt[lo:lo + LANES, :] = jnp.transpose(blk).astype(BF16)
    back[...] = ext_ref[pl.ds(0, rows), :]
    tile = 256
    for q in range(chunks):
        for r in range(2):
            copies[2 * q + r].wait()
        for r in range(2):
            first = r * halo + q * size
            val = recv[pl.ds(first, size), :]
            pieces = [p.astype(BF16) for p in three_pieces(val)]

            def add(i, carry):
                at = pl.ds(pl.multiple_of(i * tile, tile), tile)
                pick = hot[at, first:first + size]
                total = back[at, :]
                for p in pieces:
                    total = total + jnp.dot(pick, p, preferred_element_type=F32)
                back[at, :] = total
                return carry

            lax.fori_loop(0, rows // tile, add, 0)
    d_tab = back[...].astype(BF16)
    part[...] = jnp.dot(xt[...], d_tab, preferred_element_type=F32)
    part[feats:feats + 9, :] = misc_ref[0:9, :]

    offset = 0
    size = part.shape[0]
    for i, (bit, dev) in enumerate(zip(bits, partners)):
        size //= 2
        mine = (me // bit) % 2
        give = pl.multiple_of(offset + (1 - mine) * size, size)
        keep = pl.multiple_of(offset + mine * size, size)
        copy = remote(part.at[pl.ds(give, size), :], landing[i], sum_sems, i, dev)
        copy.start()
        copy.wait()
        part[pl.ds(keep, size), :] += landing[i][...]
        offset = keep
    full[pl.ds(offset, size), :] = part[pl.ds(offset, size), :]
    for i in range(len(bits) - 1, -1, -1):
        copy = remote(full.at[pl.ds(offset, size), :], full.at[pl.ds(offset, size), :], sum_sems, len(bits) + i, partners[i])
        copy.start()
        copy.wait()
        offset = pl.multiple_of(offset - ((me // bits[i]) % 2) * size, size)
        size *= 2
    grad_ref[...] = full[0:feats, :]
    tail_ref[...] = full[feats - 4:feats + 12, :]


def solution(mesh):
    num_dev = mesh.shape[GRAPH_AXIS]
    bits = []
    while 2 ** len(bits) < num_dev:
        bits.append(2 ** len(bits))

    def params(cid=None):
        if cid is None:
            return pltpu.CompilerParams(vmem_limit_bytes=VMEM_BYTES)
        return pltpu.CompilerParams(vmem_limit_bytes=VMEM_BYTES, collective_id=cid, has_side_effects=True)

    def device_step(node_feats, w_one, w_two, send_rows, edge_src, edge_dst, edge_w, labels, label_mask):
        rows, feats = node_feats.shape
        width = w_one.shape[1]
        classes = w_two.shape[1]
        halo = send_rows.shape[1]
        edges = edge_src.shape[0]
        own_hi, all_hi = rows // LANES, (rows + 2 * halo) // LANES
        w2t = jnp.zeros((CLASS_ROWS, width), BF16).at[:classes].set(w_two.astype(BF16).T)
        pair = edge_src * 2 + edge_dst * (2 << 16)
        src2, dst2, w2 = (a.reshape(edges // LANES, LANES) for a in (edge_src, edge_dst, edge_w))
        lab2, mask2 = labels.reshape(own_hi, LANES), label_mask.reshape(own_hi, LANES)

        own, halo_rows, count = pl.pallas_call(
            functools.partial(k1_body, num_dev, bits),
            out_shape=(jax.ShapeDtypeStruct((rows, width), BF16), jax.ShapeDtypeStruct((2 * halo, width), BF16),
                       jax.ShapeDtypeStruct((8, LANES), F32)),
            in_specs=[vmem()] * 4, out_specs=(vmem(),) * 3,
            scratch_shapes=[pltpu.VMEM((2 * halo, width), BF16), pltpu.VMEM((len(bits), 8, LANES), F32),
                            pltpu.VMEM((len(bits), 8, LANES), F32), pltpu.SemaphoreType.DMA((2, 4)),
                            pltpu.SemaphoreType.DMA((2, len(bits)))],
            compiler_params=params(0), name="transform_and_halo",
        )(node_feats, w_one, send_rows, mask2)

        hid, pos, tab = pl.pallas_call(
            functools.partial(k2_body, 32),
            out_shape=(jax.ShapeDtypeStruct((rows, width), BF16), jax.ShapeDtypeStruct((rows, width), BF16),
                       jax.ShapeDtypeStruct((own_hi * CLASS_ROWS, LANES), F32)),
            in_specs=[vmem(), vmem(), smem(), vmem(), vmem()], out_specs=(vmem(),) * 3,
            scratch_shapes=[pltpu.VMEM((2 * (rows + 2 * halo), LANES), F32), pltpu.VMEM((edges, LANES), F32)]
            + [pltpu.VMEM((2 * rows, LANES), F32)] * 8,
            compiler_params=params(), name="aggregate_one",
        )(own, halo_rows, pair, w2, w2t)

        d_pre, misc = pl.pallas_call(
            functools.partial(k3_body, num_dev),
            out_shape=(jax.ShapeDtypeStruct((rows, width), F32), jax.ShapeDtypeStruct((16, width), F32)),
            in_specs=[vmem()] * 11, out_specs=(vmem(),) * 2,
            scratch_shapes=[pltpu.VMEM((all_hi * CLASS_ROWS, LANES), BF16), pltpu.VMEM((2, 16, halo), BF16),
                            pltpu.VMEM((2, 16, halo), BF16), pltpu.VMEM((2, CLASS_ROWS, halo), F32),
                            pltpu.VMEM((2, CLASS_ROWS, halo), F32), pltpu.VMEM((own_hi * 24, LANES), F32),
                            pltpu.VMEM((all_hi * 24, LANES), F32), pltpu.VMEM((own_hi * 24, LANES), F32),
                            pltpu.VMEM((3 * own_hi * CLASS_ROWS, LANES), BF16), pltpu.SemaphoreType.DMA((2, 4))],
            compiler_params=params(1), name="layer_two",
        )(tab, send_rows, src2, dst2, w2, lab2, mask2, count, hid, pos, w2t)

        ext = pl.pallas_call(
            functools.partial(k4_body, 32),
            out_shape=jax.ShapeDtypeStruct((rows + 2 * halo, width), F32),
            in_specs=[vmem(), smem(), vmem()], out_specs=vmem(),
            scratch_shapes=[pltpu.VMEM((2 * rows, LANES), F32), pltpu.VMEM((edges, LANES), F32)]
            + [pltpu.VMEM((2 * (rows + 2 * halo), LANES), F32)] * 8,
            compiler_params=params(), name="scatter_one",
        )(d_pre, pair, w2)

        sum_rows_pad = 512
        landing = [pltpu.VMEM((sum_rows_pad >> (i + 1), width), F32) for i in range(len(bits))]
        grad_one, tail = pl.pallas_call(
            functools.partial(k5_body, num_dev, bits),
            out_shape=(jax.ShapeDtypeStruct((feats, width), F32), jax.ShapeDtypeStruct((16, width), F32)),
            in_specs=[vmem()] * 4, out_specs=(vmem(),) * 2,
            scratch_shapes=[pltpu.VMEM((sum_rows_pad, rows), BF16), pltpu.VMEM((rows, 2 * halo), BF16),
                            pltpu.VMEM((2 * halo, width), F32), pltpu.VMEM((rows, width), F32),
                            pltpu.VMEM((sum_rows_pad, width), F32), pltpu.VMEM((sum_rows_pad, width), F32)]
            + landing + [pltpu.SemaphoreType.DMA((2, 8)), pltpu.SemaphoreType.DMA((2, 2 * len(bits)))],
            compiler_params=params(2), name="weight_gradient",
        )(node_feats, ext, send_rows, misc)
        return tail[12, 0], grad_one, tail[4:4 + classes].T

    row_spec = P(GRAPH_AXIS)
    return jax.shard_map(device_step, mesh=mesh,
                         in_specs=(row_spec, P(), P(), row_spec, row_spec, row_spec, row_spec, row_spec, row_spec),
                         out_specs=(P(), P(), P()), check_vma=False)
```

time: 706 us -> 186 us (0.26)
  other arithmetic: 421 us -> 2.08 us
  Pallas kernels: 0 us -> 173 us
  waiting for transfers between devices: 127 us -> 0 us
  blocking collectives: 84.6 us -> 0 us
  local copies, waits for them, and re-layouts: 26.5 us -> 8.86 us
  between operations: 16.7 us -> 0.66 us
  starting transfers between devices: 15.9 us -> 0 us
  matrix products: 12.1 us -> 0 us
    scatter-add x6 -> x0, other arithmetic: 413 us -> none  [the longest x2 194 us: aggregate(): jax.ops.segment_sum(edge_w[:, None] * ext_table[edge_src], edge_dst, num_...]
    pallas_call x0 -> x5, Pallas kernels: none -> 173 us  [the longest x1 67.8 us: device_step(): pl.pallas_call(functools.partial(k5_body, num_dev, bits), out_shape=(jax....]
    psum x1 -> x0, waiting for transfers between devices: 85.6 us -> none  [device_step(): lax.psum(lax.dot_general(node_feats, d_tab_one, CONTRACT_ROWS, preferred_...]
    psum x2 -> x0, blocking collectives: 84.6 us -> none  [the longest x1 47.6 us: device_step(): lax.psum(jnp.sum(mask_f * (log_norm - picked)), GRAPH_AXIS) / label_count]
    ppermute x8 -> x0, waiting for transfers between devices: 41.9 us -> none  [the longest x2 17.5 us: scatter_back(): lax.ppermute(ext_grad[rows_loc:rows_loc + halo_rows], GRAPH_AXIS, to_prev)]
    gather x6 -> x0, local copies, waits for them, and re-layouts: 16.6 us -> none  [the longest x3 8.31 us: halo_extend(): from_next = lax.ppermute(node_table[send_rows[0]], GRAPH_AXIS, to_prev)]
    ppermute x8 -> x0, starting transfers between devices: 15.8 us -> none  [the longest x2 11.6 us: halo_extend(): from_next = lax.ppermute(node_table[send_rows[0]], GRAPH_AXIS, to_prev)]
    dot_general x5 -> x0, matrix products: 12.1 us -> none  [the longest x1 3.34 us: device_step(): lax.dot_general(d_tab_two, w_two_b, CONTRACT_COLS, preferred_element_type...]
  transfers between devices with their start and end apart: 9 -> 0, of which waited for: 9 -> 0; matrix products, arithmetic and copies ran while one was open for 1% -> 0% of each run, Pallas kernels for 0% -> 0%
where the time goes in v1:
time: 186 us; the launch traced here: 184 us
  Pallas kernels  173 us (93%)
  local copies, waits for them, and re-layouts  8.86 us (5%)
  other arithmetic  2.08 us (1%)
    pallas_call x1, Pallas kernels, device_step(): pl.pallas_call(functools.partial(k5_body, num_dev, bits), out_shape=(jax....  67.8 us
    pallas_call x1, Pallas kernels, device_step(): pl.pallas_call(functools.partial(k1_body, num_dev, bits), out_shape=(jax....  32.6 us
    pallas_call x1, Pallas kernels, device_step(): pl.pallas_call(functools.partial(k3_body, num_dev), out_shape=(jax.ShapeD...  24.8 us
    pallas_call x1, Pallas kernels, device_step(): pl.pallas_call(functools.partial(k4_body, 32), out_shape=jax.ShapeDtypeSt...  24.4 us
    pallas_call x1, Pallas kernels, device_step(): pl.pallas_call(functools.partial(k2_body, 32), out_shape=(jax.ShapeDtypeS...  23.2 us
    unnamed x2, local copies, waits for them, and re-layouts  5.76 us

profile of v1, /device:TPU:0, one launch (start us, length us, event | category | flops | bytes accessed | tf_op | source)
XLA Modules:
  0.0 184.3 jit_solution(9947196448221795342)
XLA Ops:
  0.6 0.7 convert_bitcast_fusion
  1.3 0.6 scatter.4.w2t_ref
  1.9 1.4 multiply_add_fusion.pair_ref
  3.3 3.9 %copy.13.x_ref = bf16[2048,500]{1,0:T(8,128)(2,1)} copy(bf16[2048,500]{0,1:T(8,128)(2,1)} %param.11) | data formatting | bytes 4096000 | tf_op args[0]
  7.2 32.6 %transform_and_halo.1 = (bf16[2048,256]{1,0:T(8,128)(2,1)}, bf16[2048,256]{1,0:T(8,128)(2,1)}, f32[8,128]{1,0:T(8,128)}) custom-call(bf16[2048,500]{1,0:T(8,128)(2,1)} %copy.13.x_ref, f32[500,256]{1,0:T(8,128)} %w_ref.1, s32[2,1024]{1,0:T(2,128)} %send_ref.5, s32[16,128]{1,0:T(8,128)} %bitcast.15), custom_call_target="tpu_custom_call" | custom-call | tf_op jit(solution)/shard_map/transform_and_halo/pallas_call | solution.py:417
  39.8 23.2 %aggregate_one.1 = (bf16[2048,256]{1,0:T(8,128)(2,1)}, bf16[2048,256]{1,0:T(8,128)(2,1)}, f32[128,128]{1,0:T(8,128)}) custom-call(bf16[2048,256]{1,0:T(8,128)(2,1)} %get-tuple-element.25.own_ref, bf16[2048,256]{1,0:T(8,128)(2,1)} %get-tuple-element.26.halo_ref, s32[8192]{0:T(1024)} %multiply_add_fusion.pair_ref, f32[64,128]{1,0:T(8,128)} %bitcast.10, ...), custom_call_target="tpu_custom_call" | custom-call | tf_op jit(solution)/shard_map/aggregate_one/pallas_call | solution.py:428
  63.0 24.8 %layer_two.1 = (f32[2048,256]{1,0:T(8,128)}, f32[16,256]{1,0:T(8,128)}) custom-call(f32[128,128]{1,0:T(8,128)} %get-tuple-element.27.tab_ref, s32[2,1024]{1,0:T(2,128)} %send_ref.5, s32[64,128]{1,0:T(8,128)} %bitcast.14, s32[64,128]{1,0:T(8,128)} %bitcast.13, f32[64,128]{1,0:T(8,128)} %bitcast.11, s32[16,128]{1,0:T(8,128)} %bitcast.17, s32[16,128]{1,0:T(8,128)} %bitcast.16, ...), custom_call_target="tpu_custom_call" | custom-call | tf_op jit(solution)/shard_map/layer_two/pallas_call | solution.py:438
  87.7 24.4 %scatter_one.1.ext_ref = f32[4096,256]{1,0:T(8,128)} custom-call(f32[2048,256]{1,0:T(8,128)} %get-tuple-element.31.dy_ref, s32[8192]{0:T(1024)} %multiply_add_fusion.pair_ref, f32[64,128]{1,0:T(8,128)} %bitcast.12), custom_call_target="tpu_custom_call" | custom-call | tf_op jit(solution)/shard_map/scatter_one/pallas_call | solution.py:450
  112.1 67.8 %weight_gradient.1 = (f32[500,256]{1,0:T(8,128)}, f32[16,256]{1,0:T(8,128)}) custom-call(bf16[2048,500]{1,0:T(8,128)(2,1)} %copy.13.x_ref, f32[4096,256]{1,0:T(8,128)} %scatter_one.1.ext_ref, s32[2,1024]{1,0:T(2,128)} %send_ref.5, f32[16,256]{1,0:T(8,128)} %get-tuple-element.32.misc_ref), custom_call_target="tpu_custom_call" | custom-call | tf_op jit(solution)/shard_map/weight_gradient/pallas_call | solution.py:461
  180.0 1.2 slice.22
  181.2 1.3 slice_bitcast_fusion
  182.5 1.9 %copy.15 = f32[500,256]{1,0:T(8,128)} copy(f32[500,256]{1,0:T(8,128)} %get-tuple-element.39) | data formatting | bytes 1024000

commit v2 on v1

v2 whole, which is shorter than its diff:
```python
import functools

import jax
import jax.numpy as jnp
from jax import lax
from jax.experimental import pallas as pl
from jax.experimental.pallas import tpu as pltpu
from jax.sharding import PartitionSpec as P

GRAPH_AXIS = "graph"
MESH = pl.DeviceIdType.MESH
LANES = 128
CLASS_ROWS = 8
VMEM_BYTES = 60 * 2**20
F32 = jnp.float32
BF16 = jnp.bfloat16
NT = (((1,), (1,)), ((), ()))
TN = (((0,), (0,)), ((), ()))


def vmem():
    return pl.BlockSpec(memory_space=pltpu.VMEM)


def smem():
    return pl.BlockSpec(memory_space=pltpu.SMEM)


PLANE = 8
LIST_ROWS = 80
BLOCK = 32
NUM_BUFS = 4


def ring_peers(num_dev):
    me = lax.axis_index(GRAPH_AXIS)
    return me, (me + 1) % num_dev, (me + num_dev - 1) % num_dev


def layer_peers(me, num_dev):
    return [(me + PLANE * k) % num_dev for k in range(1, num_dev // PLANE)]


def class_weights(w_ref):
    w = w_ref[...]
    return jnp.concatenate([w, jnp.zeros((CLASS_ROWS - w.shape[0], w.shape[1]), F32)], axis=0).astype(BF16)


def meet(partners):
    barrier = pltpu.get_barrier_semaphore()
    for dev in partners:
        pl.semaphore_signal(barrier, inc=1, device_id=(dev,), device_id_type=MESH)
    pl.semaphore_wait(barrier, len(partners))


def remote(src, dst, sems, slot, dev):
    return pltpu.make_async_remote_copy(
        src_ref=src, dst_ref=dst, send_sem=sems.at[0, slot], recv_sem=sems.at[1, slot],
        device_id=(dev,), device_id_type=MESH)


def three_pieces(val):
    top = val.astype(BF16).astype(F32)
    rest = val - top
    mid = rest.astype(BF16).astype(F32)
    return top, mid, rest - mid


def wide_row(ref, first):
    blk = ref[pl.ds(first, 8), :]
    return jnp.concatenate([blk[j:j + 1, :] for j in range(8)], axis=1)


def lo_hot(idx):
    lo = idx & (LANES - 1)
    node = lax.broadcasted_iota(jnp.int32, (LANES, idx.shape[1]), 0)
    return (node == lo).astype(F32).astype(BF16)


def list_places(src_ref, w_ref, rows, halo, pos, num_ref):
    src, live = src_ref[...], w_ref[...] != 0.0
    n_rows = src.shape[0]
    tri = (lax.broadcasted_iota(jnp.int32, (LANES, LANES), 0) <= lax.broadcasted_iota(jnp.int32, (LANES, LANES), 1))
    tri = tri.astype(F32).astype(BF16)
    low = (lax.broadcasted_iota(jnp.int32, (n_rows, n_rows), 1) < lax.broadcasted_iota(jnp.int32, (n_rows, n_rows), 0))
    low = low.astype(F32).astype(BF16)
    place = jnp.full(src.shape, LIST_ROWS * LANES, jnp.int32)
    start = jnp.zeros((1, 1), jnp.int32)
    lane = lax.broadcasted_iota(jnp.int32, num_ref.shape, 1)
    num = jnp.zeros(num_ref.shape, jnp.int32)
    kinds = (src < rows, (src >= rows) & (src < rows + halo), src >= rows + halo)
    for k, kind in enumerate(kinds):
        kind = kind & live
        flag = kind.astype(F32)
        inner = jnp.dot(flag.astype(BF16), tri, preferred_element_type=F32)
        row_sum = jnp.broadcast_to(jnp.sum(flag, axis=1, keepdims=True), flag.shape)
        before = jnp.dot(low, row_sum.astype(BF16), preferred_element_type=F32)
        rank = (inner + before).astype(jnp.int32) - 1
        place = jnp.where(kind, start + rank, place)
        total = jnp.sum(jnp.sum(flag, axis=1, keepdims=True), axis=0, keepdims=True).astype(jnp.int32)
        blocks = lax.shift_right_logical(total + (BLOCK - 1), BLOCK.bit_length() - 1)
        start = start + blocks * BLOCK
        num = jnp.where(lane == k, blocks, num)
    pos[...] = place
    num_ref[...] = num


def k1_body(num_dev, xt_ref, w_ref, send_ref, mask_ref, src_ref, dst_ref, ew_ref,
            own_ref, halo_ref, cnt_ref, lsrc_ref, ldst_ref, ltgt_ref, lw_ref, num_ref,
            stage, peer, cnt_send, cnt_recv, pos, acc, sems, peer_sems, cnt_sems):
    me, nxt, prv = ring_peers(num_dev)
    layer = [me - me % PLANE + (me % PLANE + k) % PLANE for k in range(1, PLANE)]
    meet([nxt, prv] + layer)
    rows = own_ref.shape[0]
    halo = send_ref.shape[1]
    total = jnp.sum(jnp.sum(mask_ref[...].astype(F32), axis=1, keepdims=True), axis=0, keepdims=True)
    cnt_send[...] = jnp.broadcast_to(total, cnt_send.shape)
    small = [remote(send_ref, peer.at[0], peer_sems, 0, nxt), remote(send_ref, peer.at[1], peer_sems, 1, prv)]
    small += [remote(cnt_send, cnt_recv.at[k], cnt_sems, k, dev) for k, dev in enumerate(layer)]
    for copy in small:
        copy.start()
    own_t = lax.dot_general(w_ref[...].astype(BF16), xt_ref[...], TN, preferred_element_type=F32)
    own_ref[...] = jnp.transpose(own_t).astype(BF16)

    blocks = halo // LANES
    ids = jnp.concatenate([send_ref[r:r + 1, b * LANES:(b + 1) * LANES] for r in range(2) for b in range(blocks)], axis=0)
    ids_col = jnp.transpose(ids)
    node = lax.broadcasted_iota(jnp.int32, (LANES, rows), 1)
    copies = []
    half = halo // 2
    for part in range(2):
        for r in (1, 0):
            for b in range(part * blocks // 2, (part + 1) * blocks // 2):
                col = ids_col[:, r * blocks + b:r * blocks + b + 1]
                pick = (node == col).astype(F32).astype(BF16)
                stage[pl.ds(r * halo + b * LANES, LANES), :] = jnp.dot(
                    pick, own_ref[...], preferred_element_type=F32).astype(BF16)
            dst_row = (1 - r) * halo + part * half
            copy = remote(stage.at[pl.ds(r * halo + part * half, half), :], halo_ref.at[pl.ds(dst_row, half), :],
                          sems, 2 * part + r, nxt if r == 1 else prv)
            copy.start()
            copies.append(copy)

    list_places(src_ref, ew_ref, rows, halo, pos, num_ref)
    for copy in small:
        copy.wait()
    for k in range(len(layer)):
        total = total + cnt_recv[k][0:1, 0:1]
    cnt_ref[...] = jnp.broadcast_to(total, cnt_ref.shape)
    theirs = jnp.concatenate([peer[s][1 - s:2 - s, b * LANES:(b + 1) * LANES] for s in range(2) for b in range(blocks)], axis=0)
    theirs = jnp.concatenate([lax.shift_right_logical(theirs, 4), theirs & 15], axis=0).astype(F32).astype(BF16)
    acc[...] = jnp.zeros_like(acc)

    def sort(i, carry):
        first = pl.multiple_of(i * 8, 8)
        src, dst, wgt, place = (wide_row(ref, first) for ref in (src_ref, dst_ref, ew_ref, pos))
        n = src.shape[1]
        at = jnp.maximum(src - rows, 0)
        cols = jnp.dot(theirs, lo_hot(at), preferred_element_type=F32)
        cols = cols[0:2 * blocks] * 16.0 + cols[2 * blocks:4 * blocks]
        mine = lax.broadcasted_iota(jnp.int32, cols.shape, 0) == lax.shift_right_logical(at, 7)
        tgt = jnp.sum(jnp.where(mine, cols, 0.0), axis=0, keepdims=True).astype(jnp.int32)
        tgt = jnp.where(src < rows, src, tgt)
        both = src + dst * 4096
        ints = [both & 255, lax.shift_right_logical(both, 8) & 255, lax.shift_right_logical(both, 16),
                tgt & 255, lax.shift_right_logical(tgt, 8)]
        cargo = [v.astype(F32) for v in ints] + list(three_pieces(wgt))
        here = lax.broadcasted_iota(jnp.int32, (LIST_ROWS, n), 0) == lax.shift_right_logical(place, 7)
        lhs = jnp.concatenate([jnp.where(here, v, 0.0).astype(BF16) for v in cargo], axis=0)
        acc[...] += lax.dot_general(lhs, lo_hot(place), NT, preferred_element_type=F32)
        return carry

    lax.fori_loop(0, src_ref.shape[0] // 8, sort, 0)
    got = [acc[p * LIST_ROWS:(p + 1) * LIST_ROWS, :] for p in range(8)]
    ints = [g.astype(jnp.int32) for g in got[:5]]
    both = ints[0] + ints[1] * 256 + ints[2] * 65536
    lsrc_ref[...] = (both & 4095) * 2
    ldst_ref[...] = lax.shift_right_logical(both, 12) * 2
    ltgt_ref[...] = (ints[3] + ints[4] * 256) * 2
    lw_ref[...] = got[5] + got[6] + got[7]
    for copy in copies:
        copy.wait()


def spread_weights(w_ref, wide, first, last):
    def body(b, carry):
        row = jnp.broadcast_to(w_ref[pl.ds(b, 1), :], (LANES, LANES))
        wide[pl.ds(pl.multiple_of(b * LANES, LANES), LANES), :] = jnp.transpose(row)
        return carry

    lax.fori_loop(first, last, body, 0)


def clear_rows(bufs):
    def body(i, carry):
        for buf in bufs:
            buf[pl.ds(pl.multiple_of(i * 64, 64), 64), :] = jnp.zeros((64, LANES), F32)
        return carry

    lax.fori_loop(0, bufs[0].shape[0] // 64, body, 0)


def row_loop(take_ref, put_ref, wide, table, bufs, first, last):
    num = len(bufs)

    def step(i, carry):
        base = i * BLOCK
        for lead in range(0, BLOCK, num):
            take = [pl.multiple_of(take_ref[base + lead + j], 2) for j in range(num)]
            put = [pl.multiple_of(put_ref[base + lead + j], 2) for j in range(num)]
            vals = [wide[pl.ds(base + lead + j, 1), :] * table[pl.ds(take[j], 2), :] for j in range(num)]
            old = [bufs[j][pl.ds(put[j], 2), :] for j in range(num)]
            for j in range(num):
                bufs[j][pl.ds(put[j], 2), :] = old[j] + vals[j]
        return carry

    lax.fori_loop(first, last, step, 0)


def list_rows(first, last):
    return first * BLOCK // LANES, (last * BLOCK + LANES - 1) // LANES


def to_rows(blk, table, first_row):
    for h in range(2):
        table[pl.ds(2 * first_row + h, blk.shape[0], stride=2), :] = blk[:, h * LANES:(h + 1) * LANES]


def sum_rows(bufs, blk):
    halves = []
    for h in range(2):
        parts = [buf[pl.ds(2 * blk * LANES + h, LANES, stride=2), :] for buf in bufs]
        while len(parts) > 1:
            parts = [a + b for a, b in zip(parts[::2], parts[1::2])]
        halves.append(parts[0])
    return jnp.concatenate(halves, axis=1)


def k2_body(own_ref, halo_ref, lsrc_ref, ldst_ref, num_ref, lw_ref, w2_ref, hid_ref, pos_ref, tab_ref, table, wide, *bufs):
    end = num_ref[0, 0] + num_ref[0, 1] + num_ref[0, 2]
    spread_weights(lw_ref, wide, *list_rows(0, end))
    rows = own_ref.shape[0]

    def widen(i, carry):
        at = pl.ds(pl.multiple_of(i * LANES, LANES), LANES)
        to_rows(own_ref[at, :].astype(F32), table, i * LANES)
        to_rows(halo_ref[at, :].astype(F32), table, rows + i * LANES)
        return carry

    lax.fori_loop(0, rows // LANES, widen, 0)
    clear_rows(bufs)
    row_loop(lsrc_ref, ldst_ref, wide, table, bufs, 0, end)
    w2t = class_weights(w2_ref)

    def finish(i, carry):
        pre = sum_rows(bufs, i)
        hid = jnp.maximum(pre, 0.0).astype(BF16)
        at = pl.ds(pl.multiple_of(i * LANES, LANES), LANES)
        hid_ref[at, :] = hid
        pos_ref[at, :] = (pre > 0.0).astype(F32).astype(BF16)
        t2 = lax.dot_general(w2t, hid, NT, preferred_element_type=F32)
        tab_ref[pl.ds(pl.multiple_of(i * CLASS_ROWS, CLASS_ROWS), CLASS_ROWS), :] = t2.astype(BF16).astype(F32)
        return carry

    lax.fori_loop(0, rows // LANES, finish, 0)


def k4_body(own_list, prev_list, next_list, pos_own_ref, pos_halo_ref, dt_own_ref, dt_halo_ref, w2_ref, xt_ref, misc_ref,
            out_ref, dt_wide, tables, wide, d_tab, *bufs):
    w2t = class_weights(w2_ref)
    rows = pos_own_ref.shape[0]
    clear_rows(bufs)
    sides = ((own_list, dt_own_ref, pos_own_ref, 0), (prev_list, dt_halo_ref.at[0], pos_halo_ref.at[0], 2),
             (next_list, dt_halo_ref.at[1], pos_halo_ref.at[1], 1))
    for (take_ref, put_ref, num_ref, lw_ref), dt_ref, pos_ref, kind in sides:
        dt_wide[...] = dt_ref[...].astype(F32)

        def widen(i, carry):
            dt = dt_wide[pl.ds(pl.multiple_of(i * CLASS_ROWS, CLASS_ROWS), CLASS_ROWS), :]
            d_hid = jnp.dot(jnp.transpose(dt).astype(BF16), w2t, preferred_element_type=F32)
            at = pl.ds(pl.multiple_of(i * LANES, LANES), LANES)
            to_rows(jnp.where(pos_ref[at, :].astype(F32) > 0.0, d_hid, 0.0), tables, i * LANES)
            return carry

        lax.fori_loop(0, rows // LANES, widen, 0)
        first = 0
        for k in range(kind):
            first = first + num_ref[0, k]
        last = first + num_ref[0, kind]
        spread_weights(lw_ref, wide, *list_rows(first, last))
        row_loop(take_ref, put_ref, wide, tables, bufs, first, last)

    def finish(i, carry):
        d_tab[pl.ds(pl.multiple_of(i * LANES, LANES), LANES), :] = sum_rows(bufs, i).astype(BF16)
        return carry

    lax.fori_loop(0, rows // LANES, finish, 0)
    feats = xt_ref.shape[0]
    out_ref[0:feats, :] = jnp.dot(xt_ref[...], d_tab[...], preferred_element_type=F32)
    out_ref[feats:feats + 12, :] = misc_ref[0:12, :]


def hi_of(idx):
    return jnp.broadcast_to(lax.shift_right_logical(idx, 7), (CLASS_ROWS, idx.shape[1]))


def pick_cols(table_b, pieces, idx, hot):
    cols = jnp.dot(table_b, hot, preferred_element_type=F32)
    rows = table_b.shape[0] // pieces
    hi = hi_of(idx)
    out = jnp.zeros(hi.shape, F32)
    for h in range(rows // CLASS_ROWS):
        part = cols[h * CLASS_ROWS:(h + 1) * CLASS_ROWS]
        for p in range(1, pieces):
            part = part + cols[p * rows + h * CLASS_ROWS:p * rows + (h + 1) * CLASS_ROWS]
        out = out + jnp.where(hi == h, part, 0.0)
    return out


def add_cols(val, idx, hot, num_hi):
    hi = hi_of(idx)
    pieces = three_pieces(val)
    rows = []
    for h in range(0, num_hi, 2):
        both = [jnp.where(hi == h + k, p, 0.0) for k in range(2) for p in pieces]
        rows.append(jnp.concatenate(both, axis=0).astype(BF16))
    return lax.dot_general(jnp.concatenate(rows, axis=0), hot, NT, preferred_element_type=F32)


def join_pieces(acc, num_hi):
    out = []
    for h in range(num_hi):
        a = acc[h * 24:h * 24 + 24, :]
        out.append(a[0:8] + a[8:16] + a[16:24])
    return out


def stack_pieces(val):
    return jnp.concatenate(three_pieces(val), axis=0).astype(BF16)


def k3_body(num_dev, tab_ref, send_ref, src_ref, dst_ref, w_ref, lab_ref, mask_ref, cnt_ref, hid_ref, pos_ref,
            ldst_ref, ltgt_ref, lw_ref, num_ref,
            dt_ref, misc_ref, dt_halo_ref, pos_halo_ref, hdst_ref, htgt_ref, hw_ref, hnum_ref,
            ext_b, fwd_send, fwd_recv, bwd_send, bwd_recv, acc_z, acc_s, acc_r, dz_b, cnt_recv,
            sems, cnt_sems, list_sems, pos_sems):
    me, nxt, prv = ring_peers(num_dev)
    layers = layer_peers(me, num_dev)
    meet([nxt, prv] + layers)
    counts = [remote(cnt_ref, cnt_recv.at[k], cnt_sems, k, dev) for k, dev in enumerate(layers)]
    for copy in counts:
        copy.start()
    late = []

    def send_late(pairs, pool, first):
        for k, (src, dst) in enumerate(pairs):
            for s, dev in enumerate((nxt, prv)):
                copy = remote(src, dst(s), pool, 2 * (first + k) + s, dev)
                copy.start()
                late.append(copy)

    chunk = pos_ref.shape[0] // 4

    def send_pos(q):
        at = pl.ds(q * chunk, chunk)
        send_late([(pos_ref.at[at, :], lambda s: pos_halo_ref.at[s, at, :])], pos_sems, q)

    own_hi = tab_ref.shape[0] // CLASS_ROWS
    halo = send_ref.shape[1]
    halo_hi = halo // LANES
    all_hi = own_hi + 2 * halo_hi
    own_b = tab_ref[...].astype(BF16)
    ext_b[pl.ds(0, own_hi * CLASS_ROWS), :] = own_b
    hot_send = [lo_hot(send_ref[r:r + 1, :]) for r in range(2)]
    copies = []
    for r in (1, 0):
        val = pick_cols(own_b, 1, send_ref[r:r + 1, :], hot_send[r])
        fwd_send[r] = jnp.concatenate([val, jnp.zeros_like(val)], axis=0).astype(BF16)
        copy = remote(fwd_send.at[r], fwd_recv.at[1 - r], sems, r, nxt if r == 1 else prv)
        copy.start()
        copies.append(copy)
    send_late([(ldst_ref, lambda s: hdst_ref.at[s]), (ltgt_ref, lambda s: htgt_ref.at[s]),
               (lw_ref, lambda s: hw_ref.at[s]), (num_ref, lambda s: hnum_ref.at[s])], list_sems, 0)
    send_pos(0)
    send_pos(1)
    acc_z[...] = jnp.zeros_like(acc_z)
    acc_s[...] = jnp.zeros_like(acc_s)
    for copy in copies:
        copy.wait()
    for r in range(2):
        got = fwd_recv[r].astype(F32)
        for j in range(0, halo_hi, 2):
            two = jnp.concatenate([got[0:8, (j + k) * LANES:(j + k + 1) * LANES] for k in range(2)], axis=0)
            ext_b[pl.ds((own_hi + r * halo_hi + j) * CLASS_ROWS, 16), :] = two.astype(BF16)

    steps = src_ref.shape[0] // 8

    def forward(i, carry):
        first = pl.multiple_of(i * 8, 8)
        src, dst = wide_row(src_ref, first), wide_row(dst_ref, first)
        val = pick_cols(ext_b[...], 1, src, lo_hot(src)) * wide_row(w_ref, first)
        acc_z[...] += add_cols(val, dst, lo_hot(dst), own_hi)
        return carry

    lax.fori_loop(0, steps, forward, 0)

    logits = join_pieces(acc_z[...], own_hi)
    cls = lax.broadcasted_iota(jnp.int32, (CLASS_ROWS, LANES), 0)
    count = cnt_ref[0:1, :]
    for k, copy in enumerate(counts):
        copy.wait()
        count = count + cnt_recv[k][0:1, :]
    count = jnp.maximum(count, 1.0)
    loss = jnp.zeros((1, LANES), F32)
    d_log = []
    for h in range(own_hi):
        z = jnp.where(cls < 7, logits[h], -jnp.inf)
        top = jnp.max(z, axis=0, keepdims=True)
        norm = jnp.log(jnp.sum(jnp.exp(z - top), axis=0, keepdims=True)) + top
        hot = cls == lab_ref[h:h + 1, :]
        mask = mask_ref[h:h + 1, :].astype(F32)
        picked = jnp.sum(jnp.where(hot, logits[h], 0.0), axis=0, keepdims=True)
        loss = loss + mask * (norm - picked)
        d_log.append((jnp.exp(z - norm) - hot.astype(F32)) * (mask / count))
    dz_b[...] = stack_pieces(jnp.concatenate(d_log, axis=0))

    def backward(i, carry):
        first = pl.multiple_of(i * 8, 8)
        src, dst = wide_row(src_ref, first), wide_row(dst_ref, first)
        val = pick_cols(dz_b[...], 3, dst, lo_hot(dst)) * wide_row(w_ref, first)
        acc_s[...] += add_cols(val, src, lo_hot(src), all_hi)
        return carry

    lax.fori_loop(0, steps, backward, 0)

    d_ext = join_pieces(acc_s[...], all_hi)
    copies = []
    for r in range(2):
        for j in range(halo_hi):
            bwd_send[r, :, j * LANES:(j + 1) * LANES] = d_ext[own_hi + r * halo_hi + j]
        copy = remote(bwd_send.at[r], bwd_recv.at[1 - r], sems, 2 + r, prv if r == 0 else nxt)
        copy.start()
        copies.append(copy)
    send_pos(2)
    for copy in copies:
        copy.wait()
    for r in range(2):
        part = add_cols(bwd_recv[r], send_ref[r:r + 1, :], hot_send[r], own_hi)
        acc_r[...] = part if r == 0 else acc_r[...] + part
    back = join_pieces(acc_r[...], own_hi)
    d_tab = [d_ext[h] + back[h] for h in range(own_hi)]
    dt_ref[...] = jnp.concatenate(d_tab, axis=0).astype(BF16)
    send_late([(dt_ref, lambda s: dt_halo_ref.at[s])], list_sems, 4)
    send_pos(3)
    grad = jnp.zeros((CLASS_ROWS, hid_ref.shape[1]), F32)
    for h in range(own_hi):
        grad = grad + jnp.dot(d_tab[h].astype(BF16), hid_ref[pl.ds(h * LANES, LANES), :], preferred_element_type=F32)
    misc_ref[0:8, :] = grad
    total = jnp.sum(loss, axis=1, keepdims=True) / count[:, 0:1]
    misc_ref[8:16, :] = jnp.broadcast_to(total, (8, misc_ref.shape[1]))
    for copy in late:
        copy.wait()


def k5_body(num_dev, part_ref, full_ref, land_core, land_chip, land_z, by_core, by_chip, sems):
    me = lax.axis_index(GRAPH_AXIS)
    core, chip, z = me % 2, (me // 2) % 4, me // PLANE
    other = me + 1 - 2 * core
    chips = [me + 2 * ((chip + k) % 4 - chip) for k in range(1, 4)]
    layers = layer_peers(me, num_dev)
    num_z = num_dev // PLANE
    meet([other] + chips + layers)
    rows = part_ref.shape[0]
    n1, n2, n3 = rows // 2, rows // 8, rows // 8 // num_z
    slot = 0
    keep = pl.multiple_of(core * n1, n1)
    copy = remote(part_ref.at[pl.ds(pl.multiple_of((1 - core) * n1, n1), n1), :], land_core, sems, slot, other)
    copy.start()
    copy.wait()
    by_core[...] = part_ref[pl.ds(keep, n1), :] + land_core[...]

    slot = 1
    copies = []
    for k, dev in enumerate(chips):
        at = pl.multiple_of(((chip + k + 1) % 4) * n2, n2)
        copies.append(remote(by_core.at[pl.ds(at, n2), :], land_chip.at[k], sems, slot + k, dev))
        copies[-1].start()
    total = by_core[pl.ds(pl.multiple_of(chip * n2, n2), n2), :]
    for k, copy in enumerate(copies):
        copy.wait()
        total = total + land_chip[k]
    by_chip[...] = total

    slot = 4
    copies = []
    for k, dev in enumerate(layers):
        at = pl.multiple_of(((z + k + 1) % num_z) * n3, n3)
        copies.append(remote(by_chip.at[pl.ds(at, n3), :], land_z.at[k], sems, slot + k, dev))
        copies[-1].start()
    total = by_chip[pl.ds(pl.multiple_of(z * n3, n3), n3), :]
    for k, copy in enumerate(copies):
        copy.wait()
        total = total + land_z[k]
    first = pl.multiple_of(core * n1 + chip * n2 + z * n3, n3)
    full_ref[pl.ds(first, n3), :] = total

    slot = 4 + len(layers)
    for at, size, devs in ((first, n3, layers), (core * n1 + chip * n2, n2, chips), (core * n1, n1, [other])):
        own = full_ref.at[pl.ds(pl.multiple_of(at, size), size), :]
        copies = [remote(own, own, sems, slot + k, dev) for k, dev in enumerate(devs)]
        slot += len(devs)
        for copy in copies:
            copy.start()
        for copy in copies:
            copy.wait()


def k6_body(full_ref, loss_ref, one_ref, two_ref):
    feats, classes = one_ref.shape[0], two_ref.shape[0]
    one_ref[...] = full_ref[0:feats, :]
    two_ref[...] = full_ref[feats:feats + classes, :]
    loss_ref[...] = full_ref[feats + 8:feats + 9, 0:1]


def solution(mesh):
    num_dev = mesh.shape[GRAPH_AXIS]

    def params(cid=None):
        if cid is None:
            return pltpu.CompilerParams(vmem_limit_bytes=VMEM_BYTES)
        return pltpu.CompilerParams(vmem_limit_bytes=VMEM_BYTES, collective_id=cid, has_side_effects=True)

    def arr(dtype, *shape):
        return jax.ShapeDtypeStruct(shape, dtype)

    def scr(dtype, *shape):
        return pltpu.VMEM(shape, dtype)

    def dma(count):
        return pltpu.SemaphoreType.DMA((2, count))

    I32 = jnp.int32

    def device_step(node_feats, w_one, w_two, send_rows, edge_src, edge_dst, edge_w, labels, label_mask):
        rows, feats = node_feats.shape
        width = w_one.shape[1]
        halo = send_rows.shape[1]
        edges = edge_src.shape[0]
        own_hi, all_hi = rows // LANES, (rows + 2 * halo) // LANES
        feats_t, w2 = node_feats.T, w_two.T
        src2, dst2, ew2 = (a.reshape(edges // LANES, LANES) for a in (edge_src, edge_dst, edge_w))
        lab2, mask2 = labels.reshape(own_hi, LANES), label_mask.reshape(own_hi, LANES)
        listed = (LIST_ROWS, LANES)
        entries = LIST_ROWS * LANES

        own, halo_rows, count, lsrc, ldst, ltgt, lw, num = pl.pallas_call(
            functools.partial(k1_body, num_dev),
            out_shape=(arr(BF16, rows, width), arr(BF16, 2 * halo, width), arr(F32, 8, LANES), arr(I32, *listed),
                       arr(I32, *listed), arr(I32, *listed), arr(F32, *listed), arr(I32, 8, LANES)),
            in_specs=[vmem()] * 7, out_specs=(vmem(),) * 8,
            scratch_shapes=[scr(BF16, 2 * halo, width), scr(I32, 2, 2, halo), scr(F32, 8, LANES),
                            scr(F32, PLANE - 1, 8, LANES), scr(I32, edges // LANES, LANES), scr(F32, 8 * LIST_ROWS, LANES),
                            dma(4), dma(2), dma(PLANE - 1)],
            compiler_params=params(0), name="transform_and_halo",
        )(feats_t, w_one, send_rows, mask2, src2, dst2, ew2)

        hid, pos, tab = pl.pallas_call(
            k2_body,
            out_shape=(arr(BF16, rows, width), arr(BF16, rows, width), arr(F32, own_hi * CLASS_ROWS, LANES)),
            in_specs=[vmem(), vmem(), smem(), smem(), smem(), vmem(), vmem()], out_specs=(vmem(),) * 3,
            scratch_shapes=[scr(F32, 2 * (rows + 2 * halo), LANES), scr(F32, entries, LANES)]
            + [scr(F32, 2 * rows, LANES)] * NUM_BUFS,
            compiler_params=params(), name="aggregate_one",
        )(own, halo_rows, lsrc.reshape(entries), ldst.reshape(entries), num, lw, w2)

        num_z = num_dev // PLANE
        d_tab, misc, d_tab_halo, pos_halo, hdst, htgt, hw, hnum = pl.pallas_call(
            functools.partial(k3_body, num_dev),
            out_shape=(arr(BF16, own_hi * CLASS_ROWS, LANES), arr(F32, 16, width), arr(BF16, 2, own_hi * CLASS_ROWS, LANES),
                       arr(BF16, 2, rows, width), arr(I32, 2, *listed), arr(I32, 2, *listed), arr(F32, 2, *listed),
                       arr(I32, 2, 8, LANES)),
            in_specs=[vmem()] * 14, out_specs=(vmem(),) * 8,
            scratch_shapes=[scr(BF16, all_hi * CLASS_ROWS, LANES), scr(BF16, 2, 16, halo), scr(BF16, 2, 16, halo),
                            scr(F32, 2, CLASS_ROWS, halo), scr(F32, 2, CLASS_ROWS, halo), scr(F32, own_hi * 24, LANES),
                            scr(F32, all_hi * 24, LANES), scr(F32, own_hi * 24, LANES),
                            scr(BF16, 3 * own_hi * CLASS_ROWS, LANES), scr(F32, num_z - 1, 8, LANES),
                            dma(4), dma(num_z - 1), dma(10), dma(8)],
            compiler_params=params(1), name="layer_two",
        )(tab, send_rows, src2, dst2, ew2, lab2, mask2, count, hid, pos, ldst, ltgt, lw, num)

        def k4(own_take, own_put, own_num, own_w, p_take, p_put, p_num, p_w, n_take, n_put, n_num, n_w, *rest):
            k4_body((own_take, own_put, own_num, own_w), (p_take, p_put, p_num, p_w), (n_take, n_put, n_num, n_w), *rest)

        sum_rows_pad = 512
        part = pl.pallas_call(
            k4,
            out_shape=arr(F32, sum_rows_pad, width),
            in_specs=[smem(), smem(), smem(), vmem()] * 3 + [vmem()] * 7, out_specs=vmem(),
            scratch_shapes=[scr(F32, own_hi * CLASS_ROWS, LANES), scr(F32, 2 * rows, LANES), scr(F32, entries, LANES),
                            scr(BF16, rows, width)] + [scr(F32, 2 * rows, LANES)] * NUM_BUFS,
            compiler_params=params(), name="scatter_one",
        )(ldst.reshape(entries), ltgt.reshape(entries), num, lw,
          hdst[0].reshape(entries), htgt[0].reshape(entries), hnum[0], hw[0],
          hdst[1].reshape(entries), htgt[1].reshape(entries), hnum[1], hw[1],
          pos, pos_halo, d_tab, d_tab_halo, w2, feats_t, misc)

        n1, n2 = sum_rows_pad // 2, sum_rows_pad // 8
        n3 = n2 // num_z
        full = pl.pallas_call(
            functools.partial(k5_body, num_dev),
            out_shape=arr(F32, sum_rows_pad, width),
            in_specs=[vmem()], out_specs=vmem(),
            scratch_shapes=[scr(F32, n1, width), scr(F32, 3, n2, width), scr(F32, num_z - 1, n3, width),
                            scr(F32, n1, width), scr(F32, n2, width), dma(2 * (1 + 3 + num_z - 1))],
            compiler_params=params(2), name="sum_gradients",
        )(part)
        loss, grad_one, grad_two = pl.pallas_call(
            k6_body,
            out_shape=(arr(F32, 1, 1), arr(F32, feats, width), arr(F32, w2.shape[0], width)),
            in_specs=[vmem()], out_specs=(vmem(),) * 3, compiler_params=params(), name="outputs",
        )(full)
        return loss.reshape(()), grad_one, grad_two.T

    row_spec = P(GRAPH_AXIS)
    return jax.shard_map(device_step, mesh=mesh,
                         in_specs=(row_spec, P(), P(), row_spec, row_spec, row_spec, row_spec, row_spec, row_spec),
                         out_specs=(P(), P(), P()), check_vma=False)
```

time: 186 us -> 148 us (0.80)
  Pallas kernels: 173 us -> 142 us
  local copies, waits for them, and re-layouts: 8.86 us -> 4.19 us
  other arithmetic: 2.08 us -> 0 us
    pallas_call x5 -> x6, Pallas kernels: 173 us -> 142 us  [the longest x1 34.4 us: device_step(): pl.pallas_call(functools.partial(k3_body, num_dev), out_shape=(arr(BF16,...]
    unnamed x2 -> x0, local copies, waits for them, and re-layouts: 5.76 us -> none
    squeeze x0 -> x2, local copies, waits for them, and re-layouts: none -> 2.69 us  [the longest x1 1.42 us: device_step(): hw[1]]
where the time goes in v2:
time: 148 us; the launch traced here: 147 us
  Pallas kernels  142 us (96%)
  local copies, waits for them, and re-layouts  4.19 us (3%)
    pallas_call x1, Pallas kernels, device_step(): pl.pallas_call(functools.partial(k3_body, num_dev), out_shape=(arr(BF16,...  34.4 us
    pallas_call x1, Pallas kernels, device_step(): pl.pallas_call(k4, out_shape=arr(F32, sum_rows_pad, width), in_specs=[sme...  33.2 us
    pallas_call x1, Pallas kernels, device_step(): pl.pallas_call(functools.partial(k5_body, num_dev), out_shape=arr(F32, su...  30.8 us
    pallas_call x1, Pallas kernels, device_step(): pl.pallas_call(k2_body, out_shape=(arr(BF16, rows, width), arr(BF16, rows...  23.2 us
    pallas_call x1, Pallas kernels, device_step(): pl.pallas_call(functools.partial(k1_body, num_dev), out_shape=(arr(BF16,...  19 us

profile of v2, /device:TPU:0, one launch (start us, length us, event | category | flops | bytes accessed | tf_op | source)
XLA Modules:
  0.0 147.2 jit_solution(5059351167651934450)
XLA Ops:
  0.6 19.0 %transform_and_halo.1 = (bf16[2048,256]{1,0:T(8,128)(2,1)}, bf16[2048,256]{1,0:T(8,128)(2,1)}, f32[8,128]{1,0:T(8,128)}, s32[80,128]{1,0:T(8,128)}, s32[80,128]{...) custom-call(bf16[500,2048]{1,0:T(8,128)(2,1)} %bitcast.28, f32[500,256]{1,0:T(8,128)} %w_ref.1, ...), custom_call_target="tpu_custom_call" | custom-call | tf_op jit(solution)/shard_map/transform_and_halo/pallas_call | solution.py:556
  19.6 23.2 %aggregate_one.1 = (bf16[2048,256]{1,0:T(8,128)(2,1)}, bf16[2048,256]{1,0:T(8,128)(2,1)}, f32[128,128]{1,0:T(8,128)}) custom-call(bf16[2048,256]{1,0:T(8,128)(2,1)} %get-tuple-element.29.own_ref, bf16[2048,256]{1,0:T(8,128)(2,1)} %get-tuple-element.30.halo_ref, s32[10240]{0:T(1024)} %bitcast.39, s32[10240]{0:T(1024)} %bitcast.30, ...), custom_call_target="tpu_custom_call" | custom-call | tf_op jit(solution)/shard_map/aggregate_one/pallas_call | solution.py:567
  42.8 34.4 %layer_two.1 = (bf16[128,128]{1,0:T(8,128)(2,1)}, f32[16,256]{1,0:T(8,128)}, bf16[2,128,128]{2,1,0:T(8,128)(2,1)}, bf16[2,2048,256]{2,1,0:T(8,128)(2,1)}, s32[2,...) custom-call(f32[128,128]{1,0:T(8,128)} %get-tuple-element.32.tab_ref, ...), custom_call_target="tpu_custom_call" | custom-call | tf_op jit(solution)/shard_map/layer_two/pallas_call | solution.py:577
  77.2 1.5 %slice_bitcast_fusion.1 = (s32[10240]{0:T(1024)}, s32[10240]{0:T(1024)}, s32[10240]{0:T(1024)}, s32[10240]{0:T(1024)}) fusion(s32[2,80,128]{2,1,0:T(8,128)} %get-tuple-element.37, s32[2,80,128]{2,1,0:T(8,128)} %get-tuple-element.36), kind=kLoop, calls=%fused_computation.1 | loop fusion | bytes 327680 | tf_op jit(solution)/shard_map/reshape;squeeze | solution.py:604
  78.7 1.3 slice_bitcast_fusion.6
  80.0 1.4 slice_bitcast_fusion
  81.4 33.2 %scatter_one.1.part_ref = f32[512,256]{1,0:T(8,128)} custom-call(s32[10240]{0:T(1024)} %bitcast.31, s32[10240]{0:T(1024)} %bitcast.32, s32[8,128]{1,0:T(8,128)} %get-tuple-element.27.num_ref.own_num, f32[80,128]{1,0:T(8,128)} %get-tuple-element.28.lw_ref.own_w, s32[10240]{0:T(1024)} %get-tuple-element.55.p_take, s32[10240]{0:T(1024)} %get-tuple-element.50.p_put, ...), custom_call_target="tpu_custom_call" | custom-call | tf_op jit(solution)/shard_map/scatter_one/pallas_call | solution.py:595
  114.6 30.8 %sum_gradients.1.full_ref = f32[512,256]{1,0:T(8,128)} custom-call(f32[512,256]{1,0:T(8,128)} %scatter_one.1.part_ref), custom_call_target="tpu_custom_call" | custom-call | tf_op jit(solution)/shard_map/sum_gradients/pallas_call | solution.py:609
  145.4 1.9 %outputs.1 = (f32[1,1]{1,0:T(1,128)}, f32[500,256]{1,0:T(8,128)}, f32[7,256]{1,0:T(8,128)}) custom-call(f32[512,256]{1,0:T(8,128)} %sum_gradients.1.full_ref), custom_call_target="tpu_custom_call" | custom-call | tf_op jit(solution)/shard_map/outputs/pallas_call | solution.py:617

commit v3 on v2

--- a/solution.py
+++ b/solution.py
@@ -106,8 +106,8 @@
 
 
 def k1_body(num_dev, xt_ref, w_ref, send_ref, mask_ref, src_ref, dst_ref, ew_ref,
-            own_ref, halo_ref, cnt_ref, lsrc_ref, ldst_ref, ltgt_ref, lw_ref, num_ref,
-            stage, peer, cnt_send, cnt_recv, pos, acc, sems, peer_sems, cnt_sems):
+            own_ref, halo_ref, cnt_ref, lsrc_ref, ldst_ref, ltgt_ref, lpair_ref, lw_ref, num_ref,
+            own_t_b, stage, peer, cnt_send, cnt_recv, pos, acc, sems, peer_sems, cnt_sems):
     me, nxt, prv = ring_peers(num_dev)
     layer = [me - me % PLANE + (me % PLANE + k) % PLANE for k in range(1, PLANE)]
     meet([nxt, prv] + layer)
@@ -120,7 +120,7 @@
     for copy in small:
         copy.start()
     own_t = lax.dot_general(w_ref[...].astype(BF16), xt_ref[...], TN, preferred_element_type=F32)
-    own_ref[...] = jnp.transpose(own_t).astype(BF16)
+    own_t_b[...] = own_t.astype(BF16)
 
     blocks = halo // LANES
     ids = jnp.concatenate([send_ref[r:r + 1, b * LANES:(b + 1) * LANES] for r in range(2) for b in range(blocks)], axis=0)
@@ -133,14 +133,15 @@
             for b in range(part * blocks // 2, (part + 1) * blocks // 2):
                 col = ids_col[:, r * blocks + b:r * blocks + b + 1]
                 pick = (node == col).astype(F32).astype(BF16)
-                stage[pl.ds(r * halo + b * LANES, LANES), :] = jnp.dot(
-                    pick, own_ref[...], preferred_element_type=F32).astype(BF16)
+                stage[pl.ds(r * halo + b * LANES, LANES), :] = lax.dot_general(
+                    pick, own_t_b[...], NT, preferred_element_type=F32).astype(BF16)
             dst_row = (1 - r) * halo + part * half
             copy = remote(stage.at[pl.ds(r * halo + part * half, half), :], halo_ref.at[pl.ds(dst_row, half), :],
                           sems, 2 * part + r, nxt if r == 1 else prv)
             copy.start()
             copies.append(copy)
 
+    own_ref[...] = jnp.transpose(own_t_b[...])
     list_places(src_ref, ew_ref, rows, halo, pos, num_ref)
     for copy in small:
         copy.wait()
@@ -174,21 +175,25 @@
     got = [acc[p * LIST_ROWS:(p + 1) * LIST_ROWS, :] for p in range(8)]
     ints = [g.astype(jnp.int32) for g in got[:5]]
     both = ints[0] + ints[1] * 256 + ints[2] * 65536
+    dst, tgt = lax.shift_right_logical(both, 12) * 2, (ints[3] + ints[4] * 256) * 2
     lsrc_ref[...] = (both & 4095) * 2
-    ldst_ref[...] = lax.shift_right_logical(both, 12) * 2
-    ltgt_ref[...] = (ints[3] + ints[4] * 256) * 2
+    ldst_ref[...] = dst
+    ltgt_ref[...] = tgt
+    lpair_ref[...] = dst + tgt * 65536
     lw_ref[...] = got[5] + got[6] + got[7]
     for copy in copies:
         copy.wait()
 
 
 def spread_weights(w_ref, wide, first, last):
-    def body(b, carry):
-        row = jnp.broadcast_to(w_ref[pl.ds(b, 1), :], (LANES, LANES))
-        wide[pl.ds(pl.multiple_of(b * LANES, LANES), LANES), :] = jnp.transpose(row)
-        return carry
-
-    lax.fori_loop(first, last, body, 0)
+    def body(g, carry):
+        cols = jnp.transpose(w_ref[pl.ds(pl.multiple_of(g * 8, 8), 8), :])
+        for j in range(8):
+            at = pl.ds(pl.multiple_of(g * 8 * LANES + j * LANES, LANES), LANES)
+            wide[at, :] = jnp.broadcast_to(cols[:, j:j + 1], (LANES, LANES))
+        return carry
+
+    lax.fori_loop(first // 8, (last + 7) // 8, body, 0)
 
 
 def clear_rows(bufs):
@@ -265,19 +270,21 @@
     lax.fori_loop(0, rows // LANES, finish, 0)
 
 
-def k4_body(own_list, prev_list, next_list, pos_own_ref, pos_halo_ref, dt_own_ref, dt_halo_ref, w2_ref, xt_ref, misc_ref,
-            out_ref, dt_wide, tables, wide, d_tab, *bufs):
-    w2t = class_weights(w2_ref)
+def k4_body(own_list, prev_list, next_list, pos_own_ref, pos_prev_ref, pos_next_ref, dt_own_ref, dt_prev_ref, dt_next_ref,
+            w2_ref, xt_ref, misc_ref,
+            out_ref, tables, wide, d_tab, *bufs):
+    w2t = class_weights(w2_ref).astype(F32)
     rows = pos_own_ref.shape[0]
+    w2_all = jnp.concatenate([w2t] * (rows // LANES), axis=0)
+    group = lax.shift_right_logical(lax.broadcasted_iota(jnp.int32, w2_all.shape, 0), 3)
     clear_rows(bufs)
-    sides = ((own_list, dt_own_ref, pos_own_ref, 0), (prev_list, dt_halo_ref.at[0], pos_halo_ref.at[0], 2),
-             (next_list, dt_halo_ref.at[1], pos_halo_ref.at[1], 1))
+    sides = ((own_list, dt_own_ref, pos_own_ref, 0), (prev_list, dt_prev_ref, pos_prev_ref, 2),
+             (next_list, dt_next_ref, pos_next_ref, 1))
     for (take_ref, put_ref, num_ref, lw_ref), dt_ref, pos_ref, kind in sides:
-        dt_wide[...] = dt_ref[...].astype(F32)
+        dt_cols = jnp.transpose(dt_ref[...].astype(F32)).astype(BF16)
 
         def widen(i, carry):
-            dt = dt_wide[pl.ds(pl.multiple_of(i * CLASS_ROWS, CLASS_ROWS), CLASS_ROWS), :]
-            d_hid = jnp.dot(jnp.transpose(dt).astype(BF16), w2t, preferred_element_type=F32)
+            d_hid = jnp.dot(dt_cols, jnp.where(group == i, w2_all, 0.0).astype(BF16), preferred_element_type=F32)
             at = pl.ds(pl.multiple_of(i * LANES, LANES), LANES)
             to_rows(jnp.where(pos_ref[at, :].astype(F32) > 0.0, d_hid, 0.0), tables, i * LANES)
             return carry
@@ -340,8 +347,9 @@
 
 
 def k3_body(num_dev, tab_ref, send_ref, src_ref, dst_ref, w_ref, lab_ref, mask_ref, cnt_ref, hid_ref, pos_ref,
-            ldst_ref, ltgt_ref, lw_ref, num_ref,
-            dt_ref, misc_ref, dt_halo_ref, pos_halo_ref, hdst_ref, htgt_ref, hw_ref, hnum_ref,
+            lpair_ref, lw_ref, num_ref,
+            dt_ref, misc_ref, dt_prev_ref, dt_next_ref, pos_prev_ref, pos_next_ref, dst_prev_ref, dst_next_ref,
+            tgt_prev_ref, tgt_next_ref, w_prev_ref, w_next_ref, num_prev_ref, num_next_ref, pairs,
             ext_b, fwd_send, fwd_recv, bwd_send, bwd_recv, acc_z, acc_s, acc_r, dz_b, cnt_recv,
             sems, cnt_sems, list_sems, pos_sems):
     me, nxt, prv = ring_peers(num_dev)
@@ -355,7 +363,7 @@
     def send_late(pairs, pool, first):
         for k, (src, dst) in enumerate(pairs):
             for s, dev in enumerate((nxt, prv)):
-                copy = remote(src, dst(s), pool, 2 * (first + k) + s, dev)
+                copy = remote(src, dst[s], pool, 2 * (first + k) + s, dev)
                 copy.start()
                 late.append(copy)
 
@@ -363,7 +371,7 @@
 
     def send_pos(q):
         at = pl.ds(q * chunk, chunk)
-        send_late([(pos_ref.at[at, :], lambda s: pos_halo_ref.at[s, at, :])], pos_sems, q)
+        send_late([(pos_ref.at[at, :], [pos_prev_ref.at[at, :], pos_next_ref.at[at, :]])], pos_sems, q)
 
     own_hi = tab_ref.shape[0] // CLASS_ROWS
     halo = send_ref.shape[1]
@@ -379,8 +387,8 @@
         copy = remote(fwd_send.at[r], fwd_recv.at[1 - r], sems, r, nxt if r == 1 else prv)
         copy.start()
         copies.append(copy)
-    send_late([(ldst_ref, lambda s: hdst_ref.at[s]), (ltgt_ref, lambda s: htgt_ref.at[s]),
-               (lw_ref, lambda s: hw_ref.at[s]), (num_ref, lambda s: hnum_ref.at[s])], list_sems, 0)
+    send_late([(lpair_ref, [pairs.at[0], pairs.at[1]]), (lw_ref, [w_prev_ref, w_next_ref]),
+               (num_ref, [num_prev_ref, num_next_ref])], list_sems, 0)
     send_pos(0)
     send_pos(1)
     acc_z[...] = jnp.zeros_like(acc_z)
@@ -450,7 +458,7 @@
     back = join_pieces(acc_r[...], own_hi)
     d_tab = [d_ext[h] + back[h] for h in range(own_hi)]
     dt_ref[...] = jnp.concatenate(d_tab, axis=0).astype(BF16)
-    send_late([(dt_ref, lambda s: dt_halo_ref.at[s])], list_sems, 4)
+    send_late([(dt_ref, [dt_prev_ref, dt_next_ref])], list_sems, 3)
     send_pos(3)
     grad = jnp.zeros((CLASS_ROWS, hid_ref.shape[1]), F32)
     for h in range(own_hi):
@@ -460,6 +468,9 @@
     misc_ref[8:16, :] = jnp.broadcast_to(total, (8, misc_ref.shape[1]))
     for copy in late:
         copy.wait()
+    for s, (dst_ref_, tgt_ref_) in enumerate(((dst_prev_ref, tgt_prev_ref), (dst_next_ref, tgt_next_ref))):
+        dst_ref_[...] = pairs[s] & 0xFFFF
+        tgt_ref_[...] = lax.shift_right_logical(pairs[s], 16)
 
 
 def k5_body(num_dev, part_ref, full_ref, land_core, land_chip, land_z, by_core, by_chip, sems):
@@ -470,49 +481,62 @@
     layers = layer_peers(me, num_dev)
     num_z = num_dev // PLANE
     meet([other] + chips + layers)
-    rows = part_ref.shape[0]
+    rows, width = part_ref.shape
     n1, n2, n3 = rows // 2, rows // 8, rows // 8 // num_z
-    slot = 0
-    keep = pl.multiple_of(core * n1, n1)
-    copy = remote(part_ref.at[pl.ds(pl.multiple_of((1 - core) * n1, n1), n1), :], land_core, sems, slot, other)
-    copy.start()
-    copy.wait()
-    by_core[...] = part_ref[pl.ds(keep, n1), :] + land_core[...]
-
-    slot = 1
-    copies = []
-    for k, dev in enumerate(chips):
-        at = pl.multiple_of(((chip + k + 1) % 4) * n2, n2)
-        copies.append(remote(by_core.at[pl.ds(at, n2), :], land_chip.at[k], sems, slot + k, dev))
-        copies[-1].start()
-    total = by_core[pl.ds(pl.multiple_of(chip * n2, n2), n2), :]
-    for k, copy in enumerate(copies):
-        copy.wait()
-        total = total + land_chip[k]
-    by_chip[...] = total
-
-    slot = 4
-    copies = []
-    for k, dev in enumerate(layers):
-        at = pl.multiple_of(((z + k + 1) % num_z) * n3, n3)
-        copies.append(remote(by_chip.at[pl.ds(at, n3), :], land_z.at[k], sems, slot + k, dev))
-        copies[-1].start()
-    total = by_chip[pl.ds(pl.multiple_of(z * n3, n3), n3), :]
-    for k, copy in enumerate(copies):
-        copy.wait()
-        total = total + land_z[k]
-    first = pl.multiple_of(core * n1 + chip * n2 + z * n3, n3)
-    full_ref[pl.ds(first, n3), :] = total
-
-    slot = 4 + len(layers)
-    for at, size, devs in ((first, n3, layers), (core * n1 + chip * n2, n2, chips), (core * n1, n1, [other])):
-        own = full_ref.at[pl.ds(pl.multiple_of(at, size), size), :]
-        copies = [remote(own, own, sems, slot + k, dev) for k, dev in enumerate(devs)]
-        slot += len(devs)
-        for copy in copies:
+    parts = [pl.ds(c * LANES, LANES) for c in range(width // LANES)]
+    used = [0]
+
+    def send(pairs):
+        out = []
+        for src, dst, dev in pairs:
+            out.append(remote(src, dst, sems, used[0], dev))
+            used[0] += 1
+        for copy in out:
             copy.start()
+        return out
+
+    def wait(copies):
         for copy in copies:
             copy.wait()
+
+    def at(first, size):
+        return pl.ds(pl.multiple_of(first, size), size)
+
+    flying = [send([(part_ref.at[at((1 - core) * n1, n1), c], land_core.at[:, c], other)]) for c in parts]
+    for i, c in enumerate(parts):
+        wait(flying[i])
+        by_core[:, c] = part_ref[at(core * n1, n1), c] + land_core[:, c]
+        flying[i] = send([(by_core.at[at((chip + k + 1) % 4 * n2, n2), c], land_chip.at[k, :, c], dev)
+                          for k, dev in enumerate(chips)])
+    for i, c in enumerate(parts):
+        wait(flying[i])
+        total = by_core[at(chip * n2, n2), c]
+        for k in range(len(chips)):
+            total = total + land_chip[k, :, c]
+        by_chip[:, c] = total
+        flying[i] = send([(by_chip.at[at((z + k + 1) % num_z * n3, n3), c], land_z.at[k, :, c], dev)
+                          for k, dev in enumerate(layers)])
+    first = core * n1 + chip * n2 + z * n3
+    gathers = ((first, n3, layers), (core * n1 + chip * n2, n2, chips), (core * n1, n1, [other]))
+
+    def gather(level, c):
+        first, size, devs = gathers[level]
+        own = full_ref.at[at(first, size), c]
+        return send([(own, own, dev) for dev in devs])
+
+    for i, c in enumerate(parts):
+        wait(flying[i])
+        total = by_chip[at(z * n3, n3), c]
+        for k in range(len(layers)):
+            total = total + land_z[k, :, c]
+        full_ref[at(first, n3), c] = total
+        flying[i] = gather(0, c)
+    for level in (1, 2):
+        for i, c in enumerate(parts):
+            wait(flying[i])
+            flying[i] = gather(level, c)
+    for copies in flying:
+        wait(copies)
 
 
 def k6_body(full_ref, loss_ref, one_ref, two_ref):
@@ -553,12 +577,12 @@
         listed = (LIST_ROWS, LANES)
         entries = LIST_ROWS * LANES
 
-        own, halo_rows, count, lsrc, ldst, ltgt, lw, num = pl.pallas_call(
+        own, halo_rows, count, lsrc, ldst, ltgt, lpair, lw, num = pl.pallas_call(
             functools.partial(k1_body, num_dev),
             out_shape=(arr(BF16, rows, width), arr(BF16, 2 * halo, width), arr(F32, 8, LANES), arr(I32, *listed),
-                       arr(I32, *listed), arr(I32, *listed), arr(F32, *listed), arr(I32, 8, LANES)),
-            in_specs=[vmem()] * 7, out_specs=(vmem(),) * 8,
-            scratch_shapes=[scr(BF16, 2 * halo, width), scr(I32, 2, 2, halo), scr(F32, 8, LANES),
+                       arr(I32, *listed), arr(I32, *listed), arr(I32, *listed), arr(F32, *listed), arr(I32, 8, LANES)),
+            in_specs=[vmem()] * 7, out_specs=(vmem(),) * 9,
+            scratch_shapes=[scr(BF16, width, rows), scr(BF16, 2 * halo, width), scr(I32, 2, 2, halo), scr(F32, 8, LANES),
                             scr(F32, PLANE - 1, 8, LANES), scr(I32, edges // LANES, LANES), scr(F32, 8 * LIST_ROWS, LANES),
                             dma(4), dma(2), dma(PLANE - 1)],
             compiler_params=params(0), name="transform_and_halo",
@@ -574,19 +598,21 @@
         )(own, halo_rows, lsrc.reshape(entries), ldst.reshape(entries), num, lw, w2)
 
         num_z = num_dev // PLANE
-        d_tab, misc, d_tab_halo, pos_halo, hdst, htgt, hw, hnum = pl.pallas_call(
+        tab_b = arr(BF16, own_hi * CLASS_ROWS, LANES)
+        (d_tab, misc, d_prev, d_next, pos_prev, pos_next, dst_prev, dst_next, tgt_prev, tgt_next, w_prev, w_next,
+         num_prev, num_next) = pl.pallas_call(
             functools.partial(k3_body, num_dev),
-            out_shape=(arr(BF16, own_hi * CLASS_ROWS, LANES), arr(F32, 16, width), arr(BF16, 2, own_hi * CLASS_ROWS, LANES),
-                       arr(BF16, 2, rows, width), arr(I32, 2, *listed), arr(I32, 2, *listed), arr(F32, 2, *listed),
-                       arr(I32, 2, 8, LANES)),
-            in_specs=[vmem()] * 14, out_specs=(vmem(),) * 8,
-            scratch_shapes=[scr(BF16, all_hi * CLASS_ROWS, LANES), scr(BF16, 2, 16, halo), scr(BF16, 2, 16, halo),
-                            scr(F32, 2, CLASS_ROWS, halo), scr(F32, 2, CLASS_ROWS, halo), scr(F32, own_hi * 24, LANES),
-                            scr(F32, all_hi * 24, LANES), scr(F32, own_hi * 24, LANES),
+            out_shape=(tab_b, arr(F32, 16, width), tab_b, tab_b, arr(BF16, rows, width), arr(BF16, rows, width),
+                       arr(I32, *listed), arr(I32, *listed), arr(I32, *listed), arr(I32, *listed),
+                       arr(F32, *listed), arr(F32, *listed), arr(I32, 8, LANES), arr(I32, 8, LANES)),
+            in_specs=[vmem()] * 13, out_specs=(vmem(),) * 14,
+            scratch_shapes=[scr(I32, 2, *listed), scr(BF16, all_hi * CLASS_ROWS, LANES), scr(BF16, 2, 16, halo),
+                            scr(BF16, 2, 16, halo), scr(F32, 2, CLASS_ROWS, halo), scr(F32, 2, CLASS_ROWS, halo),
+                            scr(F32, own_hi * 24, LANES), scr(F32, all_hi * 24, LANES), scr(F32, own_hi * 24, LANES),
                             scr(BF16, 3 * own_hi * CLASS_ROWS, LANES), scr(F32, num_z - 1, 8, LANES),
-                            dma(4), dma(num_z - 1), dma(10), dma(8)],
+                            dma(4), dma(num_z - 1), dma(8), dma(8)],
             compiler_params=params(1), name="layer_two",
-        )(tab, send_rows, src2, dst2, ew2, lab2, mask2, count, hid, pos, ldst, ltgt, lw, num)
+        )(tab, send_rows, src2, dst2, ew2, lab2, mask2, count, hid, pos, lpair, lw, num)
 
         def k4(own_take, own_put, own_num, own_w, p_take, p_put, p_num, p_w, n_take, n_put, n_num, n_w, *rest):
             k4_body((own_take, own_put, own_num, own_w), (p_take, p_put, p_num, p_w), (n_take, n_put, n_num, n_w), *rest)
@@ -595,14 +621,13 @@
         part = pl.pallas_call(
             k4,
             out_shape=arr(F32, sum_rows_pad, width),
-            in_specs=[smem(), smem(), smem(), vmem()] * 3 + [vmem()] * 7, out_specs=vmem(),
-            scratch_shapes=[scr(F32, own_hi * CLASS_ROWS, LANES), scr(F32, 2 * rows, LANES), scr(F32, entries, LANES),
-                            scr(BF16, rows, width)] + [scr(F32, 2 * rows, LANES)] * NUM_BUFS,
+            in_specs=[smem(), smem(), smem(), vmem()] * 3 + [vmem()] * 9, out_specs=vmem(),
+            scratch_shapes=[scr(F32, 2 * rows, LANES), scr(F32, entries, LANES), scr(BF16, rows, width)] + [scr(F32, 2 * rows, LANES)] * NUM_BUFS,
             compiler_params=params(), name="scatter_one",
         )(ldst.reshape(entries), ltgt.reshape(entries), num, lw,
-          hdst[0].reshape(entries), htgt[0].reshape(entries), hnum[0], hw[0],
-          hdst[1].reshape(entries), htgt[1].reshape(entries), hnum[1], hw[1],
-          pos, pos_halo, d_tab, d_tab_halo, w2, feats_t, misc)
+          dst_prev.reshape(entries), tgt_prev.reshape(entries), num_prev, w_prev,
+          dst_next.reshape(entries), tgt_next.reshape(entries), num_next, w_next,
+          pos, pos_prev, pos_next, d_tab, d_prev, d_next, w2, feats_t, misc)
 
         n1, n2 = sum_rows_pad // 2, sum_rows_pad // 8
         n3 = n2 // num_z
@@ -611,7 +636,7 @@
             out_shape=arr(F32, sum_rows_pad, width),
             in_specs=[vmem()], out_specs=vmem(),
             scratch_shapes=[scr(F32, n1, width), scr(F32, 3, n2, width), scr(F32, num_z - 1, n3, width),
-                            scr(F32, n1, width), scr(F32, n2, width), dma(2 * (1 + 3 + num_z - 1))],
+                            scr(F32, n1, width), scr(F32, n2, width), dma(4 * (1 + 3 + num_z - 1))],
             compiler_params=params(2), name="sum_gradients",
         )(part)
         loss, grad_one, grad_two = pl.pallas_call(

time: 148 us -> 134 us (0.905)
  Pallas kernels: 142 us -> 134 us
  local copies, waits for them, and re-layouts: 4.19 us -> 0 us
    pallas_call x1, Pallas kernels: 33.2 us -> 24.1 us  [device_step(): pl.pallas_call(k4, out_shape=arr(F32, sum_rows_pad, width), in_specs=[sme...]
    pallas_call x1, Pallas kernels: 23.2 us -> 15.7 us  [device_step(): pl.pallas_call(k2_body, out_shape=(arr(BF16, rows, width), arr(BF16, rows...]
    pallas_call x1, Pallas kernels: 34.4 us -> 38.6 us  [device_step(): pl.pallas_call(functools.partial(k3_body, num_dev), out_shape=(tab_b, arr...]
    squeeze x2 -> x0, local copies, waits for them, and re-layouts: 2.69 us -> none  [the longest x1 1.42 us: device_step(): hw[1]]
    pallas_call x1, Pallas kernels: 19 us -> 21.5 us  [device_step(): pl.pallas_call(functools.partial(k1_body, num_dev), out_shape=(arr(BF16,...]
    another operation x1 -> x0, local copies, waits for them, and re-layouts: 1.5 us -> none  [device_step(): htgt[1].reshape(entries)]
where the time goes in v3:
time: 134 us
  Pallas kernels  134 us (100%)
    pallas_call x1, Pallas kernels, device_step(): pl.pallas_call(functools.partial(k3_body, num_dev), out_shape=(tab_b, arr...  38.6 us
    pallas_call x1, Pallas kernels, device_step(): pl.pallas_call(functools.partial(k5_body, num_dev), out_shape=arr(F32, su...  31.8 us
    pallas_call x1, Pallas kernels, device_step(): pl.pallas_call(k4, out_shape=arr(F32, sum_rows_pad, width), in_specs=[sme...  24.1 us
    pallas_call x1, Pallas kernels, device_step(): pl.pallas_call(functools.partial(k1_body, num_dev), out_shape=(arr(BF16,...  21.5 us
    pallas_call x1, Pallas kernels, device_step(): pl.pallas_call(k2_body, out_shape=(arr(BF16, rows, width), arr(BF16, rows...  15.7 us

profile of v3, /device:TPU:0, one launch (start us, length us, event | category | flops | bytes accessed | tf_op | source)
XLA Modules:
  0.0 134.2 jit_solution(6886940125012707768)
XLA Ops:
  0.6 21.5 %transform_and_halo.1 = (bf16[2048,256]{1,0:T(8,128)(2,1)}, bf16[2048,256]{1,0:T(8,128)(2,1)}, f32[8,128]{1,0:T(8,128)}, s32[80,128]{1,0:T(8,128)}, s32[80,128]{...) custom-call(bf16[500,2048]{1,0:T(8,128)(2,1)} %bitcast.16, ...), custom_call_target="tpu_custom_call" | custom-call | tf_op jit(solution)/shard_map/transform_and_halo/pallas_call | solution.py:580
  22.1 15.7 %aggregate_one.1 = (bf16[2048,256]{1,0:T(8,128)(2,1)}, bf16[2048,256]{1,0:T(8,128)(2,1)}, f32[128,128]{1,0:T(8,128)}) custom-call(bf16[2048,256]{1,0:T(8,128)(2,1)} %get-tuple-element.36.own_ref, bf16[2048,256]{1,0:T(8,128)(2,1)} %get-tuple-element.37.halo_ref, s32[10240]{0:T(1024)} %bitcast.31, s32[10240]{0:T(1024)} %bitcast.18, ...), custom_call_target="tpu_custom_call" | custom-call | tf_op jit(solution)/shard_map/aggregate_one/pallas_call | solution.py:591
  37.8 38.6 %layer_two.1 = (bf16[128,128]{1,0:T(8,128)(2,1)}, f32[16,256]{1,0:T(8,128)}, bf16[128,128]{1,0:T(8,128)(2,1)}, bf16[128,128]{1,0:T(8,128)(2,1)}, bf16[2048,256]{...) custom-call(f32[128,128]{1,0:T(8,128)} %get-tuple-element.39.tab_ref, ...), custom_call_target="tpu_custom_call" | custom-call | tf_op jit(solution)/shard_map/layer_two/pallas_call | solution.py:603
  76.4 24.1 %scatter_one.1.part_ref = f32[512,256]{1,0:T(8,128)} custom-call(s32[10240]{0:T(1024)} %bitcast.19, s32[10240]{0:T(1024)} %bitcast.26, s32[8,128]{1,0:T(8,128)} %get-tuple-element.34.num_ref.own_num, f32[80,128]{1,0:T(8,128)} %get-tuple-element.35.lw_ref.own_w, s32[10240]{0:T(1024)} %bitcast.27, s32[10240]{0:T(1024)} %bitcast.29, ...), custom_call_target="tpu_custom_call" | custom-call | tf_op jit(solution)/shard_map/scatter_one/pallas_call | solution.py:621
  100.5 31.8 %sum_gradients.1.full_ref = f32[512,256]{1,0:T(8,128)} custom-call(f32[512,256]{1,0:T(8,128)} %scatter_one.1.part_ref), custom_call_target="tpu_custom_call" | custom-call | tf_op jit(solution)/shard_map/sum_gradients/pallas_call | solution.py:634
  132.3 1.9 %outputs.1 = (f32[1,1]{1,0:T(1,128)}, f32[500,256]{1,0:T(8,128)}, f32[7,256]{1,0:T(8,128)}) custom-call(f32[512,256]{1,0:T(8,128)} %sum_gradients.1.full_ref), custom_call_target="tpu_custom_call" | custom-call | tf_op jit(solution)/shard_map/outputs/pallas_call | solution.py:642

commit v4 on v3

--- a/solution.py
+++ b/solution.py
@@ -11,7 +11,7 @@
 MESH = pl.DeviceIdType.MESH
 LANES = 128
 CLASS_ROWS = 8
-VMEM_BYTES = 60 * 2**20
+VMEM_BYTES = 28 * 2**20
 F32 = jnp.float32
 BF16 = jnp.bfloat16
 NT = (((1,), (1,)), ((), ()))
@@ -22,14 +22,19 @@
     return pl.BlockSpec(memory_space=pltpu.VMEM)
 
 
+def hbm():
+    return pl.BlockSpec(memory_space=pl.ANY)
+
+
 def smem():
     return pl.BlockSpec(memory_space=pltpu.SMEM)
 
 
 PLANE = 8
 LIST_ROWS = 80
-BLOCK = 32
+BLOCK = 128
 NUM_BUFS = 4
+CHUNK = 1024
 
 
 def ring_peers(num_dev):
@@ -105,84 +110,54 @@
     num_ref[...] = num
 
 
-def k1_body(num_dev, xt_ref, w_ref, send_ref, mask_ref, src_ref, dst_ref, ew_ref,
-            own_ref, halo_ref, cnt_ref, lsrc_ref, ldst_ref, ltgt_ref, lpair_ref, lw_ref, num_ref,
-            own_t_b, stage, peer, cnt_send, cnt_recv, pos, acc, sems, peer_sems, cnt_sems):
-    me, nxt, prv = ring_peers(num_dev)
-    layer = [me - me % PLANE + (me % PLANE + k) % PLANE for k in range(1, PLANE)]
-    meet([nxt, prv] + layer)
-    rows = own_ref.shape[0]
+def k1_body(xt_hbm, w_hbm, send_hbm, own_t_ref, to_next_ref, to_prev_ref, xt_ref, w_ref, send_ref, sems):
+    copies = [pltpu.make_async_copy(a, b, sems.at[k])
+              for k, (a, b) in enumerate(((send_hbm, send_ref), (w_hbm, w_ref), (xt_hbm, xt_ref)))]
+    for copy in copies:
+        copy.start()
+    copies[0].wait()
     halo = send_ref.shape[1]
-    total = jnp.sum(jnp.sum(mask_ref[...].astype(F32), axis=1, keepdims=True), axis=0, keepdims=True)
-    cnt_send[...] = jnp.broadcast_to(total, cnt_send.shape)
-    small = [remote(send_ref, peer.at[0], peer_sems, 0, nxt), remote(send_ref, peer.at[1], peer_sems, 1, prv)]
-    small += [remote(cnt_send, cnt_recv.at[k], cnt_sems, k, dev) for k, dev in enumerate(layer)]
-    for copy in small:
-        copy.start()
-    own_t = lax.dot_general(w_ref[...].astype(BF16), xt_ref[...], TN, preferred_element_type=F32)
-    own_t_b[...] = own_t.astype(BF16)
-
+    rows = xt_ref.shape[1]
     blocks = halo // LANES
     ids = jnp.concatenate([send_ref[r:r + 1, b * LANES:(b + 1) * LANES] for r in range(2) for b in range(blocks)], axis=0)
     ids_col = jnp.transpose(ids)
+    copies[1].wait()
+    w_b = w_ref[...].astype(BF16)
+    copies[2].wait()
+    own_t_ref[...] = lax.dot_general(w_b, xt_ref[...], TN, preferred_element_type=F32).astype(BF16)
     node = lax.broadcasted_iota(jnp.int32, (LANES, rows), 1)
-    copies = []
-    half = halo // 2
-    for part in range(2):
-        for r in (1, 0):
-            for b in range(part * blocks // 2, (part + 1) * blocks // 2):
-                col = ids_col[:, r * blocks + b:r * blocks + b + 1]
-                pick = (node == col).astype(F32).astype(BF16)
-                stage[pl.ds(r * halo + b * LANES, LANES), :] = lax.dot_general(
-                    pick, own_t_b[...], NT, preferred_element_type=F32).astype(BF16)
-            dst_row = (1 - r) * halo + part * half
-            copy = remote(stage.at[pl.ds(r * halo + part * half, half), :], halo_ref.at[pl.ds(dst_row, half), :],
-                          sems, 2 * part + r, nxt if r == 1 else prv)
-            copy.start()
-            copies.append(copy)
-
-    own_ref[...] = jnp.transpose(own_t_b[...])
+    for r, out in ((1, to_next_ref), (0, to_prev_ref)):
+        for b in range(blocks):
+            pick = (node == ids_col[:, r * blocks + b:r * blocks + b + 1]).astype(F32).astype(BF16)
+            out[b * LANES:(b + 1) * LANES, :] = lax.dot_general(
+                pick, own_t_ref[...], NT, preferred_element_type=F32).astype(BF16)
+
+
+def sort_edges(src_ref, dst_ref, ew_ref, rows, halo, pos, acc, lsrc_ref, ldst_ref, lpair_ref, lw_ref, num_ref):
     list_places(src_ref, ew_ref, rows, halo, pos, num_ref)
-    for copy in small:
-        copy.wait()
-    for k in range(len(layer)):
-        total = total + cnt_recv[k][0:1, 0:1]
-    cnt_ref[...] = jnp.broadcast_to(total, cnt_ref.shape)
-    theirs = jnp.concatenate([peer[s][1 - s:2 - s, b * LANES:(b + 1) * LANES] for s in range(2) for b in range(blocks)], axis=0)
-    theirs = jnp.concatenate([lax.shift_right_logical(theirs, 4), theirs & 15], axis=0).astype(F32).astype(BF16)
     acc[...] = jnp.zeros_like(acc)
 
     def sort(i, carry):
         first = pl.multiple_of(i * 8, 8)
         src, dst, wgt, place = (wide_row(ref, first) for ref in (src_ref, dst_ref, ew_ref, pos))
-        n = src.shape[1]
-        at = jnp.maximum(src - rows, 0)
-        cols = jnp.dot(theirs, lo_hot(at), preferred_element_type=F32)
-        cols = cols[0:2 * blocks] * 16.0 + cols[2 * blocks:4 * blocks]
-        mine = lax.broadcasted_iota(jnp.int32, cols.shape, 0) == lax.shift_right_logical(at, 7)
-        tgt = jnp.sum(jnp.where(mine, cols, 0.0), axis=0, keepdims=True).astype(jnp.int32)
-        tgt = jnp.where(src < rows, src, tgt)
         both = src + dst * 4096
-        ints = [both & 255, lax.shift_right_logical(both, 8) & 255, lax.shift_right_logical(both, 16),
-                tgt & 255, lax.shift_right_logical(tgt, 8)]
+        ints = [both & 255, lax.shift_right_logical(both, 8) & 255, lax.shift_right_logical(both, 16)]
         cargo = [v.astype(F32) for v in ints] + list(three_pieces(wgt))
-        here = lax.broadcasted_iota(jnp.int32, (LIST_ROWS, n), 0) == lax.shift_right_logical(place, 7)
+        here = lax.broadcasted_iota(jnp.int32, (LIST_ROWS, src.shape[1]), 0) == lax.shift_right_logical(place, 7)
         lhs = jnp.concatenate([jnp.where(here, v, 0.0).astype(BF16) for v in cargo], axis=0)
         acc[...] += lax.dot_general(lhs, lo_hot(place), NT, preferred_element_type=F32)
         return carry
 
     lax.fori_loop(0, src_ref.shape[0] // 8, sort, 0)
-    got = [acc[p * LIST_ROWS:(p + 1) * LIST_ROWS, :] for p in range(8)]
-    ints = [g.astype(jnp.int32) for g in got[:5]]
+    got = [acc[p * LIST_ROWS:(p + 1) * LIST_ROWS, :] for p in range(6)]
+    ints = [g.astype(jnp.int32) for g in got[:3]]
     both = ints[0] + ints[1] * 256 + ints[2] * 65536
-    dst, tgt = lax.shift_right_logical(both, 12) * 2, (ints[3] + ints[4] * 256) * 2
-    lsrc_ref[...] = (both & 4095) * 2
+    src, dst = both & 4095, lax.shift_right_logical(both, 12) * 2
+    src = jnp.where(src < rows, src, src - rows)
+    lsrc_ref[...] = src * 2
     ldst_ref[...] = dst
-    ltgt_ref[...] = tgt
-    lpair_ref[...] = dst + tgt * 65536
-    lw_ref[...] = got[5] + got[6] + got[7]
-    for copy in copies:
-        copy.wait()
+    lpair_ref[...] = dst + src * 65536
+    lw_ref[...] = got[3] + got[4] + got[5]
 
 
 def spread_weights(w_ref, wide, first, last):
@@ -205,21 +180,50 @@
     lax.fori_loop(0, bufs[0].shape[0] // 64, body, 0)
 
 
-def row_loop(take_ref, put_ref, wide, table, bufs, first, last):
+def chunk_copies(lists, fast, sems, c):
+    at = pl.ds(pl.multiple_of(c * 8, 8), CHUNK // LANES)
+    return [pltpu.make_async_copy(a.at[at, :], b.at[at, :], sems.at[k, c]) for k, (a, b) in enumerate(zip(lists, fast))]
+
+
+def chunks_of(first, last):
+    per = CHUNK // BLOCK
+    return first // per, (last + per - 1) // per
+
+
+def start_lists(lists, fast, sems, first, last):
+    def body(c, carry):
+        for copy in chunk_copies(lists, fast, sems, c):
+            copy.start()
+        return carry
+
+    lax.fori_loop(*chunks_of(first, last), body, 0)
+
+
+def row_loop(lists, fast, sems, wide, table, bufs, first, last, rename=None):
     num = len(bufs)
+    take_ref, put_ref = fast
+    per = CHUNK // BLOCK
 
     def step(i, carry):
         base = i * BLOCK
         for lead in range(0, BLOCK, num):
-            take = [pl.multiple_of(take_ref[base + lead + j], 2) for j in range(num)]
-            put = [pl.multiple_of(put_ref[base + lead + j], 2) for j in range(num)]
+            take = [pl.multiple_of(take_ref[i, lead + j], 2) for j in range(num)]
+            put = [put_ref[i, lead + j] for j in range(num)]
+            if rename is not None:
+                put = [rename[p] for p in put]
+            put = [pl.multiple_of(p, 2) for p in put]
             vals = [wide[pl.ds(base + lead + j, 1), :] * table[pl.ds(take[j], 2), :] for j in range(num)]
             old = [bufs[j][pl.ds(put[j], 2), :] for j in range(num)]
             for j in range(num):
                 bufs[j][pl.ds(put[j], 2), :] = old[j] + vals[j]
         return carry
 
-    lax.fori_loop(first, last, step, 0)
+    def chunk(c, carry):
+        for copy in chunk_copies(lists, fast, sems, c):
+            copy.wait()
+        return lax.fori_loop(jnp.maximum(first, c * per), jnp.minimum(last, c * per + per), step, carry)
+
+    lax.fori_loop(*chunks_of(first, last), chunk, 0)
 
 
 def list_rows(first, last):
@@ -241,64 +245,133 @@
     return jnp.concatenate(halves, axis=1)
 
 
-def k2_body(own_ref, halo_ref, lsrc_ref, ldst_ref, num_ref, lw_ref, w2_ref, hid_ref, pos_ref, tab_ref, table, wide, *bufs):
-    end = num_ref[0, 0] + num_ref[0, 1] + num_ref[0, 2]
-    spread_weights(lw_ref, wide, *list_rows(0, end))
-    rows = own_ref.shape[0]
+def k2a_body(own_t_ref, src_ref, dst_ref, ew_ref, part_ref, lsrc_ref, ldst_ref, lpair_ref, lw_ref, num_ref,
+             pos, acc, table, wide, num_fast, src_fast, dst_fast, num_sem, sems, *bufs):
+    rows = part_ref.shape[0]
+    sort_edges(src_ref, dst_ref, ew_ref, rows, rows // 2, pos, acc, lsrc_ref, ldst_ref, lpair_ref, lw_ref, num_ref)
 
     def widen(i, carry):
         at = pl.ds(pl.multiple_of(i * LANES, LANES), LANES)
-        to_rows(own_ref[at, :].astype(F32), table, i * LANES)
-        to_rows(halo_ref[at, :].astype(F32), table, rows + i * LANES)
+        to_rows(jnp.transpose(own_t_ref[:, at].astype(F32)), table, i * LANES)
         return carry
 
     lax.fori_loop(0, rows // LANES, widen, 0)
     clear_rows(bufs)
-    row_loop(lsrc_ref, ldst_ref, wide, table, bufs, 0, end)
+    copy = pltpu.make_async_copy(num_ref, num_fast, num_sem)
+    copy.start()
+    copy.wait()
+    end = num_fast[0, 0]
+    lists, fast = (lsrc_ref, ldst_ref), (src_fast, dst_fast)
+    start_lists(lists, fast, sems, 0, end)
+    spread_weights(lw_ref, wide, *list_rows(0, end))
+    row_loop(lists, fast, sems, wide, table, bufs, 0, end)
+
+    def finish(i, carry):
+        part_ref[pl.ds(pl.multiple_of(i * LANES, LANES), LANES), :] = sum_rows(bufs, i)
+        return carry
+
+    lax.fori_loop(0, rows // LANES, finish, 0)
+
+
+def k2b_body(part_ref, prev_ref, next_ref, lsrc_ref, ldst_ref, num_ref, lw_ref, w2_ref,
+             hid_ref, pos_a_ref, pos_b_ref, tab_ref, table, wide, src_fast, dst_fast, sems, *bufs):
+    first = num_ref[0, 0]
+    end = first + num_ref[0, 1] + num_ref[0, 2]
+    lists, fast = (lsrc_ref, ldst_ref), (src_fast, dst_fast)
+    start_lists(lists, fast, sems, first, end)
+    spread_weights(lw_ref, wide, *list_rows(first, end))
+    halo = prev_ref.shape[0]
+
+    def widen(i, carry):
+        at = pl.ds(pl.multiple_of(i * LANES, LANES), LANES)
+        to_rows(prev_ref[at, :].astype(F32), table, i * LANES)
+        to_rows(next_ref[at, :].astype(F32), table, halo + i * LANES)
+        return carry
+
+    lax.fori_loop(0, halo // LANES, widen, 0)
+    clear_rows(bufs)
+    row_loop(lists, fast, sems, wide, table, bufs, first, end)
     w2t = class_weights(w2_ref)
 
+    for side, pos_ref in enumerate((pos_a_ref, pos_b_ref)):
+        lead = side * pos_ref.shape[0] // LANES
+
+        def finish(j, carry):
+            i = lead + j
+            at = pl.ds(pl.multiple_of(i * LANES, LANES), LANES)
+            pre = part_ref[at, :] + sum_rows(bufs, i)
+            hid = jnp.maximum(pre, 0.0).astype(BF16)
+            hid_ref[at, :] = hid
+            pos_ref[pl.ds(pl.multiple_of(j * LANES, LANES), LANES), :] = (pre > 0.0).astype(F32).astype(BF16)
+            t2 = lax.dot_general(w2t, hid, NT, preferred_element_type=F32)
+            tab_ref[pl.ds(pl.multiple_of(i * CLASS_ROWS, CLASS_ROWS), CLASS_ROWS), :] = t2.astype(BF16).astype(F32)
+            return carry
+
+        lax.fori_loop(0, pos_ref.shape[0] // LANES, finish, 0)
+
+
+def stack_classes(w2_ref, blocks):
+    w2_all = jnp.concatenate([class_weights(w2_ref).astype(F32)] * blocks, axis=0)
+    return w2_all, lax.shift_right_logical(lax.broadcasted_iota(jnp.int32, w2_all.shape, 0), 3)
+
+
+def fill_table(dt_ref, pos_refs, w2_all, group, table):
+    dt_cols = jnp.transpose(dt_ref[...].astype(F32)).astype(BF16)
+    for side, pos_ref in enumerate(pos_refs):
+        lead = side * pos_ref.shape[0] // LANES
+
+        def widen(j, carry):
+            i = lead + j
+            d_hid = jnp.dot(dt_cols, jnp.where(group == i, w2_all, 0.0).astype(BF16), preferred_element_type=F32)
+            at = pl.ds(pl.multiple_of(j * LANES, LANES), LANES)
+            to_rows(jnp.where(pos_ref[at, :].astype(F32) > 0.0, d_hid, 0.0), table, i * LANES)
+            return carry
+
+        lax.fori_loop(0, pos_ref.shape[0] // LANES, widen, 0)
+
+
+def k4a_body(ldst_ref, lsrc_ref, num_ref, lw_ref, pos_a_ref, pos_b_ref, dt_ref, w2_ref, part_ref,
+             table, wide, take_fast, put_fast, sems, *bufs):
+    rows = part_ref.shape[0]
+    lists, fast, end = (ldst_ref, lsrc_ref), (take_fast, put_fast), num_ref[0, 0]
+    start_lists(lists, fast, sems, 0, end)
+    w2_all, group = stack_classes(w2_ref, rows // LANES)
+    clear_rows(bufs)
+    fill_table(dt_ref, (pos_a_ref, pos_b_ref), w2_all, group, table)
+    spread_weights(lw_ref, wide, *list_rows(0, end))
+    row_loop(lists, fast, sems, wide, table, bufs, 0, end)
+
     def finish(i, carry):
-        pre = sum_rows(bufs, i)
-        hid = jnp.maximum(pre, 0.0).astype(BF16)
+        part_ref[pl.ds(pl.multiple_of(i * LANES, LANES), LANES), :] = sum_rows(bufs, i)
+        return carry
+
+    lax.fori_loop(0, rows // LANES, finish, 0)
+
+
+def k4b_body(part_ref, num_ref, names_ref, prev_dst, prev_src, prev_w, next_dst, next_src, next_w,
+             prev_dt, prev_a, prev_b, next_dt, next_a, next_b, w2_ref, xt_ref, misc_ref, out_ref,
+             table, wide, d_tab, *rest):
+    fasts, pools, bufs = (rest[0:2], rest[2:4]), rest[4:6], rest[6:]
+    rows = part_ref.shape[0]
+    sides = (((prev_dst, prev_src), prev_w, prev_dt, (prev_a, prev_b), 1, 2),
+             ((next_dst, next_src), next_w, next_dt, (next_a, next_b), 2, 1))
+    spans = []
+    for (lists, _, _, _, row, kind), fast, pool in zip(sides, fasts, pools):
+        first = num_ref[row, 0]
+        if kind == 2:
+            first = first + num_ref[row, 1]
+        spans.append((first, first + num_ref[row, kind]))
+        start_lists(lists, fast, pool, *spans[-1])
+    w2_all, group = stack_classes(w2_ref, rows // LANES)
+    clear_rows(bufs)
+    for (lists, w_ref, dt_ref, pos_refs, _, _), fast, pool, span in zip(sides, fasts, pools, spans):
+        fill_table(dt_ref, pos_refs, w2_all, group, table)
+        spread_weights(w_ref, wide, *list_rows(*span))
+        row_loop(lists, fast, pool, wide, table, bufs, *span, rename=names_ref)
+
+    def finish(i, carry):
         at = pl.ds(pl.multiple_of(i * LANES, LANES), LANES)
-        hid_ref[at, :] = hid
-        pos_ref[at, :] = (pre > 0.0).astype(F32).astype(BF16)
-        t2 = lax.dot_general(w2t, hid, NT, preferred_element_type=F32)
-        tab_ref[pl.ds(pl.multiple_of(i * CLASS_ROWS, CLASS_ROWS), CLASS_ROWS), :] = t2.astype(BF16).astype(F32)
-        return carry
-
-    lax.fori_loop(0, rows // LANES, finish, 0)
-
-
-def k4_body(own_list, prev_list, next_list, pos_own_ref, pos_prev_ref, pos_next_ref, dt_own_ref, dt_prev_ref, dt_next_ref,
-            w2_ref, xt_ref, misc_ref,
-            out_ref, tables, wide, d_tab, *bufs):
-    w2t = class_weights(w2_ref).astype(F32)
-    rows = pos_own_ref.shape[0]
-    w2_all = jnp.concatenate([w2t] * (rows // LANES), axis=0)
-    group = lax.shift_right_logical(lax.broadcasted_iota(jnp.int32, w2_all.shape, 0), 3)
-    clear_rows(bufs)
-    sides = ((own_list, dt_own_ref, pos_own_ref, 0), (prev_list, dt_prev_ref, pos_prev_ref, 2),
-             (next_list, dt_next_ref, pos_next_ref, 1))
-    for (take_ref, put_ref, num_ref, lw_ref), dt_ref, pos_ref, kind in sides:
-        dt_cols = jnp.transpose(dt_ref[...].astype(F32)).astype(BF16)
-
-        def widen(i, carry):
-            d_hid = jnp.dot(dt_cols, jnp.where(group == i, w2_all, 0.0).astype(BF16), preferred_element_type=F32)
-            at = pl.ds(pl.multiple_of(i * LANES, LANES), LANES)
-            to_rows(jnp.where(pos_ref[at, :].astype(F32) > 0.0, d_hid, 0.0), tables, i * LANES)
-            return carry
-
-        lax.fori_loop(0, rows // LANES, widen, 0)
-        first = 0
-        for k in range(kind):
-            first = first + num_ref[0, k]
-        last = first + num_ref[0, kind]
-        spread_weights(lw_ref, wide, *list_rows(first, last))
-        row_loop(take_ref, put_ref, wide, tables, bufs, first, last)
-
-    def finish(i, carry):
-        d_tab[pl.ds(pl.multiple_of(i * LANES, LANES), LANES), :] = sum_rows(bufs, i).astype(BF16)
+        d_tab[at, :] = (part_ref[at, :] + sum_rows(bufs, i)).astype(BF16)
         return carry
 
     lax.fori_loop(0, rows // LANES, finish, 0)
@@ -346,16 +419,19 @@
     return jnp.concatenate(three_pieces(val), axis=0).astype(BF16)
 
 
-def k3_body(num_dev, tab_ref, send_ref, src_ref, dst_ref, w_ref, lab_ref, mask_ref, cnt_ref, hid_ref, pos_ref,
+def k3_body(num_dev, tab_ref, send_ref, src_ref, dst_ref, w_ref, lab_ref, mask_ref, hid_ref, pos_ref,
             lpair_ref, lw_ref, num_ref,
             dt_ref, misc_ref, dt_prev_ref, dt_next_ref, pos_prev_ref, pos_next_ref, dst_prev_ref, dst_next_ref,
-            tgt_prev_ref, tgt_next_ref, w_prev_ref, w_next_ref, num_prev_ref, num_next_ref, pairs,
-            ext_b, fwd_send, fwd_recv, bwd_send, bwd_recv, acc_z, acc_s, acc_r, dz_b, cnt_recv,
+            put_prev_ref, put_next_ref, w_prev_ref, w_next_ref, nums_ref, names_ref, pairs, nums,
+            ext_b, fwd_send, fwd_recv, bwd_send, bwd_recv, acc_z, acc_s, acc_r, dz_b, cnt_send, cnt_recv,
             sems, cnt_sems, list_sems, pos_sems):
     me, nxt, prv = ring_peers(num_dev)
     layers = layer_peers(me, num_dev)
-    meet([nxt, prv] + layers)
-    counts = [remote(cnt_ref, cnt_recv.at[k], cnt_sems, k, dev) for k, dev in enumerate(layers)]
+    layer = [me - me % PLANE + (me % PLANE + k) % PLANE for k in range(1, PLANE)]
+    meet([nxt, prv] + layer + layers)
+    total = jnp.sum(jnp.sum(mask_ref[...].astype(F32), axis=1, keepdims=True), axis=0, keepdims=True)
+    cnt_send[0] = jnp.broadcast_to(total, cnt_send.shape[1:])
+    counts = [remote(cnt_send.at[0], cnt_recv.at[k], cnt_sems, k, dev) for k, dev in enumerate(layer)]
     for copy in counts:
         copy.start()
     late = []
@@ -367,7 +443,7 @@
                 copy.start()
                 late.append(copy)
 
-    chunk = pos_ref.shape[0] // 4
+    chunk = pos_ref.shape[0] // 2
 
     def send_pos(q):
         at = pl.ds(q * chunk, chunk)
@@ -388,7 +464,16 @@
         copy.start()
         copies.append(copy)
     send_late([(lpair_ref, [pairs.at[0], pairs.at[1]]), (lw_ref, [w_prev_ref, w_next_ref]),
-               (num_ref, [num_prev_ref, num_next_ref])], list_sems, 0)
+               (num_ref, [nums.at[0], nums.at[1]])], list_sems, 0)
+    for copy in counts:
+        copy.wait()
+    for k in range(len(layer)):
+        total = total + cnt_recv[k][0:1, 0:1]
+    cnt_send[1] = jnp.broadcast_to(total, cnt_send.shape[1:])
+    counts = [remote(cnt_send.at[1], cnt_recv.at[len(layer) + k], cnt_sems, len(layer) + k, dev)
+              for k, dev in enumerate(layers)]
+    for copy in counts:
+        copy.start()
     send_pos(0)
     send_pos(1)
     acc_z[...] = jnp.zeros_like(acc_z)
@@ -414,10 +499,10 @@
 
     logits = join_pieces(acc_z[...], own_hi)
     cls = lax.broadcasted_iota(jnp.int32, (CLASS_ROWS, LANES), 0)
-    count = cnt_ref[0:1, :]
+    count = jnp.broadcast_to(total, (1, LANES))
     for k, copy in enumerate(counts):
         copy.wait()
-        count = count + cnt_recv[k][0:1, :]
+        count = count + cnt_recv[len(layer) + k][0:1, :]
     count = jnp.maximum(count, 1.0)
     loss = jnp.zeros((1, LANES), F32)
     d_log = []
@@ -449,7 +534,6 @@
         copy = remote(bwd_send.at[r], bwd_recv.at[1 - r], sems, 2 + r, prv if r == 0 else nxt)
         copy.start()
         copies.append(copy)
-    send_pos(2)
     for copy in copies:
         copy.wait()
     for r in range(2):
@@ -459,7 +543,6 @@
     d_tab = [d_ext[h] + back[h] for h in range(own_hi)]
     dt_ref[...] = jnp.concatenate(d_tab, axis=0).astype(BF16)
     send_late([(dt_ref, [dt_prev_ref, dt_next_ref])], list_sems, 3)
-    send_pos(3)
     grad = jnp.zeros((CLASS_ROWS, hid_ref.shape[1]), F32)
     for h in range(own_hi):
         grad = grad + jnp.dot(d_tab[h].astype(BF16), hid_ref[pl.ds(h * LANES, LANES), :], preferred_element_type=F32)
@@ -468,9 +551,13 @@
     misc_ref[8:16, :] = jnp.broadcast_to(total, (8, misc_ref.shape[1]))
     for copy in late:
         copy.wait()
-    for s, (dst_ref_, tgt_ref_) in enumerate(((dst_prev_ref, tgt_prev_ref), (dst_next_ref, tgt_next_ref))):
-        dst_ref_[...] = pairs[s] & 0xFFFF
-        tgt_ref_[...] = lax.shift_right_logical(pairs[s], 16)
+    for s, (to_dst, to_put) in enumerate(((dst_prev_ref, put_prev_ref), (dst_next_ref, put_next_ref))):
+        to_dst[...] = pairs[s] & 0xFFFF
+        to_put[...] = lax.shift_right_logical(pairs[s], 16)
+    row = lax.broadcasted_iota(jnp.int32, nums_ref.shape, 0)
+    nums_ref[...] = jnp.where(row == 0, num_ref[0:1, :], jnp.where(row == 1, nums[0, 0:1, :], nums[1, 0:1, :]))
+    names_ref[...] = 2 * jnp.concatenate(
+        [send_ref[r:r + 1, j * LANES:(j + 1) * LANES] for r in (1, 0) for j in range(halo_hi)], axis=0)
 
 
 def k5_body(num_dev, part_ref, full_ref, land_core, land_chip, land_z, by_core, by_chip, sems):
@@ -576,58 +663,84 @@
         lab2, mask2 = labels.reshape(own_hi, LANES), label_mask.reshape(own_hi, LANES)
         listed = (LIST_ROWS, LANES)
         entries = LIST_ROWS * LANES
-
-        own, halo_rows, count, lsrc, ldst, ltgt, lpair, lw, num = pl.pallas_call(
-            functools.partial(k1_body, num_dev),
-            out_shape=(arr(BF16, rows, width), arr(BF16, 2 * halo, width), arr(F32, 8, LANES), arr(I32, *listed),
-                       arr(I32, *listed), arr(I32, *listed), arr(I32, *listed), arr(F32, *listed), arr(I32, 8, LANES)),
-            in_specs=[vmem()] * 7, out_specs=(vmem(),) * 9,
-            scratch_shapes=[scr(BF16, width, rows), scr(BF16, 2 * halo, width), scr(I32, 2, 2, halo), scr(F32, 8, LANES),
-                            scr(F32, PLANE - 1, 8, LANES), scr(I32, edges // LANES, LANES), scr(F32, 8 * LIST_ROWS, LANES),
-                            dma(4), dma(2), dma(PLANE - 1)],
-            compiler_params=params(0), name="transform_and_halo",
-        )(feats_t, w_one, send_rows, mask2, src2, dst2, ew2)
-
-        hid, pos, tab = pl.pallas_call(
-            k2_body,
-            out_shape=(arr(BF16, rows, width), arr(BF16, rows, width), arr(F32, own_hi * CLASS_ROWS, LANES)),
-            in_specs=[vmem(), vmem(), smem(), smem(), smem(), vmem(), vmem()], out_specs=(vmem(),) * 3,
-            scratch_shapes=[scr(F32, 2 * (rows + 2 * halo), LANES), scr(F32, entries, LANES)]
-            + [scr(F32, 2 * rows, LANES)] * NUM_BUFS,
-            compiler_params=params(), name="aggregate_one",
-        )(own, halo_rows, lsrc.reshape(entries), ldst.reshape(entries), num, lw, w2)
+        fast_list = pltpu.SMEM(listed, I32)
+        list_dma = dma(entries // CHUNK)
+
+        half = rows // 2
+        busy = pl.CostEstimate(flops=8 * 10**9, bytes_accessed=10**7, transcendentals=0)
+        own_t, to_next, to_prev = pl.pallas_call(
+            k1_body,
+            out_shape=(arr(BF16, width, rows), arr(BF16, halo, width), arr(BF16, halo, width)),
+            in_specs=[pl.BlockSpec(memory_space=pltpu.HBM)] * 3, out_specs=(vmem(),) * 3,
+            scratch_shapes=[scr(BF16, feats, rows), scr(F32, feats, width), pltpu.VMEM((2, halo), I32),
+                            pltpu.SemaphoreType.DMA((3,))],
+            compiler_params=params(), name="transform",
+        )(feats_t, w_one, send_rows)
+        from_prev = lax.ppermute(to_next, GRAPH_AXIS, [(g, (g + 1) % num_dev) for g in range(num_dev)])
+        from_next = lax.ppermute(to_prev, GRAPH_AXIS, [(g, (g - 1) % num_dev) for g in range(num_dev)])
+
+        bufs = [scr(F32, 2 * rows, LANES)] * NUM_BUFS
+        lists_in = (arr(I32, *listed), arr(I32, *listed), arr(I32, *listed), arr(F32, *listed), arr(I32, 8, LANES))
+        part_own, lsrc, ldst, lpair, lw, num = pl.pallas_call(
+            k2a_body,
+            out_shape=(arr(F32, rows, width),) + lists_in,
+            in_specs=[vmem()] * 4, out_specs=(vmem(),) * 6,
+            scratch_shapes=[scr(I32, edges // LANES, LANES), scr(F32, 6 * LIST_ROWS, LANES), scr(F32, 2 * rows, LANES),
+                            scr(F32, entries, LANES), pltpu.SMEM((8, LANES), I32), fast_list, fast_list,
+                            pltpu.SemaphoreType.DMA, list_dma] + bufs,
+            compiler_params=params(), cost_estimate=busy, name="aggregate_own",
+        )(own_t, src2, dst2, ew2)
+
+        hid, pos_a, pos_b, tab = pl.pallas_call(
+            k2b_body,
+            out_shape=(arr(BF16, rows, width), arr(BF16, half, width), arr(BF16, half, width),
+                       arr(F32, own_hi * CLASS_ROWS, LANES)),
+            in_specs=[vmem(), vmem(), vmem(), hbm(), hbm(), smem(), vmem(), vmem()], out_specs=(vmem(),) * 4,
+            scratch_shapes=[scr(F32, 4 * halo, LANES), scr(F32, entries, LANES), fast_list, fast_list, list_dma] + bufs,
+            compiler_params=params(), name="aggregate_halo",
+        )(part_own, from_prev, from_next, lsrc, ldst, num, lw, w2)
 
         num_z = num_dev // PLANE
         tab_b = arr(BF16, own_hi * CLASS_ROWS, LANES)
-        (d_tab, misc, d_prev, d_next, pos_prev, pos_next, dst_prev, dst_next, tgt_prev, tgt_next, w_prev, w_next,
-         num_prev, num_next) = pl.pallas_call(
+        pos_half = arr(BF16, half, width)
+        list_i = arr(I32, *listed)
+        (d_tab, misc, d_prev, d_next, prev_a, next_a, dst_prev, dst_next, put_prev, put_next, w_prev, w_next,
+         nums, names) = pl.pallas_call(
             functools.partial(k3_body, num_dev),
-            out_shape=(tab_b, arr(F32, 16, width), tab_b, tab_b, arr(BF16, rows, width), arr(BF16, rows, width),
-                       arr(I32, *listed), arr(I32, *listed), arr(I32, *listed), arr(I32, *listed),
-                       arr(F32, *listed), arr(F32, *listed), arr(I32, 8, LANES), arr(I32, 8, LANES)),
-            in_specs=[vmem()] * 13, out_specs=(vmem(),) * 14,
-            scratch_shapes=[scr(I32, 2, *listed), scr(BF16, all_hi * CLASS_ROWS, LANES), scr(BF16, 2, 16, halo),
-                            scr(BF16, 2, 16, halo), scr(F32, 2, CLASS_ROWS, halo), scr(F32, 2, CLASS_ROWS, halo),
-                            scr(F32, own_hi * 24, LANES), scr(F32, all_hi * 24, LANES), scr(F32, own_hi * 24, LANES),
-                            scr(BF16, 3 * own_hi * CLASS_ROWS, LANES), scr(F32, num_z - 1, 8, LANES),
-                            dma(4), dma(num_z - 1), dma(8), dma(8)],
+            out_shape=(tab_b, arr(F32, 16, width), tab_b, tab_b, pos_half, pos_half, list_i, list_i, list_i, list_i,
+                       arr(F32, *listed), arr(F32, *listed), arr(I32, 8, LANES), arr(I32, 2 * halo // LANES, LANES)),
+            in_specs=[vmem()] * 12, out_specs=(vmem(),) * 14,
+            scratch_shapes=[scr(I32, 2, *listed), scr(I32, 2, 8, LANES), scr(BF16, all_hi * CLASS_ROWS, LANES),
+                            scr(BF16, 2, 16, halo), scr(BF16, 2, 16, halo), scr(F32, 2, CLASS_ROWS, halo),
+                            scr(F32, 2, CLASS_ROWS, halo), scr(F32, own_hi * 24, LANES), scr(F32, all_hi * 24, LANES),
+                            scr(F32, own_hi * 24, LANES), scr(BF16, 3 * own_hi * CLASS_ROWS, LANES),
+                            scr(F32, 2, 8, LANES), scr(F32, PLANE + num_z - 2, 8, LANES),
+                            dma(4), dma(PLANE + num_z - 2), dma(8), dma(4)],
             compiler_params=params(1), name="layer_two",
-        )(tab, send_rows, src2, dst2, ew2, lab2, mask2, count, hid, pos, lpair, lw, num)
-
-        def k4(own_take, own_put, own_num, own_w, p_take, p_put, p_num, p_w, n_take, n_put, n_num, n_w, *rest):
-            k4_body((own_take, own_put, own_num, own_w), (p_take, p_put, p_num, p_w), (n_take, n_put, n_num, n_w), *rest)
+        )(tab, send_rows, src2, dst2, ew2, lab2, mask2, hid, pos_a, lpair, lw, num)
+
+        pos_b_late, d_tab = lax.optimization_barrier((pos_b, d_tab))
+        prev_b = lax.ppermute(pos_b_late, GRAPH_AXIS, [(g, (g + 1) % num_dev) for g in range(num_dev)])
+        next_b = lax.ppermute(pos_b_late, GRAPH_AXIS, [(g, (g - 1) % num_dev) for g in range(num_dev)])
+        part_own = pl.pallas_call(
+            k4a_body,
+            out_shape=arr(F32, rows, width),
+            in_specs=[hbm(), hbm(), smem()] + [vmem()] * 5, out_specs=vmem(),
+            scratch_shapes=[scr(F32, 2 * rows, LANES), scr(F32, entries, LANES), fast_list, fast_list, list_dma] + bufs,
+            compiler_params=params(), cost_estimate=busy, name="scatter_own",
+        )(ldst, lsrc, num, lw, pos_a, pos_b, d_tab, w2)
 
         sum_rows_pad = 512
         part = pl.pallas_call(
-            k4,
+            k4b_body,
             out_shape=arr(F32, sum_rows_pad, width),
-            in_specs=[smem(), smem(), smem(), vmem()] * 3 + [vmem()] * 9, out_specs=vmem(),
-            scratch_shapes=[scr(F32, 2 * rows, LANES), scr(F32, entries, LANES), scr(BF16, rows, width)] + [scr(F32, 2 * rows, LANES)] * NUM_BUFS,
-            compiler_params=params(), name="scatter_one",
-        )(ldst.reshape(entries), ltgt.reshape(entries), num, lw,
-          dst_prev.reshape(entries), tgt_prev.reshape(entries), num_prev, w_prev,
-          dst_next.reshape(entries), tgt_next.reshape(entries), num_next, w_next,
-          pos, pos_prev, pos_next, d_tab, d_prev, d_next, w2, feats_t, misc)
+            in_specs=[vmem(), smem(), smem()] + [hbm(), hbm(), vmem()] * 2 + [vmem()] * 9, out_specs=vmem(),
+            scratch_shapes=[scr(F32, 2 * rows, LANES), scr(F32, entries, LANES), scr(BF16, rows, width)]
+            + [fast_list] * 4 + [list_dma] * 2 + bufs,
+            compiler_params=params(), name="scatter_peers",
+        )(part_own, nums, names.reshape(2 * halo), dst_prev, put_prev, w_prev,
+          dst_next, put_next, w_next,
+          d_prev, prev_a, prev_b, d_next, next_a, next_b, w2, feats_t, misc)
 
         n1, n2 = sum_rows_pad // 2, sum_rows_pad // 8
         n3 = n2 // num_z

time: 134 us -> 120 us (0.90)
  Pallas kernels: 134 us -> 105 us
  starting transfers between devices: 0 us -> 11.9 us
  local copies, waits for them, and re-layouts: 0 us -> 3.35 us
    ppermute x0 -> x4, starting transfers between devices: none -> 11.9 us  [the longest x1 5.98 us: device_step(): lax.ppermute(to_prev, GRAPH_AXIS, [(g, (g - 1) % num_dev) for g in range(...]
    pallas_call x1, Pallas kernels: 31.8 us -> 21.3 us  [device_step(): pl.pallas_call(functools.partial(k5_body, num_dev), out_shape=arr(F32, su...]
    pallas_call x1, Pallas kernels: 38.6 us -> 28.3 us  [device_step(): pl.pallas_call(functools.partial(k3_body, num_dev), out_shape=(tab_b, arr...]
    pallas_call x3 -> x5, Pallas kernels: 61.3 us -> 54.8 us  [the longest x1 16.6 us: device_step(): pl.pallas_call(k2a_body, out_shape=(arr(F32, rows, width),) + lists_in, i...]
    unnamed x0 -> x22, local copies, waits for them, and re-layouts: none -> 3.35 us
  transfers between devices with their start and end apart: 0 -> 4, of which waited for: 0 -> 0; matrix products, arithmetic and copies ran while one was open for 0% -> 0% of each run, Pallas kernels for 0% -> 25%
where the time goes in v4:
time: 120 us; the launch traced here: 121 us
  Pallas kernels  105 us (88%)
  starting transfers between devices  11.9 us (10%)
  local copies, waits for them, and re-layouts  3.35 us (3%)
    pallas_call x1, Pallas kernels, device_step(): pl.pallas_call(functools.partial(k3_body, num_dev), out_shape=(tab_b, arr...  28.3 us
    pallas_call x1, Pallas kernels, device_step(): pl.pallas_call(functools.partial(k5_body, num_dev), out_shape=arr(F32, su...  21.3 us
    pallas_call x1, Pallas kernels, device_step(): pl.pallas_call(k2a_body, out_shape=(arr(F32, rows, width),) + lists_in, i...  16.6 us
    pallas_call x1, Pallas kernels, device_step(): pl.pallas_call(k4a_body, out_shape=arr(F32, rows, width), in_specs=[hbm()...  13.7 us
    pallas_call x1, Pallas kernels, device_step(): pl.pallas_call(k4b_body, out_shape=arr(F32, sum_rows_pad, width), in_spec...  10.6 us
    pallas_call x1, Pallas kernels, device_step(): pl.pallas_call(k1_body, out_shape=(arr(BF16, width, rows), arr(BF16, halo...  7.05 us
    pallas_call x1, Pallas kernels, device_step(): pl.pallas_call(k2b_body, out_shape=(arr(BF16, rows, width), arr(BF16, hal...  6.77 us
    ppermute x1, starting transfers between devices, device_step(): lax.ppermute(to_prev, GRAPH_AXIS, [(g, (g - 1) % num_dev) for g in range(...  5.98 us
  transfers between devices with their start and end apart: 4, of which 0 were waited for; matrix products, arithmetic and copies ran while one was open for 0% of the time, Pallas kernels for 25%

profile of v4, /device:TPU:0, one launch (start us, length us, event | category | flops | bytes accessed | tf_op | source)
XLA Modules:
  0.0 121.3 jit_solution(17550092740382775084)
XLA Ops:
  0.6 0.0 copy-start
  0.6 1.6 %copy-done = bf16[2048,500]{0,1:T(8,128)(2,1)S(1)} copy-done((bf16[2048,500]{0,1:T(8,128)(2,1)S(1)}, bf16[2048,500]{0,1:T(8,128)(2,1)}, u32[]{:S(2)}) %copy-start) | copy-done | bytes 2048024
  2.2 0.0 copy-start.2
  2.2 1.0 copy-done.2
  3.3 0.0 copy-start.6
  3.3 0.7 copy-done.6
  4.0 0.0 copy-start.3
  4.0 0.0 copy-start.4
  4.0 0.0 copy-start.5
  4.0 7.0 %transform.1 = (bf16[256,2048]{1,0:T(8,128)(2,1)S(1)}, bf16[1024,256]{1,0:T(8,128)(2,1)S(1)}, bf16[1024,256]{1,0:T(8,128)(2,1)S(1)}) custom-call(bf16[500,2048]{1,0:T(8,128)(2,1)S(1)} %bitcast.10, f32[500,256]{1,0:T(8,128)S(1)} %copy-done.2, s32[2,1024]{1,0:T(2,128)S(1)} %copy-done.6), custom_call_target="tpu_custom_call" | custom-call | tf_op jit(solution)/shard_map/transform/pallas_call | solution.py:671
  11.0 0.6 collective-permute-start
  11.6 6.0 %collective-permute-start.1 = (bf16[1024,256]{1,0:T(8,128)(2,1)S(1)}, bf16[1024,256]{1,0:T(8,128)(2,1)S(1)}, u32[]{:S(2)}, u32[]{:S(2)}) collective-permute-start(bf16[1024,256]{1,0:T(8,128)(2,1)S(1)} %get-tuple-element.42), channel_id=1, source_target_pairs={{0,31},{1,0},{2,1},{3,2},{4,3},{5,4},{6,5},{7,6},{8,7},{9,8},{10,9... | collective-permute-start | bytes 1572872 | tf_op jit(solution)/shard_map/ppermute | solution.py:680
  17.6 0.0 copy-done.3
  17.6 0.0 copy-done.4
  17.6 0.0 copy-done.5
  17.6 0.0 copy-start.8
  17.6 16.6 %aggregate_own.1 = (f32[2048,256]{1,0:T(8,128)S(1)}, s32[80,128]{1,0:T(8,128)S(1)}, s32[80,128]{1,0:T(8,128)S(1)}, s32[80,128]{1,0:T(8,128)S(1)}, f32[80,128]{1,0:T(8,128)S(1)}, /*index=5*/s32[8,128]{1,0:T(8,128)S(1)}) custom-call(bf16[256,2048]{1,0:T(8,128)(2,1)S(1)} %get-tuple-element.35.own_t_ref, s32[64,128]{1,0:T(8,128)S(1)} %bitcast.12, ...), custom_call_target="tpu_custom_call" | custom-call | flops 8000000000 | bytes 10000000 | tf_op jit(solution)/shard_map/aggregate_own/pallas_call | solution.py:684
  34.2 0.0 copy-start.7
  34.2 0.0 copy-start.9
  34.2 0.0 copy-start.10
  34.3 0.0 collective-permute-done.prev_ref
  34.3 0.0 collective-permute-done.1.next_ref
  34.3 0.0 copy-done.8
  34.3 6.8 %aggregate_halo.1 = (bf16[2048,256]{1,0:T(8,128)(2,1)S(1)}, bf16[1024,256]{1,0:T(8,128)(2,1)S(1)}, bf16[1024,256]{1,0:T(8,128)(2,1)S(1)}, f32[128,128]{1,0:T(8,128)S(1)}) custom-call(f32[2048,256]{1,0:T(8,128)S(1)} %get-tuple-element.40.part_ref, bf16[1024,256]{1,0:T(8,128)(2,1)S(1)} %collective-permute-done.prev_ref, ...), custom_call_target="tpu_custom_call" | custom-call | tf_op jit(solution)/shard_map/aggregate_halo/pallas_call | solution.py:694
  41.1 0.0 copy-done.7
  41.1 0.0 copy-done.9
  41.1 0.0 copy-done.10
  41.1 28.3 %layer_two.1 = (bf16[128,128]{1,0:T(8,128)(2,1)S(1)}, f32[16,256]{1,0:T(8,128)S(1)}, bf16[128,128]{1,0:T(8,128)(2,1)S(1)}, bf16[128,128]{1,0:T(8,128)(2,1)S(1)},...) custom-call(f32[128,128]{1,0:T(8,128)S(1)} %get-tuple-element.45.tab, ...), custom_call_target="tpu_custom_call" | custom-call | tf_op jit(solution)/shard_map/layer_two/pallas_call | solution.py:708
  69.4 0.0 copy-start.1
  69.4 0.1 collective-permute-start.2
  69.5 5.3 %collective-permute-start.3 = (bf16[1024,256]{1,0:T(8,128)(2,1)S(1)}, bf16[1024,256]{1,0:T(8,128)(2,1)S(1)}, u32[]{:S(2)}, u32[]{:S(2)}) collective-permute-start(bf16[1024,256]{1,0:T(8,128)(2,1)S(1)} %get-tuple-element.60.pos_b_ref), channel_id=1, source_target_pairs={{0,31},{1,0},{2,1},{3,2},{4,3},{5,4},{6,5},{7,6},{8,7},{9,8},{10,9... | collective-permute-start | bytes 1572872 | tf_op jit(solution)/shard_map/ppermute | solution.py:724
  74.8 13.7 %scatter_own.1.part_ref = f32[2048,256]{1,0:T(8,128)S(1)} custom-call(s32[80,128]{1,0:T(8,128)S(1)} %get-tuple-element.36.ldst_ref, s32[80,128]{1,0:T(8,128)S(1)} %get-tuple-element.37.lsrc_ref, s32[8,128]{1,0:T(8,128)S(1)} %get-tuple-element.38.num_ref, f32[80,128]{1,0:T(8,128)S(1)} %get-tuple-element.39.lw_ref, ...), custom_call_target="tpu_custom_call" | custom-call | flops 8000000000 | bytes 10000000 | tf_op jit(solution)/shard_map/scatter_own/pallas_call | solution.py:725
  88.5 0.0 collective-permute-done.2.prev_b
  88.6 0.0 collective-permute-done.3.next_b
  88.6 0.0 copy-done.1
  88.6 10.6 %scatter_peers.1.part_ref = f32[512,256]{1,0:T(8,128)S(1)} custom-call(f32[2048,256]{1,0:T(8,128)S(1)} %scatter_own.1.part_ref, s32[8,128]{1,0:T(8,128)S(1)} %get-tuple-element.50.num_ref, s32[2048]{0:T(1024)S(1)} %bitcast.23, s32[80,128]{1,0:T(8,128)S(1)} %get-tuple-element.52.prev_dst, s32[80,128]{1,0:T(8,128)S(1)} %get-tuple-element.53.prev_src, ...), custom_call_target="tpu_custom_call" | custom-call | tf_op jit(solution)/shard_map/scatter_peers/pallas_call | solution.py:734
  99.2 21.3 %sum_gradients.1.full_ref = f32[512,256]{1,0:T(8,128)S(1)} custom-call(f32[512,256]{1,0:T(8,128)S(1)} %scatter_peers.1.part_ref), custom_call_target="tpu_custom_call" | custom-call | tf_op jit(solution)/shard_map/sum_gradients/pallas_call | solution.py:747
  120.5 0.8 outputs.1
Async XLA Ops:
  0.6 1.6 %copy-start = (bf16[2048,500]{0,1:T(8,128)(2,1)S(1)}, bf16[2048,500]{0,1:T(8,128)(2,1)}, u32[]{:S(2)}) copy-start(bf16[2048,500]{0,1:T(8,128)(2,1)} %param.9) | copy-start | bytes 6144004
  2.2 1.0 copy-start.2
  3.3 0.7 copy-start.6
  4.0 13.6 %copy-start.3 = (s32[8192]{0:T(1024)S(1)}, s32[8192]{0:T(1024)}, u32[]{:S(2)}) copy-start(s32[8192]{0:T(1024)} %param.13) | copy-start | bytes 98308
  4.0 13.6 %copy-start.4 = (s32[8192]{0:T(1024)S(1)}, s32[8192]{0:T(1024)}, u32[]{:S(2)}) copy-start(s32[8192]{0:T(1024)} %param.14) | copy-start | bytes 98308
  4.0 13.6 %copy-start.5 = (f32[8192]{0:T(1024)S(1)}, f32[8192]{0:T(1024)}, u32[]{:S(2)}) copy-start(f32[8192]{0:T(1024)} %param.15) | copy-start | bytes 98308
  11.0 23.2 %collective-permute-start = (bf16[1024,256]{1,0:T(8,128)(2,1)S(1)}, bf16[1024,256]{1,0:T(8,128)(2,1)S(1)}, u32[]{:S(2)}, u32[]{:S(2)}) collective-permute-start(bf16[1024,256]{1,0:T(8,128)(2,1)S(1)} %get-tuple-element.41), channel_id=1, source_target_pairs={{0,1},{1,2},{2,3},{3,4},{4,5},{5,6},{6,7},{7,8},{8,9},{9,10},{10,1... | collective-permute-start | bytes 1572872 | tf_op jit(solution)/shard_map/ppermute | solution.py:679
  11.6 22.7 %collective-permute-start.1 = (bf16[1024,256]{1,0:T(8,128)(2,1)S(1)}, bf16[1024,256]{1,0:T(8,128)(2,1)S(1)}, u32[]{:S(2)}, u32[]{:S(2)}) collective-permute-start(bf16[1024,256]{1,0:T(8,128)(2,1)S(1)} %get-tuple-element.42), channel_id=1, source_target_pairs={{0,31},{1,0},{2,1},{3,2},{4,3},{5,4},{6,5},{7,6},{8,7},{9,8},{10,9... | collective-permute-start | bytes 1572872 | tf_op jit(solution)/shard_map/ppermute | solution.py:680
  17.6 16.7 %copy-start.8 = (f32[256,7]{0,1:T(8,128)S(1)}, f32[256,7]{0,1:T(8,128)}, u32[]{:S(2)}) copy-start(f32[256,7]{0,1:T(8,128)} %param.11) | copy-start | bytes 21508
  34.2 6.8 %copy-start.7 = (s32[2,1024]{1,0:T(2,128)S(1)}, s32[2,1024]{1,0:T(2,128)}, u32[]{:S(2)}) copy-start(s32[2,1024]{1,0:T(2,128)} %send_ref.1) | copy-start | bytes 24580
  34.2 6.8 %copy-start.9 = (s32[2048]{0:T(1024)S(1)}, s32[2048]{0:T(1024)}, u32[]{:S(2)}) copy-start(s32[2048]{0:T(1024)} %param.16) | copy-start | bytes 24580
  34.2 6.8 %copy-start.10 = (s32[2048]{0:T(1024)S(1)}, s32[2048]{0:T(1024)}, u32[]{:S(2)}) copy-start(s32[2048]{0:T(1024)} %param.17) | copy-start | bytes 24580
  69.4 19.2 %copy-start.1 = (bf16[2048,500]{0,1:T(8,128)(2,1)S(1)}, bf16[2048,500]{0,1:T(8,128)(2,1)}, u32[]{:S(2)}) copy-start(bf16[2048,500]{0,1:T(8,128)(2,1)} %param.9) | copy-start | bytes 6144004
  69.4 19.1 %collective-permute-start.2 = (bf16[1024,256]{1,0:T(8,128)(2,1)S(1)}, bf16[1024,256]{1,0:T(8,128)(2,1)S(1)}, u32[]{:S(2)}, u32[]{:S(2)}) collective-permute-start(bf16[1024,256]{1,0:T(8,128)(2,1)S(1)} %get-tuple-element.60.pos_b_ref), channel_id=1, source_target_pairs={{0,1},{1,2},{2,3},{3,4},{4,5},{5,6},{6,7},{7,8},{8,9},{9,10},{10,1... | collective-permute-start | bytes 1572872 | tf_op jit(solution)/shard_map/ppermute | solution.py:723
  69.5 19.1 %collective-permute-start.3 = (bf16[1024,256]{1,0:T(8,128)(2,1)S(1)}, bf16[1024,256]{1,0:T(8,128)(2,1)S(1)}, u32[]{:S(2)}, u32[]{:S(2)}) collective-permute-start(bf16[1024,256]{1,0:T(8,128)(2,1)S(1)} %get-tuple-element.60.pos_b_ref), channel_id=1, source_target_pairs={{0,31},{1,0},{2,1},{3,2},{4,3},{5,4},{6,5},{7,6},{8,7},{9,8},{10,9... | collective-permute-start | bytes 1572872 | tf_op jit(solution)/shard_map/ppermute | solution.py:724

commit v5 on v4

--- a/solution.py
+++ b/solution.py
@@ -12,6 +12,8 @@
 LANES = 128
 CLASS_ROWS = 8
 VMEM_BYTES = 28 * 2**20
+K1_VMEM = 50 * 2**20
+OWN_VMEM = 34 * 2**20
 F32 = jnp.float32
 BF16 = jnp.bfloat16
 NT = (((1,), (1,)), ((), ()))
@@ -34,6 +36,8 @@
 LIST_ROWS = 80
 BLOCK = 128
 NUM_BUFS = 4
+OWN_BUFS = 6
+EARLY_ROWS = 768
 CHUNK = 1024
 
 
@@ -76,10 +80,22 @@
     return jnp.concatenate([blk[j:j + 1, :] for j in range(8)], axis=1)
 
 
+def packed(row):
+    return jnp.broadcast_to(row, (16, row.shape[1])).astype(jnp.int16)
+
+
+def hot_rows(row, count):
+    n = row.shape[1]
+    ids = lax.broadcasted_iota(jnp.int32, (count, LANES), 0).astype(jnp.int16)
+    return jnp.concatenate([ids] * (n // LANES), axis=1) == jnp.concatenate([packed(row)] * (count // 16), axis=0)
+
+
+def ones_at(mask):
+    return jnp.where(mask, jnp.ones((), BF16), jnp.zeros((), BF16))
+
+
 def lo_hot(idx):
-    lo = idx & (LANES - 1)
-    node = lax.broadcasted_iota(jnp.int32, (LANES, idx.shape[1]), 0)
-    return (node == lo).astype(F32).astype(BF16)
+    return ones_at(hot_rows(idx & (LANES - 1), LANES))
 
 
 def list_places(src_ref, w_ref, rows, halo, pos, num_ref):
@@ -110,7 +126,7 @@
     num_ref[...] = num
 
 
-def k1_body(xt_hbm, w_hbm, send_hbm, own_t_ref, to_next_ref, to_prev_ref, xt_ref, w_ref, send_ref, sems):
+def k1_body(xt_hbm, w_hbm, send_hbm, own_t_ref, to_next_ref, to_prev_ref, xt_ref, w_ref, send_ref, hot, sems):
     copies = [pltpu.make_async_copy(a, b, sems.at[k])
               for k, (a, b) in enumerate(((send_hbm, send_ref), (w_hbm, w_ref), (xt_hbm, xt_ref)))]
     for copy in copies:
@@ -121,16 +137,16 @@
     blocks = halo // LANES
     ids = jnp.concatenate([send_ref[r:r + 1, b * LANES:(b + 1) * LANES] for r in range(2) for b in range(blocks)], axis=0)
     ids_col = jnp.transpose(ids)
+    node = lax.broadcasted_iota(jnp.int32, (LANES, rows), 1).astype(jnp.int16)
+    for b in range(2 * blocks):
+        col = jnp.broadcast_to(ids_col[:, b:b + 1], (LANES, LANES)).astype(jnp.int16)
+        hot[b * LANES:(b + 1) * LANES, :] = ones_at(node == jnp.concatenate([col] * (rows // LANES), axis=1))
     copies[1].wait()
     w_b = w_ref[...].astype(BF16)
     copies[2].wait()
     own_t_ref[...] = lax.dot_general(w_b, xt_ref[...], TN, preferred_element_type=F32).astype(BF16)
-    node = lax.broadcasted_iota(jnp.int32, (LANES, rows), 1)
     for r, out in ((1, to_next_ref), (0, to_prev_ref)):
-        for b in range(blocks):
-            pick = (node == ids_col[:, r * blocks + b:r * blocks + b + 1]).astype(F32).astype(BF16)
-            out[b * LANES:(b + 1) * LANES, :] = lax.dot_general(
-                pick, own_t_ref[...], NT, preferred_element_type=F32).astype(BF16)
+        out[...] = lax.dot_general(hot[r * halo:(r + 1) * halo, :], own_t_ref[...], NT, preferred_element_type=F32).astype(BF16)
 
 
 def sort_edges(src_ref, dst_ref, ew_ref, rows, halo, pos, acc, lsrc_ref, ldst_ref, lpair_ref, lw_ref, num_ref):
@@ -143,8 +159,9 @@
         both = src + dst * 4096
         ints = [both & 255, lax.shift_right_logical(both, 8) & 255, lax.shift_right_logical(both, 16)]
         cargo = [v.astype(F32) for v in ints] + list(three_pieces(wgt))
-        here = lax.broadcasted_iota(jnp.int32, (LIST_ROWS, src.shape[1]), 0) == lax.shift_right_logical(place, 7)
-        lhs = jnp.concatenate([jnp.where(here, v, 0.0).astype(BF16) for v in cargo], axis=0)
+        here = hot_rows(lax.shift_right_logical(place, 7), LIST_ROWS)
+        cargo = [jnp.concatenate([jnp.broadcast_to(v, (16, v.shape[1])).astype(BF16)] * (LIST_ROWS // 16), axis=0) for v in cargo]
+        lhs = jnp.concatenate([jnp.where(here, v, jnp.zeros((), BF16)) for v in cargo], axis=0)
         acc[...] += lax.dot_general(lhs, lo_hot(place), NT, preferred_element_type=F32)
         return carry
 
@@ -226,6 +243,50 @@
     lax.fori_loop(*chunks_of(first, last), chunk, 0)
 
 
+def slot_copies(lists, slots, sems, c):
+    at = pl.ds(pl.multiple_of(c * 8, 8), 8)
+    return lambda slot: [pltpu.make_async_copy(a.at[at, :], b, sems.at[slot, k]) for k, (a, b) in enumerate(zip(lists, slots[slot]))]
+
+
+def start_slots(lists, slots, sems):
+    for slot in range(2):
+        for copy in slot_copies(lists, slots, sems, slot)(slot):
+            copy.start()
+
+
+def slot_loop(lists, slots, sems, wide, table, bufs, last):
+    num = len(bufs)
+    pairs = jnp.maximum((last + 15) // 16, 1)
+
+    def group(k, carry):
+        for slot in range(2):
+            take_ref, put_ref = slots[slot]
+            for copy in slot_copies(lists, slots, sems, 2 * k + slot)(slot):
+                copy.wait()
+            for r in range(8):
+                row = 16 * k + 8 * slot + r
+
+                @pl.when(row < last)
+                def _():
+                    base = pl.multiple_of(row * LANES, LANES)
+                    for lead in range(0, LANES, num):
+                        here = range(min(num, LANES - lead))
+                        take = [pl.multiple_of(take_ref[r, lead + j], 2) for j in here]
+                        put = [pl.multiple_of(put_ref[r, lead + j], 2) for j in here]
+                        vals = [wide[pl.ds(base + lead + j, 1), :] * table[pl.ds(take[j], 2), :] for j in here]
+                        old = [bufs[j][pl.ds(put[j], 2), :] for j in here]
+                        for j in here:
+                            bufs[j][pl.ds(put[j], 2), :] = old[j] + vals[j]
+
+            @pl.when(k + 1 < pairs)
+            def _():
+                for copy in slot_copies(lists, slots, sems, 2 * k + 2 + slot)(slot):
+                    copy.start()
+        return carry
+
+    lax.fori_loop(0, pairs, group, 0)
+
+
 def list_rows(first, last):
     return first * BLOCK // LANES, (last * BLOCK + LANES - 1) // LANES
 
@@ -240,13 +301,13 @@
     for h in range(2):
         parts = [buf[pl.ds(2 * blk * LANES + h, LANES, stride=2), :] for buf in bufs]
         while len(parts) > 1:
-            parts = [a + b for a, b in zip(parts[::2], parts[1::2])]
+            parts = [a + b for a, b in zip(parts[::2], parts[1::2])] + parts[len(parts) // 2 * 2:]
         halves.append(parts[0])
     return jnp.concatenate(halves, axis=1)
 
 
 def k2a_body(own_t_ref, src_ref, dst_ref, ew_ref, part_ref, lsrc_ref, ldst_ref, lpair_ref, lw_ref, num_ref,
-             pos, acc, table, wide, num_fast, src_fast, dst_fast, num_sem, sems, *bufs):
+             pos, acc, table, wide, num_fast, src_a, dst_a, src_b, dst_b, sems, slot_sems, *bufs):
     rows = part_ref.shape[0]
     sort_edges(src_ref, dst_ref, ew_ref, rows, rows // 2, pos, acc, lsrc_ref, ldst_ref, lpair_ref, lw_ref, num_ref)
 
@@ -256,15 +317,15 @@
         return carry
 
     lax.fori_loop(0, rows // LANES, widen, 0)
+    copy = pltpu.make_async_copy(num_ref, num_fast, sems.at[0])
+    copy.start()
+    lists, slots = (lsrc_ref, ldst_ref), ((src_a, dst_a), (src_b, dst_b))
+    start_slots(lists, slots, slot_sems)
     clear_rows(bufs)
-    copy = pltpu.make_async_copy(num_ref, num_fast, num_sem)
-    copy.start()
     copy.wait()
     end = num_fast[0, 0]
-    lists, fast = (lsrc_ref, ldst_ref), (src_fast, dst_fast)
-    start_lists(lists, fast, sems, 0, end)
     spread_weights(lw_ref, wide, *list_rows(0, end))
-    row_loop(lists, fast, sems, wide, table, bufs, 0, end)
+    slot_loop(lists, slots, slot_sems, wide, table, bufs, end)
 
     def finish(i, carry):
         part_ref[pl.ds(pl.multiple_of(i * LANES, LANES), LANES), :] = sum_rows(bufs, i)
@@ -293,9 +354,7 @@
     row_loop(lists, fast, sems, wide, table, bufs, first, end)
     w2t = class_weights(w2_ref)
 
-    for side, pos_ref in enumerate((pos_a_ref, pos_b_ref)):
-        lead = side * pos_ref.shape[0] // LANES
-
+    for pos_ref, lead in ((pos_a_ref, 0), (pos_b_ref, pos_a_ref.shape[0] // LANES)):
         def finish(j, carry):
             i = lead + j
             at = pl.ds(pl.multiple_of(i * LANES, LANES), LANES)
@@ -317,9 +376,7 @@
 
 def fill_table(dt_ref, pos_refs, w2_all, group, table):
     dt_cols = jnp.transpose(dt_ref[...].astype(F32)).astype(BF16)
-    for side, pos_ref in enumerate(pos_refs):
-        lead = side * pos_ref.shape[0] // LANES
-
+    for pos_ref, lead in zip(pos_refs, (0, pos_refs[0].shape[0] // LANES)):
         def widen(j, carry):
             i = lead + j
             d_hid = jnp.dot(dt_cols, jnp.where(group == i, w2_all, 0.0).astype(BF16), preferred_element_type=F32)
@@ -331,15 +388,15 @@
 
 
 def k4a_body(ldst_ref, lsrc_ref, num_ref, lw_ref, pos_a_ref, pos_b_ref, dt_ref, w2_ref, part_ref,
-             table, wide, take_fast, put_fast, sems, *bufs):
+             table, wide, take_a, put_a, take_b, put_b, slot_sems, *bufs):
     rows = part_ref.shape[0]
-    lists, fast, end = (ldst_ref, lsrc_ref), (take_fast, put_fast), num_ref[0, 0]
-    start_lists(lists, fast, sems, 0, end)
+    lists, slots, end = (ldst_ref, lsrc_ref), ((take_a, put_a), (take_b, put_b)), num_ref[0, 0]
+    start_slots(lists, slots, slot_sems)
     w2_all, group = stack_classes(w2_ref, rows // LANES)
     clear_rows(bufs)
     fill_table(dt_ref, (pos_a_ref, pos_b_ref), w2_all, group, table)
     spread_weights(lw_ref, wide, *list_rows(0, end))
-    row_loop(lists, fast, sems, wide, table, bufs, 0, end)
+    slot_loop(lists, slots, slot_sems, wide, table, bufs, end)
 
     def finish(i, carry):
         part_ref[pl.ds(pl.multiple_of(i * LANES, LANES), LANES), :] = sum_rows(bufs, i)
@@ -398,12 +455,15 @@
 
 
 def add_cols(val, idx, hot, num_hi):
-    hi = hi_of(idx)
-    pieces = three_pieces(val)
+    hi = packed(lax.shift_right_logical(idx, 7))
+    low_half = lax.broadcasted_iota(jnp.int32, hi.shape, 0) >= CLASS_ROWS
+    mixed = hi - low_half.astype(jnp.int32).astype(jnp.int16)
+    top, mid, low = three_pieces(val)
+    pieces = [jnp.concatenate(two, axis=0).astype(BF16) for two in ((top, mid), (low, top), (mid, low))]
     rows = []
     for h in range(0, num_hi, 2):
-        both = [jnp.where(hi == h + k, p, 0.0) for k in range(2) for p in pieces]
-        rows.append(jnp.concatenate(both, axis=0).astype(BF16))
+        masks = (hi == jnp.int16(h), mixed == jnp.int16(h), hi == jnp.int16(h + 1))
+        rows += [jnp.where(m, p, jnp.zeros((), BF16)) for m, p in zip(masks, pieces)]
     return lax.dot_general(jnp.concatenate(rows, axis=0), hot, NT, preferred_element_type=F32)
 
 
@@ -443,7 +503,7 @@
                 copy.start()
                 late.append(copy)
 
-    chunk = pos_ref.shape[0] // 2
+    chunk = pos_ref.shape[0] // 3
 
     def send_pos(q):
         at = pl.ds(q * chunk, chunk)
@@ -465,6 +525,7 @@
         copies.append(copy)
     send_late([(lpair_ref, [pairs.at[0], pairs.at[1]]), (lw_ref, [w_prev_ref, w_next_ref]),
                (num_ref, [nums.at[0], nums.at[1]])], list_sems, 0)
+    send_pos(0)
     for copy in counts:
         copy.wait()
     for k in range(len(layer)):
@@ -474,8 +535,8 @@
               for k, dev in enumerate(layers)]
     for copy in counts:
         copy.start()
-    send_pos(0)
     send_pos(1)
+    send_pos(2)
     acc_z[...] = jnp.zeros_like(acc_z)
     acc_s[...] = jnp.zeros_like(acc_s)
     for copy in copies:
@@ -666,34 +727,35 @@
         fast_list = pltpu.SMEM(listed, I32)
         list_dma = dma(entries // CHUNK)
 
-        half = rows // 2
+        late_rows = rows - EARLY_ROWS
         busy = pl.CostEstimate(flops=8 * 10**9, bytes_accessed=10**7, transcendentals=0)
         own_t, to_next, to_prev = pl.pallas_call(
             k1_body,
             out_shape=(arr(BF16, width, rows), arr(BF16, halo, width), arr(BF16, halo, width)),
             in_specs=[pl.BlockSpec(memory_space=pltpu.HBM)] * 3, out_specs=(vmem(),) * 3,
             scratch_shapes=[scr(BF16, feats, rows), scr(F32, feats, width), pltpu.VMEM((2, halo), I32),
-                            pltpu.SemaphoreType.DMA((3,))],
-            compiler_params=params(), name="transform",
+                            scr(BF16, 2 * halo, rows), pltpu.SemaphoreType.DMA((3,))],
+            compiler_params=pltpu.CompilerParams(vmem_limit_bytes=K1_VMEM), name="transform",
         )(feats_t, w_one, send_rows)
         from_prev = lax.ppermute(to_next, GRAPH_AXIS, [(g, (g + 1) % num_dev) for g in range(num_dev)])
         from_next = lax.ppermute(to_prev, GRAPH_AXIS, [(g, (g - 1) % num_dev) for g in range(num_dev)])
 
-        bufs = [scr(F32, 2 * rows, LANES)] * NUM_BUFS
+        bufs, own_bufs = ([scr(F32, 2 * rows, LANES)] * n for n in (NUM_BUFS, OWN_BUFS))
+        fast_row = pltpu.SMEM((8, LANES), I32)
         lists_in = (arr(I32, *listed), arr(I32, *listed), arr(I32, *listed), arr(F32, *listed), arr(I32, 8, LANES))
         part_own, lsrc, ldst, lpair, lw, num = pl.pallas_call(
             k2a_body,
             out_shape=(arr(F32, rows, width),) + lists_in,
             in_specs=[vmem()] * 4, out_specs=(vmem(),) * 6,
             scratch_shapes=[scr(I32, edges // LANES, LANES), scr(F32, 6 * LIST_ROWS, LANES), scr(F32, 2 * rows, LANES),
-                            scr(F32, entries, LANES), pltpu.SMEM((8, LANES), I32), fast_list, fast_list,
-                            pltpu.SemaphoreType.DMA, list_dma] + bufs,
-            compiler_params=params(), cost_estimate=busy, name="aggregate_own",
+                            scr(F32, entries, LANES), fast_row, fast_row, fast_row, fast_row, fast_row,
+                            pltpu.SemaphoreType.DMA((1,)), dma(2)] + own_bufs,
+            compiler_params=pltpu.CompilerParams(vmem_limit_bytes=OWN_VMEM), cost_estimate=busy, name="aggregate_own",
         )(own_t, src2, dst2, ew2)
 
         hid, pos_a, pos_b, tab = pl.pallas_call(
             k2b_body,
-            out_shape=(arr(BF16, rows, width), arr(BF16, half, width), arr(BF16, half, width),
+            out_shape=(arr(BF16, rows, width), arr(BF16, EARLY_ROWS, width), arr(BF16, late_rows, width),
                        arr(F32, own_hi * CLASS_ROWS, LANES)),
             in_specs=[vmem(), vmem(), vmem(), hbm(), hbm(), smem(), vmem(), vmem()], out_specs=(vmem(),) * 4,
             scratch_shapes=[scr(F32, 4 * halo, LANES), scr(F32, entries, LANES), fast_list, fast_list, list_dma] + bufs,
@@ -702,12 +764,12 @@
 
         num_z = num_dev // PLANE
         tab_b = arr(BF16, own_hi * CLASS_ROWS, LANES)
-        pos_half = arr(BF16, half, width)
+        pos_early = arr(BF16, EARLY_ROWS, width)
         list_i = arr(I32, *listed)
         (d_tab, misc, d_prev, d_next, prev_a, next_a, dst_prev, dst_next, put_prev, put_next, w_prev, w_next,
          nums, names) = pl.pallas_call(
             functools.partial(k3_body, num_dev),
-            out_shape=(tab_b, arr(F32, 16, width), tab_b, tab_b, pos_half, pos_half, list_i, list_i, list_i, list_i,
+            out_shape=(tab_b, arr(F32, 16, width), tab_b, tab_b, pos_early, pos_early, list_i, list_i, list_i, list_i,
                        arr(F32, *listed), arr(F32, *listed), arr(I32, 8, LANES), arr(I32, 2 * halo // LANES, LANES)),
             in_specs=[vmem()] * 12, out_specs=(vmem(),) * 14,
             scratch_shapes=[scr(I32, 2, *listed), scr(I32, 2, 8, LANES), scr(BF16, all_hi * CLASS_ROWS, LANES),
@@ -715,7 +777,7 @@
                             scr(F32, 2, CLASS_ROWS, halo), scr(F32, own_hi * 24, LANES), scr(F32, all_hi * 24, LANES),
                             scr(F32, own_hi * 24, LANES), scr(BF16, 3 * own_hi * CLASS_ROWS, LANES),
                             scr(F32, 2, 8, LANES), scr(F32, PLANE + num_z - 2, 8, LANES),
-                            dma(4), dma(PLANE + num_z - 2), dma(8), dma(4)],
+                            dma(4), dma(PLANE + num_z - 2), dma(8), dma(6)],
             compiler_params=params(1), name="layer_two",
         )(tab, send_rows, src2, dst2, ew2, lab2, mask2, hid, pos_a, lpair, lw, num)
 
@@ -726,8 +788,9 @@
             k4a_body,
             out_shape=arr(F32, rows, width),
             in_specs=[hbm(), hbm(), smem()] + [vmem()] * 5, out_specs=vmem(),
-            scratch_shapes=[scr(F32, 2 * rows, LANES), scr(F32, entries, LANES), fast_list, fast_list, list_dma] + bufs,
-            compiler_params=params(), cost_estimate=busy, name="scatter_own",
+            scratch_shapes=[scr(F32, 2 * rows, LANES), scr(F32, entries, LANES), fast_row, fast_row, fast_row, fast_row,
+                            dma(2)] + own_bufs,
+            compiler_params=pltpu.CompilerParams(vmem_limit_bytes=OWN_VMEM), cost_estimate=busy, name="scatter_own",
         )(ldst, lsrc, num, lw, pos_a, pos_b, d_tab, w2)
 
         sum_rows_pad = 512

time: 120 us -> 116 us (0.967); the launches traced: 121 us -> 116 us
  Pallas kernels: 105 us -> 101 us
  local copies, waits for them, and re-layouts: 3.35 us -> 1.76 us
    pallas_call x1, Pallas kernels: 28.3 us -> 33.6 us  [device_step(): pl.pallas_call(functools.partial(k3_body, num_dev), out_shape=(tab_b, arr...]
    pallas_call x1, Pallas kernels: 16.6 us -> 11.5 us  [device_step(): pl.pallas_call(k2a_body, out_shape=(arr(F32, rows, width),) + lists_in, i...]
    pallas_call x1, Pallas kernels: 13.7 us -> 9.2 us  [device_step(): pl.pallas_call(k4a_body, out_shape=arr(F32, rows, width), in_specs=[hbm()...]
    pallas_call x1, Pallas kernels: 21.3 us -> 25.7 us  [device_step(): pl.pallas_call(functools.partial(k5_body, num_dev), out_shape=arr(F32, su...]
    pallas_call x1, Pallas kernels: 7.05 us -> 4.85 us  [device_step(): pl.pallas_call(k1_body, out_shape=(arr(BF16, width, rows), arr(BF16, halo...]
    unnamed x22 -> x18, local copies, waits for them, and re-layouts: 3.35 us -> 1.76 us
  transfers between devices with their start and end apart: 4 -> 4, of which waited for: 0 -> 0; matrix products, arithmetic and copies ran while one was open for 0% -> 0% of each run, Pallas kernels for 25% -> 18%
where the time goes in v5:
time: 116 us
  Pallas kernels  101 us (87%)
  starting transfers between devices  11.9 us (10%)
  local copies, waits for them, and re-layouts  1.76 us (2%)
    pallas_call x1, Pallas kernels, device_step(): pl.pallas_call(functools.partial(k3_body, num_dev), out_shape=(tab_b, arr...  33.6 us
    pallas_call x1, Pallas kernels, device_step(): pl.pallas_call(functools.partial(k5_body, num_dev), out_shape=arr(F32, su...  25.7 us
    pallas_call x1, Pallas kernels, device_step(): pl.pallas_call(k2a_body, out_shape=(arr(F32, rows, width),) + lists_in, i...  11.5 us
    pallas_call x1, Pallas kernels, device_step(): pl.pallas_call(k4b_body, out_shape=arr(F32, sum_rows_pad, width), in_spec...  9.8 us
    pallas_call x1, Pallas kernels, device_step(): pl.pallas_call(k4a_body, out_shape=arr(F32, rows, width), in_specs=[hbm()...  9.2 us
    pallas_call x1, Pallas kernels, device_step(): pl.pallas_call(k2b_body, out_shape=(arr(BF16, rows, width), arr(BF16, EAR...  6.02 us
    ppermute x1, starting transfers between devices, device_step(): lax.ppermute(to_prev, GRAPH_AXIS, [(g, (g - 1) % num_dev) for g in range(...  5.98 us
    ppermute x1, starting transfers between devices, device_step(): lax.ppermute(pos_b_late, GRAPH_AXIS, [(g, (g - 1) % num_dev) for g in ran...  5.33 us
  transfers between devices with their start and end apart: 4, of which 0 were waited for; matrix products, arithmetic and copies ran while one was open for 0% of the time, Pallas kernels for 18%

profile of v5, /device:TPU:0, one launch (start us, length us, event | category | flops | bytes accessed | tf_op | source)
XLA Modules:
  0.0 116.0 jit_solution(17941631221649256992)
XLA Ops:
  0.6 0.0 copy-start.1
  0.6 1.0 copy-done.1
  1.7 0.0 copy-start.2
  1.7 0.7 copy-done.2
  2.4 0.0 copy-start.4
  2.4 0.0 copy-start.5
  2.4 0.0 copy-start.6
  2.4 4.8 %transform.1 = (bf16[256,2048]{1,0:T(8,128)(2,1)S(1)}, bf16[1024,256]{1,0:T(8,128)(2,1)S(1)}, bf16[1024,256]{1,0:T(8,128)(2,1)S(1)}) custom-call(bf16[500,2048]{1,0:T(8,128)(2,1)} %bitcast.10, f32[500,256]{1,0:T(8,128)S(1)} %copy-done.1, s32[2,1024]{1,0:T(2,128)S(1)} %copy-done.2), custom_call_target="tpu_custom_call" | custom-call | tf_op jit(solution)/shard_map/transform/pallas_call | solution.py:732
  7.2 0.6 collective-permute-start
  7.8 6.0 %collective-permute-start.1 = (bf16[1024,256]{1,0:T(8,128)(2,1)S(1)}, bf16[1024,256]{1,0:T(8,128)(2,1)S(1)}, u32[]{:S(2)}, u32[]{:S(2)}) collective-permute-start(bf16[1024,256]{1,0:T(8,128)(2,1)S(1)} %get-tuple-element.42), channel_id=1, source_target_pairs={{0,31},{1,0},{2,1},{3,2},{4,3},{5,4},{6,5},{7,6},{8,7},{9,8},{10,9... | collective-permute-start | bytes 1572872 | tf_op jit(solution)/shard_map/ppermute | solution.py:741
  13.8 0.0 copy-done.4
  13.8 0.0 copy-done.5
  13.8 0.0 copy-done.6
  13.8 0.0 copy-start.3
  13.8 11.5 %aggregate_own.1 = (f32[2048,256]{1,0:T(8,128)S(1)}, s32[80,128]{1,0:T(8,128)S(1)}, s32[80,128]{1,0:T(8,128)S(1)}, s32[80,128]{1,0:T(8,128)S(1)}, f32[80,128]{1,0:T(8,128)S(1)}, /*index=5*/s32[8,128]{1,0:T(8,128)S(1)}) custom-call(bf16[256,2048]{1,0:T(8,128)(2,1)S(1)} %get-tuple-element.35.own_t_ref, s32[64,128]{1,0:T(8,128)S(1)} %bitcast.15, ...), custom_call_target="tpu_custom_call" | custom-call | flops 8000000000 | bytes 10000000 | tf_op jit(solution)/shard_map/aggregate_own/pallas_call | solution.py:746
  25.3 0.0 copy-start.7
  25.3 0.0 copy-start.8
  25.3 0.0 collective-permute-done.prev_ref
  25.3 0.0 collective-permute-done.1.next_ref
  25.3 0.0 copy-done.3
  25.3 6.0 %aggregate_halo.1 = (bf16[2048,256]{1,0:T(8,128)(2,1)S(1)}, bf16[768,256]{1,0:T(8,128)(2,1)S(1)}, bf16[1280,256]{1,0:T(8,128)(2,1)S(1)}, f32[128,128]{1,0:T(8,128)S(1)}) custom-call(f32[2048,256]{1,0:T(8,128)S(1)} %get-tuple-element.40.part_ref, bf16[1024,256]{1,0:T(8,128)(2,1)S(1)} %collective-permute-done.prev_ref, ...), custom_call_target="tpu_custom_call" | custom-call | tf_op jit(solution)/shard_map/aggregate_halo/pallas_call | solution.py:756
  31.4 0.0 copy-done.7
  31.4 0.0 copy-done.8
  31.4 33.6 %layer_two.1 = (bf16[128,128]{1,0:T(8,128)(2,1)S(1)}, f32[16,256]{1,0:T(8,128)S(1)}, bf16[128,128]{1,0:T(8,128)(2,1)S(1)}, bf16[128,128]{1,0:T(8,128)(2,1)S(1)},...) custom-call(f32[128,128]{1,0:T(8,128)S(1)} %get-tuple-element.45.tab, ...), custom_call_target="tpu_custom_call" | custom-call | tf_op jit(solution)/shard_map/layer_two/pallas_call | solution.py:770
  65.0 0.0 copy-start
  65.0 0.1 collective-permute-start.2
  65.0 5.3 %collective-permute-start.3 = (bf16[1280,256]{1,0:T(8,128)(2,1)S(1)}, bf16[1280,256]{1,0:T(8,128)(2,1)S(1)}, u32[]{:S(2)}, u32[]{:S(2)}) collective-permute-start(bf16[1280,256]{1,0:T(8,128)(2,1)S(1)} %get-tuple-element.60.pos_b_ref), channel_id=1, source_target_pairs={{0,31},{1,0},{2,1},{3,2},{4,3},{5,4},{6,5},{7,6},{8,7},{9,8},{10,9... | collective-permute-start | bytes 1966088 | tf_op jit(solution)/shard_map/ppermute | solution.py:786
  70.4 9.2 %scatter_own.1.part_ref = f32[2048,256]{1,0:T(8,128)S(1)} custom-call(s32[80,128]{1,0:T(8,128)S(1)} %get-tuple-element.36.ldst_ref, s32[80,128]{1,0:T(8,128)S(1)} %get-tuple-element.37.lsrc_ref, s32[8,128]{1,0:T(8,128)S(1)} %get-tuple-element.38.num_ref, f32[80,128]{1,0:T(8,128)S(1)} %get-tuple-element.39.lw_ref, ...), custom_call_target="tpu_custom_call" | custom-call | flops 8000000000 | bytes 10000000 | tf_op jit(solution)/shard_map/scatter_own/pallas_call | solution.py:787
  79.6 0.0 collective-permute-done.2.prev_b
  79.6 0.0 collective-permute-done.3.next_b
  79.6 0.0 copy-done
  79.6 9.8 %scatter_peers.1.part_ref = f32[512,256]{1,0:T(8,128)S(1)} custom-call(f32[2048,256]{1,0:T(8,128)S(1)} %scatter_own.1.part_ref, s32[8,128]{1,0:T(8,128)S(1)} %get-tuple-element.50.num_ref, s32[2048]{0:T(1024)S(1)} %bitcast.23, s32[80,128]{1,0:T(8,128)S(1)} %get-tuple-element.52.prev_dst, s32[80,128]{1,0:T(8,128)S(1)} %get-tuple-element.53.prev_src, ...), custom_call_target="tpu_custom_call" | custom-call | tf_op jit(solution)/shard_map/scatter_peers/pallas_call | solution.py:797
  89.4 25.7 %sum_gradients.1.full_ref = f32[512,256]{1,0:T(8,128)S(1)} custom-call(f32[512,256]{1,0:T(8,128)S(1)} %scatter_peers.1.part_ref), custom_call_target="tpu_custom_call" | custom-call | tf_op jit(solution)/shard_map/sum_gradients/pallas_call | solution.py:810
  115.2 0.8 outputs.1
Async XLA Ops:
  0.6 1.0 copy-start.1
  1.7 0.7 copy-start.2
  2.4 11.4 %copy-start.4 = (s32[8192]{0:T(1024)S(1)}, s32[8192]{0:T(1024)}, u32[]{:S(2)}) copy-start(s32[8192]{0:T(1024)} %param.13) | copy-start | bytes 98308
  2.4 11.4 %copy-start.5 = (s32[8192]{0:T(1024)S(1)}, s32[8192]{0:T(1024)}, u32[]{:S(2)}) copy-start(s32[8192]{0:T(1024)} %param.14) | copy-start | bytes 98308
  2.4 11.4 %copy-start.6 = (f32[8192]{0:T(1024)S(1)}, f32[8192]{0:T(1024)}, u32[]{:S(2)}) copy-start(f32[8192]{0:T(1024)} %param.15) | copy-start | bytes 98308
  7.2 18.1 %collective-permute-start = (bf16[1024,256]{1,0:T(8,128)(2,1)S(1)}, bf16[1024,256]{1,0:T(8,128)(2,1)S(1)}, u32[]{:S(2)}, u32[]{:S(2)}) collective-permute-start(bf16[1024,256]{1,0:T(8,128)(2,1)S(1)} %get-tuple-element.41), channel_id=1, source_target_pairs={{0,1},{1,2},{2,3},{3,4},{4,5},{5,6},{6,7},{7,8},{8,9},{9,10},{10,1... | collective-permute-start | bytes 1572872 | tf_op jit(solution)/shard_map/ppermute | solution.py:740
  7.8 17.5 %collective-permute-start.1 = (bf16[1024,256]{1,0:T(8,128)(2,1)S(1)}, bf16[1024,256]{1,0:T(8,128)(2,1)S(1)}, u32[]{:S(2)}, u32[]{:S(2)}) collective-permute-start(bf16[1024,256]{1,0:T(8,128)(2,1)S(1)} %get-tuple-element.42), channel_id=1, source_target_pairs={{0,31},{1,0},{2,1},{3,2},{4,3},{5,4},{6,5},{7,6},{8,7},{9,8},{10,9... | collective-permute-start | bytes 1572872 | tf_op jit(solution)/shard_map/ppermute | solution.py:741
  13.8 11.5 %copy-start.3 = (f32[256,7]{0,1:T(8,128)S(1)}, f32[256,7]{0,1:T(8,128)}, u32[]{:S(2)}) copy-start(f32[256,7]{0,1:T(8,128)} %param.11) | copy-start | bytes 21508
  25.3 6.1 %copy-start.7 = (s32[2048]{0:T(1024)S(1)}, s32[2048]{0:T(1024)}, u32[]{:S(2)}) copy-start(s32[2048]{0:T(1024)} %param.16) | copy-start | bytes 24580
  25.3 6.1 %copy-start.8 = (s32[2048]{0:T(1024)S(1)}, s32[2048]{0:T(1024)}, u32[]{:S(2)}) copy-start(s32[2048]{0:T(1024)} %param.17) | copy-start | bytes 24580
  65.0 14.6 %copy-start = (bf16[2048,500]{0,1:T(8,128)(2,1)S(1)}, bf16[2048,500]{0,1:T(8,128)(2,1)}, u32[]{:S(2)}) copy-start(bf16[2048,500]{0,1:T(8,128)(2,1)} %param.9) | copy-start | bytes 6144004
  65.0 14.6 %collective-permute-start.2 = (bf16[1280,256]{1,0:T(8,128)(2,1)S(1)}, bf16[1280,256]{1,0:T(8,128)(2,1)S(1)}, u32[]{:S(2)}, u32[]{:S(2)}) collective-permute-start(bf16[1280,256]{1,0:T(8,128)(2,1)S(1)} %get-tuple-element.60.pos_b_ref), channel_id=1, source_target_pairs={{0,1},{1,2},{2,3},{3,4},{4,5},{5,6},{6,7},{7,8},{8,9},{9,10},{10,1... | collective-permute-start | bytes 1966088 | tf_op jit(solution)/shard_map/ppermute | solution.py:785
  65.0 14.5 %collective-permute-start.3 = (bf16[1280,256]{1,0:T(8,128)(2,1)S(1)}, bf16[1280,256]{1,0:T(8,128)(2,1)S(1)}, u32[]{:S(2)}, u32[]{:S(2)}) collective-permute-start(bf16[1280,256]{1,0:T(8,128)(2,1)S(1)} %get-tuple-element.60.pos_b_ref), channel_id=1, source_target_pairs={{0,31},{1,0},{2,1},{3,2},{4,3},{5,4},{6,5},{7,6},{8,7},{9,8},{10,9... | collective-permute-start | bytes 1966088 | tf_op jit(solution)/shard_map/ppermute | solution.py:786

commit v6 on v5

--- a/solution.py
+++ b/solution.py
@@ -374,8 +374,8 @@
     return w2_all, lax.shift_right_logical(lax.broadcasted_iota(jnp.int32, w2_all.shape, 0), 3)
 
 
-def fill_table(dt_ref, pos_refs, w2_all, group, table):
-    dt_cols = jnp.transpose(dt_ref[...].astype(F32)).astype(BF16)
+def fill_table(dt, pos_refs, w2_all, group, table):
+    dt_cols = jnp.transpose(dt).astype(BF16)
     for pos_ref, lead in zip(pos_refs, (0, pos_refs[0].shape[0] // LANES)):
         def widen(j, carry):
             i = lead + j
@@ -394,7 +394,7 @@
     start_slots(lists, slots, slot_sems)
     w2_all, group = stack_classes(w2_ref, rows // LANES)
     clear_rows(bufs)
-    fill_table(dt_ref, (pos_a_ref, pos_b_ref), w2_all, group, table)
+    fill_table(dt_ref[...].astype(F32), (pos_a_ref, pos_b_ref), w2_all, group, table)
     spread_weights(lw_ref, wide, *list_rows(0, end))
     slot_loop(lists, slots, slot_sems, wide, table, bufs, end)
 
@@ -406,12 +406,15 @@
 
 
 def k4b_body(part_ref, num_ref, names_ref, prev_dst, prev_src, prev_w, next_dst, next_src, next_w,
-             prev_dt, prev_a, prev_b, next_dt, next_a, next_b, w2_ref, xt_ref, misc_ref, out_ref,
-             table, wide, d_tab, *rest):
+             prev_a, prev_late, next_a, next_late, w2_ref, xt_ref, misc_ref, out_ref,
+             table, wide, d_tab, names, names_sem, *rest):
     fasts, pools, bufs = (rest[0:2], rest[2:4]), rest[4:6], rest[6:]
     rows = part_ref.shape[0]
-    sides = (((prev_dst, prev_src), prev_w, prev_dt, (prev_a, prev_b), 1, 2),
-             ((next_dst, next_src), next_w, next_dt, (next_a, next_b), 2, 1))
+    late_rows = rows - prev_a.shape[0]
+    load = pltpu.make_async_copy(names_ref, names, names_sem)
+    load.start()
+    sides = (((prev_dst, prev_src), prev_w, prev_late, prev_a, 1, 2),
+             ((next_dst, next_src), next_w, next_late, next_a, 2, 1))
     spans = []
     for (lists, _, _, _, row, kind), fast, pool in zip(sides, fasts, pools):
         first = num_ref[row, 0]
@@ -421,10 +424,14 @@
         start_lists(lists, fast, pool, *spans[-1])
     w2_all, group = stack_classes(w2_ref, rows // LANES)
     clear_rows(bufs)
-    for (lists, w_ref, dt_ref, pos_refs, _, _), fast, pool, span in zip(sides, fasts, pools, spans):
-        fill_table(dt_ref, pos_refs, w2_all, group, table)
+    for (lists, w_ref, late, early, _, _), fast, pool, span in zip(sides, fasts, pools, spans):
+        dt = late[late_rows:, :].astype(F32)
+        dt = jnp.concatenate([dt[:, 0:LANES], dt[:, LANES:]], axis=0)
+        fill_table(dt, (early, late.at[0:late_rows, :]), w2_all, group, table)
         spread_weights(w_ref, wide, *list_rows(*span))
-        row_loop(lists, fast, pool, wide, table, bufs, *span, rename=names_ref)
+        if late is prev_late:
+            load.wait()
+        row_loop(lists, fast, pool, wide, table, bufs, *span, rename=names)
 
     def finish(i, carry):
         at = pl.ds(pl.multiple_of(i * LANES, LANES), LANES)
@@ -441,10 +448,10 @@
     return jnp.broadcast_to(lax.shift_right_logical(idx, 7), (CLASS_ROWS, idx.shape[1]))
 
 
-def pick_cols(table_b, pieces, idx, hot):
+def pick_cols(table_b, pieces, idx, hot, first=0):
     cols = jnp.dot(table_b, hot, preferred_element_type=F32)
     rows = table_b.shape[0] // pieces
-    hi = hi_of(idx)
+    hi = hi_of(idx) - first
     out = jnp.zeros(hi.shape, F32)
     for h in range(rows // CLASS_ROWS):
         part = cols[h * CLASS_ROWS:(h + 1) * CLASS_ROWS]
@@ -454,8 +461,8 @@
     return out
 
 
-def add_cols(val, idx, hot, num_hi):
-    hi = packed(lax.shift_right_logical(idx, 7))
+def add_cols(val, idx, hot, num_hi, first=0):
+    hi = packed(lax.shift_right_logical(idx, 7) - first)
     low_half = lax.broadcasted_iota(jnp.int32, hi.shape, 0) >= CLASS_ROWS
     mixed = hi - low_half.astype(jnp.int32).astype(jnp.int16)
     top, mid, low = three_pieces(val)
@@ -479,11 +486,11 @@
     return jnp.concatenate(three_pieces(val), axis=0).astype(BF16)
 
 
-def k3_body(num_dev, tab_ref, send_ref, src_ref, dst_ref, w_ref, lab_ref, mask_ref, hid_ref, pos_ref,
+def k3_body(num_dev, tab_ref, send_ref, src_ref, dst_ref, w_ref, lab_ref, mask_ref, hid_ref, pos_ref, pos_late_ref,
             lpair_ref, lw_ref, num_ref,
-            dt_ref, misc_ref, dt_prev_ref, dt_next_ref, pos_prev_ref, pos_next_ref, dst_prev_ref, dst_next_ref,
+            dt_ref, misc_ref, late_ref, pos_prev_ref, pos_next_ref, dst_prev_ref, dst_next_ref,
             put_prev_ref, put_next_ref, w_prev_ref, w_next_ref, nums_ref, names_ref, pairs, nums,
-            ext_b, fwd_send, fwd_recv, bwd_send, bwd_recv, acc_z, acc_s, acc_r, dz_b, cnt_send, cnt_recv,
+            ext_b, fwd_send, fwd_recv, bwd_send, bwd_recv, vals, acc_z, acc_s, acc_o, acc_r, dz_b, cnt_send, cnt_recv,
             sems, cnt_sems, list_sems, pos_sems):
     me, nxt, prv = ring_peers(num_dev)
     layers = layer_peers(me, num_dev)
@@ -539,6 +546,17 @@
     send_pos(2)
     acc_z[...] = jnp.zeros_like(acc_z)
     acc_s[...] = jnp.zeros_like(acc_s)
+    acc_o[...] = jnp.zeros_like(acc_o)
+    late_rows = pos_late_ref.shape[0]
+    late_ref[0:late_rows, :] = pos_late_ref[...]
+    steps = src_ref.shape[0] // 8
+
+    def own_forward(i, carry):
+        src = wide_row(src_ref, pl.multiple_of(i * 8, 8))
+        vals[i] = pick_cols(ext_b[0:own_hi * CLASS_ROWS, :], 1, src, lo_hot(src))
+        return carry
+
+    lax.fori_loop(0, steps, own_forward, 0)
     for copy in copies:
         copy.wait()
     for r in range(2):
@@ -547,12 +565,12 @@
             two = jnp.concatenate([got[0:8, (j + k) * LANES:(j + k + 1) * LANES] for k in range(2)], axis=0)
             ext_b[pl.ds((own_hi + r * halo_hi + j) * CLASS_ROWS, 16), :] = two.astype(BF16)
 
-    steps = src_ref.shape[0] // 8
 
     def forward(i, carry):
         first = pl.multiple_of(i * 8, 8)
         src, dst = wide_row(src_ref, first), wide_row(dst_ref, first)
-        val = pick_cols(ext_b[...], 1, src, lo_hot(src)) * wide_row(w_ref, first)
+        val = vals[i] + pick_cols(ext_b[own_hi * CLASS_ROWS:, :], 1, src, lo_hot(src), own_hi)
+        val = val * wide_row(w_ref, first)
         acc_z[...] += add_cols(val, dst, lo_hot(dst), own_hi)
         return carry
 
@@ -582,28 +600,39 @@
         first = pl.multiple_of(i * 8, 8)
         src, dst = wide_row(src_ref, first), wide_row(dst_ref, first)
         val = pick_cols(dz_b[...], 3, dst, lo_hot(dst)) * wide_row(w_ref, first)
-        acc_s[...] += add_cols(val, src, lo_hot(src), all_hi)
+        vals[i] = val
+        acc_s[...] += add_cols(val, src, lo_hot(src), 2 * halo_hi, own_hi)
         return carry
 
     lax.fori_loop(0, steps, backward, 0)
 
-    d_ext = join_pieces(acc_s[...], all_hi)
+    d_halo = join_pieces(acc_s[...], 2 * halo_hi)
     copies = []
     for r in range(2):
         for j in range(halo_hi):
-            bwd_send[r, :, j * LANES:(j + 1) * LANES] = d_ext[own_hi + r * halo_hi + j]
+            bwd_send[r, :, j * LANES:(j + 1) * LANES] = d_halo[r * halo_hi + j]
         copy = remote(bwd_send.at[r], bwd_recv.at[1 - r], sems, 2 + r, prv if r == 0 else nxt)
         copy.start()
         copies.append(copy)
+
+    def own_backward(i, carry):
+        src = wide_row(src_ref, pl.multiple_of(i * 8, 8))
+        acc_o[...] += add_cols(vals[i], src, lo_hot(src), own_hi)
+        return carry
+
+    lax.fori_loop(0, steps, own_backward, 0)
+    d_own = join_pieces(acc_o[...], own_hi)
     for copy in copies:
         copy.wait()
     for r in range(2):
         part = add_cols(bwd_recv[r], send_ref[r:r + 1, :], hot_send[r], own_hi)
         acc_r[...] = part if r == 0 else acc_r[...] + part
     back = join_pieces(acc_r[...], own_hi)
-    d_tab = [d_ext[h] + back[h] for h in range(own_hi)]
+    d_tab = [d_own[h] + back[h] for h in range(own_hi)]
+    half = own_hi // 2
     dt_ref[...] = jnp.concatenate(d_tab, axis=0).astype(BF16)
-    send_late([(dt_ref, [dt_prev_ref, dt_next_ref])], list_sems, 3)
+    late_ref[late_rows:, :] = jnp.concatenate(
+        [jnp.concatenate(d_tab[:half], axis=0), jnp.concatenate(d_tab[half:], axis=0)], axis=1).astype(BF16)
     grad = jnp.zeros((CLASS_ROWS, hid_ref.shape[1]), F32)
     for h in range(own_hi):
         grad = grad + jnp.dot(d_tab[h].astype(BF16), hid_ref[pl.ds(h * LANES, LANES), :], preferred_element_type=F32)
@@ -630,8 +659,9 @@
     num_z = num_dev // PLANE
     meet([other] + chips + layers)
     rows, width = part_ref.shape
+    rows //= 2
     n1, n2, n3 = rows // 2, rows // 8, rows // 8 // num_z
-    parts = [pl.ds(c * LANES, LANES) for c in range(width // LANES)]
+    parts = [(p, pl.ds(c * LANES, LANES)) for p in range(2) for c in range(width // LANES)]
     used = [0]
 
     def send(pairs):
@@ -650,39 +680,42 @@
     def at(first, size):
         return pl.ds(pl.multiple_of(first, size), size)
 
-    flying = [send([(part_ref.at[at((1 - core) * n1, n1), c], land_core.at[:, c], other)]) for c in parts]
-    for i, c in enumerate(parts):
+    def run(p, size):
+        return pl.ds(p * size, size)
+
+    flying = [send([(part_ref.at[at(p * rows + (1 - core) * n1, n1), c], land_core.at[run(p, n1), c], other)]) for p, c in parts]
+    for i, (p, c) in enumerate(parts):
         wait(flying[i])
-        by_core[:, c] = part_ref[at(core * n1, n1), c] + land_core[:, c]
-        flying[i] = send([(by_core.at[at((chip + k + 1) % 4 * n2, n2), c], land_chip.at[k, :, c], dev)
+        by_core[run(p, n1), c] = part_ref[at(p * rows + core * n1, n1), c] + land_core[run(p, n1), c]
+        flying[i] = send([(by_core.at[at(p * n1 + (chip + k + 1) % 4 * n2, n2), c], land_chip.at[k, run(p, n2), c], dev)
                           for k, dev in enumerate(chips)])
-    for i, c in enumerate(parts):
+    for i, (p, c) in enumerate(parts):
         wait(flying[i])
-        total = by_core[at(chip * n2, n2), c]
+        total = by_core[at(p * n1 + chip * n2, n2), c]
         for k in range(len(chips)):
-            total = total + land_chip[k, :, c]
-        by_chip[:, c] = total
-        flying[i] = send([(by_chip.at[at((z + k + 1) % num_z * n3, n3), c], land_z.at[k, :, c], dev)
+            total = total + land_chip[k, run(p, n2), c]
+        by_chip[run(p, n2), c] = total
+        flying[i] = send([(by_chip.at[at(p * n2 + (z + k + 1) % num_z * n3, n3), c], land_z.at[k, run(p, n3), c], dev)
                           for k, dev in enumerate(layers)])
-    first = core * n1 + chip * n2 + z * n3
-    gathers = ((first, n3, layers), (core * n1 + chip * n2, n2, chips), (core * n1, n1, [other]))
-
-    def gather(level, c):
+    firsts = (core * n1 + chip * n2 + z * n3, core * n1 + chip * n2, core * n1)
+    gathers = list(zip(firsts, (n3, n2, n1), (layers, chips, [other])))
+
+    def gather(level, p, c):
         first, size, devs = gathers[level]
-        own = full_ref.at[at(first, size), c]
+        own = full_ref.at[at(p * rows + first, size), c]
         return send([(own, own, dev) for dev in devs])
 
-    for i, c in enumerate(parts):
+    for i, (p, c) in enumerate(parts):
         wait(flying[i])
-        total = by_chip[at(z * n3, n3), c]
+        total = by_chip[at(p * n2 + z * n3, n3), c]
         for k in range(len(layers)):
-            total = total + land_z[k, :, c]
-        full_ref[at(first, n3), c] = total
-        flying[i] = gather(0, c)
+            total = total + land_z[k, run(p, n3), c]
+        full_ref[at(p * rows + firsts[0], n3), c] = total
+        flying[i] = gather(0, p, c)
     for level in (1, 2):
-        for i, c in enumerate(parts):
+        for i, (p, c) in enumerate(parts):
             wait(flying[i])
-            flying[i] = gather(level, c)
+            flying[i] = gather(level, p, c)
     for copies in flying:
         wait(copies)
 
@@ -766,24 +799,24 @@
         tab_b = arr(BF16, own_hi * CLASS_ROWS, LANES)
         pos_early = arr(BF16, EARLY_ROWS, width)
         list_i = arr(I32, *listed)
-        (d_tab, misc, d_prev, d_next, prev_a, next_a, dst_prev, dst_next, put_prev, put_next, w_prev, w_next,
+        (d_tab, misc, late, prev_a, next_a, dst_prev, dst_next, put_prev, put_next, w_prev, w_next,
          nums, names) = pl.pallas_call(
             functools.partial(k3_body, num_dev),
-            out_shape=(tab_b, arr(F32, 16, width), tab_b, tab_b, pos_early, pos_early, list_i, list_i, list_i, list_i,
+            out_shape=(tab_b, arr(F32, 16, width), arr(BF16, late_rows + own_hi * CLASS_ROWS * LANES // width, width), pos_early, pos_early, list_i, list_i, list_i, list_i,
                        arr(F32, *listed), arr(F32, *listed), arr(I32, 8, LANES), arr(I32, 2 * halo // LANES, LANES)),
-            in_specs=[vmem()] * 12, out_specs=(vmem(),) * 14,
+            in_specs=[vmem()] * 13, out_specs=(vmem(),) * 13,
             scratch_shapes=[scr(I32, 2, *listed), scr(I32, 2, 8, LANES), scr(BF16, all_hi * CLASS_ROWS, LANES),
                             scr(BF16, 2, 16, halo), scr(BF16, 2, 16, halo), scr(F32, 2, CLASS_ROWS, halo),
-                            scr(F32, 2, CLASS_ROWS, halo), scr(F32, own_hi * 24, LANES), scr(F32, all_hi * 24, LANES),
-                            scr(F32, own_hi * 24, LANES), scr(BF16, 3 * own_hi * CLASS_ROWS, LANES),
+                            scr(F32, 2, CLASS_ROWS, halo), scr(F32, edges // 1024, CLASS_ROWS, 1024),
+                            scr(F32, own_hi * 24, LANES), scr(F32, 2 * halo // LANES * 24, LANES),
+                            scr(F32, own_hi * 24, LANES), scr(F32, own_hi * 24, LANES), scr(BF16, 3 * own_hi * CLASS_ROWS, LANES),
                             scr(F32, 2, 8, LANES), scr(F32, PLANE + num_z - 2, 8, LANES),
-                            dma(4), dma(PLANE + num_z - 2), dma(8), dma(6)],
+                            dma(4), dma(PLANE + num_z - 2), dma(6), dma(6)],
             compiler_params=params(1), name="layer_two",
-        )(tab, send_rows, src2, dst2, ew2, lab2, mask2, hid, pos_a, lpair, lw, num)
-
-        pos_b_late, d_tab = lax.optimization_barrier((pos_b, d_tab))
-        prev_b = lax.ppermute(pos_b_late, GRAPH_AXIS, [(g, (g + 1) % num_dev) for g in range(num_dev)])
-        next_b = lax.ppermute(pos_b_late, GRAPH_AXIS, [(g, (g - 1) % num_dev) for g in range(num_dev)])
+        )(tab, send_rows, src2, dst2, ew2, lab2, mask2, hid, pos_a, pos_b, lpair, lw, num)
+
+        prev_late = lax.ppermute(late, GRAPH_AXIS, [(g, (g + 1) % num_dev) for g in range(num_dev)])
+        next_late = lax.ppermute(late, GRAPH_AXIS, [(g, (g - 1) % num_dev) for g in range(num_dev)])
         part_own = pl.pallas_call(
             k4a_body,
             out_shape=arr(F32, rows, width),
@@ -797,13 +830,14 @@
         part = pl.pallas_call(
             k4b_body,
             out_shape=arr(F32, sum_rows_pad, width),
-            in_specs=[vmem(), smem(), smem()] + [hbm(), hbm(), vmem()] * 2 + [vmem()] * 9, out_specs=vmem(),
-            scratch_shapes=[scr(F32, 2 * rows, LANES), scr(F32, entries, LANES), scr(BF16, rows, width)]
+            in_specs=[vmem(), smem(), vmem()] + [hbm(), hbm(), vmem()] * 2 + [vmem()] * 7, out_specs=vmem(),
+            scratch_shapes=[scr(F32, 2 * rows, LANES), scr(F32, entries, LANES), scr(BF16, rows, width),
+                            pltpu.SMEM((2 * halo,), I32), pltpu.SemaphoreType.DMA]
             + [fast_list] * 4 + [list_dma] * 2 + bufs,
             compiler_params=params(), name="scatter_peers",
         )(part_own, nums, names.reshape(2 * halo), dst_prev, put_prev, w_prev,
           dst_next, put_next, w_next,
-          d_prev, prev_a, prev_b, d_next, next_a, next_b, w2, feats_t, misc)
+          prev_a, prev_late, next_a, next_late, w2, feats_t, misc)
 
         n1, n2 = sum_rows_pad // 2, sum_rows_pad // 8
         n3 = n2 // num_z
@@ -812,7 +846,7 @@
             out_shape=arr(F32, sum_rows_pad, width),
             in_specs=[vmem()], out_specs=vmem(),
             scratch_shapes=[scr(F32, n1, width), scr(F32, 3, n2, width), scr(F32, num_z - 1, n3, width),
-                            scr(F32, n1, width), scr(F32, n2, width), dma(4 * (1 + 3 + num_z - 1))],
+                            scr(F32, n1, width), scr(F32, n2, width), dma(8 * (1 + 3 + num_z - 1))],
             compiler_params=params(2), name="sum_gradients",
         )(part)
         loss, grad_one, grad_two = pl.pallas_call(

time: 116 us -> 111 us (0.957)
  Pallas kernels: 101 us -> 95.5 us
    pallas_call x1, Pallas kernels: 33.6 us -> 26.1 us  [device_step(): pl.pallas_call(functools.partial(k3_body, num_dev), out_shape=(tab_b, arr...]
  transfers between devices with their start and end apart: 4 -> 4, of which waited for: 0 -> 0; matrix products, arithmetic and copies ran while one was open for 0% -> 0% of each run, Pallas kernels for 18% -> 20%
where the time goes in v6:
time: 111 us; the launch traced here: 110 us
  Pallas kernels  95.5 us (86%)
  starting transfers between devices  11.9 us (11%)
  local copies, waits for them, and re-layouts  1.76 us (2%)
    pallas_call x1, Pallas kernels, device_step(): pl.pallas_call(functools.partial(k3_body, num_dev), out_shape=(tab_b, arr...  26.1 us
    pallas_call x1, Pallas kernels, device_step(): pl.pallas_call(functools.partial(k5_body, num_dev), out_shape=arr(F32, su...  25.4 us
    pallas_call x1, Pallas kernels, device_step(): pl.pallas_call(k2a_body, out_shape=(arr(F32, rows, width),) + lists_in, i...  12.1 us
    pallas_call x1, Pallas kernels, device_step(): pl.pallas_call(k4b_body, out_shape=arr(F32, sum_rows_pad, width), in_spec...  10.7 us
    pallas_call x1, Pallas kernels, device_step(): pl.pallas_call(k4a_body, out_shape=arr(F32, rows, width), in_specs=[hbm()...  9.79 us
    ppermute x1, starting transfers between devices, device_step(): lax.ppermute(to_prev, GRAPH_AXIS, [(g, (g - 1) % num_dev) for g in range(...  5.98 us
    pallas_call x1, Pallas kernels, device_step(): pl.pallas_call(k2b_body, out_shape=(arr(BF16, rows, width), arr(BF16, EAR...  5.73 us
    ppermute x1, starting transfers between devices, device_step(): lax.ppermute(late, GRAPH_AXIS, [(g, (g - 1) % num_dev) for g in range(num...  4.95 us
  transfers between devices with their start and end apart: 4, of which 0 were waited for; matrix products, arithmetic and copies ran while one was open for 0% of the time, Pallas kernels for 20%

profile of v6, /device:TPU:0, one launch (start us, length us, event | category | flops | bytes accessed | tf_op | source)
XLA Modules:
  0.0 110.0 jit_solution(6778703041910071635)
XLA Ops:
  0.6 0.0 copy-start.1
  0.6 1.0 copy-done.1
  1.7 0.0 copy-start.5
  1.7 0.7 copy-done.5
  2.4 0.0 copy-start.2
  2.4 0.0 copy-start.3
  2.4 0.0 copy-start.4
  2.4 4.8 %transform.1 = (bf16[256,2048]{1,0:T(8,128)(2,1)S(1)}, bf16[1024,256]{1,0:T(8,128)(2,1)S(1)}, bf16[1024,256]{1,0:T(8,128)(2,1)S(1)}) custom-call(bf16[500,2048]{1,0:T(8,128)(2,1)} %bitcast.10, f32[500,256]{1,0:T(8,128)S(1)} %copy-done.1, s32[2,1024]{1,0:T(2,128)S(1)} %copy-done.5), custom_call_target="tpu_custom_call" | custom-call | tf_op jit(solution)/shard_map/transform/pallas_call | solution.py:765
  7.2 0.6 collective-permute-start
  7.8 6.0 %collective-permute-start.1 = (bf16[1024,256]{1,0:T(8,128)(2,1)S(1)}, bf16[1024,256]{1,0:T(8,128)(2,1)S(1)}, u32[]{:S(2)}, u32[]{:S(2)}) collective-permute-start(bf16[1024,256]{1,0:T(8,128)(2,1)S(1)} %get-tuple-element.39), channel_id=1, source_target_pairs={{0,31},{1,0},{2,1},{3,2},{4,3},{5,4},{6,5},{7,6},{8,7},{9,8},{10,9... | collective-permute-start | bytes 1572872 | tf_op jit(solution)/shard_map/ppermute | solution.py:774
  13.8 0.0 copy-done.2
  13.8 0.0 copy-done.3
  13.8 0.0 copy-done.4
  13.8 0.0 copy-start.6
  13.8 12.1 %aggregate_own.1 = (f32[2048,256]{1,0:T(8,128)S(1)}, s32[80,128]{1,0:T(8,128)S(1)}, s32[80,128]{1,0:T(8,128)S(1)}, s32[80,128]{1,0:T(8,128)S(1)}, f32[80,128]{1,0:T(8,128)S(1)}, /*index=5*/s32[8,128]{1,0:T(8,128)S(1)}) custom-call(bf16[256,2048]{1,0:T(8,128)(2,1)S(1)} %get-tuple-element.32.own_t_ref, s32[64,128]{1,0:T(8,128)S(1)} %bitcast.12, ...), custom_call_target="tpu_custom_call" | custom-call | flops 8000000000 | bytes 10000000 | tf_op jit(solution)/shard_map/aggregate_own/pallas_call | solution.py:779
  25.9 0.0 copy-start.7
  25.9 0.0 copy-start.8
  25.9 0.0 collective-permute-done.prev_ref
  25.9 0.0 collective-permute-done.1.next_ref
  25.9 0.0 copy-done.6
  25.9 5.7 %aggregate_halo.1 = (bf16[2048,256]{1,0:T(8,128)(2,1)S(1)}, bf16[768,256]{1,0:T(8,128)(2,1)S(1)}, bf16[1280,256]{1,0:T(8,128)(2,1)S(1)}, f32[128,128]{1,0:T(8,128)S(1)}) custom-call(f32[2048,256]{1,0:T(8,128)S(1)} %get-tuple-element.37.part_ref, bf16[1024,256]{1,0:T(8,128)(2,1)S(1)} %collective-permute-done.prev_ref, ...), custom_call_target="tpu_custom_call" | custom-call | tf_op jit(solution)/shard_map/aggregate_halo/pallas_call | solution.py:789
  31.7 0.0 copy-done.7
  31.7 0.0 copy-done.8
  31.7 26.1 %layer_two.1 = (bf16[128,128]{1,0:T(8,128)(2,1)S(1)}, f32[16,256]{1,0:T(8,128)S(1)}, bf16[1344,256]{1,0:T(8,128)(2,1)S(1)}, bf16[768,256]{1,0:T(8,128)(2,1)S(1)}...) custom-call(f32[128,128]{1,0:T(8,128)S(1)} %get-tuple-element.42.tab, ...), custom_call_target="tpu_custom_call" | custom-call | tf_op jit(solution)/shard_map/layer_two/pallas_call | solution.py:803
  57.8 0.4 collective-permute-start.2
  58.3 5.0 %collective-permute-start.3 = (bf16[1344,256]{1,0:T(8,128)(2,1)S(1)}, bf16[1344,256]{1,0:T(8,128)(2,1)S(1)}, u32[]{:S(2)}, u32[]{:S(2)}) collective-permute-start(bf16[1344,256]{1,0:T(8,128)(2,1)S(1)} %get-tuple-element.55), channel_id=1, source_target_pairs={{0,31},{1,0},{2,1},{3,2},{4,3},{5,4},{6,5},{7,6},{8,7},{9,8},{10,9... | collective-permute-start | bytes 2064392 | tf_op jit(solution)/shard_map/ppermute | solution.py:819
  63.2 0.0 copy-start
  63.2 9.8 %scatter_own.1.part_ref = f32[2048,256]{1,0:T(8,128)S(1)} custom-call(s32[80,128]{1,0:T(8,128)S(1)} %get-tuple-element.33.ldst_ref, s32[80,128]{1,0:T(8,128)S(1)} %get-tuple-element.34.lsrc_ref, s32[8,128]{1,0:T(8,128)S(1)} %get-tuple-element.35.num_ref, f32[80,128]{1,0:T(8,128)S(1)} %get-tuple-element.36.lw_ref, ...), custom_call_target="tpu_custom_call" | custom-call | flops 8000000000 | bytes 10000000 | tf_op jit(solution)/shard_map/scatter_own/pallas_call | solution.py:820
  73.0 0.0 collective-permute-done.2.prev_late
  73.0 0.0 collective-permute-done.3.next_late
  73.0 0.0 copy-done
  73.1 10.7 %scatter_peers.1.part_ref = f32[512,256]{1,0:T(8,128)S(1)} custom-call(f32[2048,256]{1,0:T(8,128)S(1)} %scatter_own.1.part_ref, s32[8,128]{1,0:T(8,128)S(1)} %get-tuple-element.46.num_ref, s32[2048]{0:T(1024)S(1)} %bitcast.23, s32[80,128]{1,0:T(8,128)S(1)} %get-tuple-element.48.prev_dst, s32[80,128]{1,0:T(8,128)S(1)} %get-tuple-element.49.prev_src, ...), custom_call_target="tpu_custom_call" | custom-call | tf_op jit(solution)/shard_map/scatter_peers/pallas_call | solution.py:830
  83.8 25.4 %sum_gradients.1.full_ref = f32[512,256]{1,0:T(8,128)S(1)} custom-call(f32[512,256]{1,0:T(8,128)S(1)} %scatter_peers.1.part_ref), custom_call_target="tpu_custom_call" | custom-call | tf_op jit(solution)/shard_map/sum_gradients/pallas_call | solution.py:844
  109.2 0.8 outputs.1
Async XLA Ops:
  0.6 1.0 copy-start.1
  1.7 0.7 copy-start.5
  2.4 11.4 %copy-start.2 = (s32[8192]{0:T(1024)S(1)}, s32[8192]{0:T(1024)}, u32[]{:S(2)}) copy-start(s32[8192]{0:T(1024)} %param.13) | copy-start | bytes 98308
  2.4 11.4 %copy-start.3 = (s32[8192]{0:T(1024)S(1)}, s32[8192]{0:T(1024)}, u32[]{:S(2)}) copy-start(s32[8192]{0:T(1024)} %param.14) | copy-start | bytes 98308
  2.4 11.4 %copy-start.4 = (f32[8192]{0:T(1024)S(1)}, f32[8192]{0:T(1024)}, u32[]{:S(2)}) copy-start(f32[8192]{0:T(1024)} %param.15) | copy-start | bytes 98308
  7.2 18.7 %collective-permute-start = (bf16[1024,256]{1,0:T(8,128)(2,1)S(1)}, bf16[1024,256]{1,0:T(8,128)(2,1)S(1)}, u32[]{:S(2)}, u32[]{:S(2)}) collective-permute-start(bf16[1024,256]{1,0:T(8,128)(2,1)S(1)} %get-tuple-element.38), channel_id=1, source_target_pairs={{0,1},{1,2},{2,3},{3,4},{4,5},{5,6},{6,7},{7,8},{8,9},{9,10},{10,1... | collective-permute-start | bytes 1572872 | tf_op jit(solution)/shard_map/ppermute | solution.py:773
  7.8 18.1 %collective-permute-start.1 = (bf16[1024,256]{1,0:T(8,128)(2,1)S(1)}, bf16[1024,256]{1,0:T(8,128)(2,1)S(1)}, u32[]{:S(2)}, u32[]{:S(2)}) collective-permute-start(bf16[1024,256]{1,0:T(8,128)(2,1)S(1)} %get-tuple-element.39), channel_id=1, source_target_pairs={{0,31},{1,0},{2,1},{3,2},{4,3},{5,4},{6,5},{7,6},{8,7},{9,8},{10,9... | collective-permute-start | bytes 1572872 | tf_op jit(solution)/shard_map/ppermute | solution.py:774
  13.8 12.1 %copy-start.6 = (f32[256,7]{0,1:T(8,128)S(1)}, f32[256,7]{0,1:T(8,128)}, u32[]{:S(2)}) copy-start(f32[256,7]{0,1:T(8,128)} %param.11) | copy-start | bytes 21508
  25.9 5.8 %copy-start.7 = (s32[2048]{0:T(1024)S(1)}, s32[2048]{0:T(1024)}, u32[]{:S(2)}) copy-start(s32[2048]{0:T(1024)} %param.16) | copy-start | bytes 24580
  25.9 5.8 %copy-start.8 = (s32[2048]{0:T(1024)S(1)}, s32[2048]{0:T(1024)}, u32[]{:S(2)}) copy-start(s32[2048]{0:T(1024)} %param.17) | copy-start | bytes 24580
  57.8 15.2 %collective-permute-start.2 = (bf16[1344,256]{1,0:T(8,128)(2,1)S(1)}, bf16[1344,256]{1,0:T(8,128)(2,1)S(1)}, u32[]{:S(2)}, u32[]{:S(2)}) collective-permute-start(bf16[1344,256]{1,0:T(8,128)(2,1)S(1)} %get-tuple-element.55), channel_id=1, source_target_pairs={{0,1},{1,2},{2,3},{3,4},{4,5},{5,6},{6,7},{7,8},{8,9},{9,10},{10,1... | collective-permute-start | bytes 2064392 | tf_op jit(solution)/shard_map/ppermute | solution.py:818
  58.3 14.8 %collective-permute-start.3 = (bf16[1344,256]{1,0:T(8,128)(2,1)S(1)}, bf16[1344,256]{1,0:T(8,128)(2,1)S(1)}, u32[]{:S(2)}, u32[]{:S(2)}) collective-permute-start(bf16[1344,256]{1,0:T(8,128)(2,1)S(1)} %get-tuple-element.55), channel_id=1, source_target_pairs={{0,31},{1,0},{2,1},{3,2},{4,3},{5,4},{6,5},{7,6},{8,7},{9,8},{10,9... | collective-permute-start | bytes 2064392 | tf_op jit(solution)/shard_map/ppermute | solution.py:819
  63.2 9.8 %copy-start = (bf16[2048,500]{0,1:T(8,128)(2,1)S(1)}, bf16[2048,500]{0,1:T(8,128)(2,1)}, u32[]{:S(2)}) copy-start(bf16[2048,500]{0,1:T(8,128)(2,1)} %param.9) | copy-start | bytes 6144004

commit v7 on v6

--- a/solution.py
+++ b/solution.py
@@ -36,8 +36,9 @@
 LIST_ROWS = 80
 BLOCK = 128
 NUM_BUFS = 4
-OWN_BUFS = 6
+OWN_BUFS = 5
 EARLY_ROWS = 768
+STEP_ROWS = 32
 CHUNK = 1024
 
 
@@ -76,8 +77,14 @@
 
 
 def wide_row(ref, first):
-    blk = ref[pl.ds(first, 8), :]
-    return jnp.concatenate([blk[j:j + 1, :] for j in range(8)], axis=1)
+    blk = ref[pl.ds(first, STEP_ROWS), :]
+    return jnp.concatenate([blk[j:j + 1, :] for j in range(STEP_ROWS)], axis=1)
+
+
+def number(ref, row, lane):
+    here = lax.broadcasted_iota(jnp.int32, ref.shape, 0) == row
+    here = here & (lax.broadcasted_iota(jnp.int32, ref.shape, 1) == lane)
+    return jnp.sum(jnp.where(here, ref[...].astype(F32), 0.0)).astype(jnp.int32)
 
 
 def packed(row):
@@ -154,7 +161,7 @@
     acc[...] = jnp.zeros_like(acc)
 
     def sort(i, carry):
-        first = pl.multiple_of(i * 8, 8)
+        first = pl.multiple_of(i * STEP_ROWS, STEP_ROWS)
         src, dst, wgt, place = (wide_row(ref, first) for ref in (src_ref, dst_ref, ew_ref, pos))
         both = src + dst * 4096
         ints = [both & 255, lax.shift_right_logical(both, 8) & 255, lax.shift_right_logical(both, 16)]
@@ -165,7 +172,7 @@
         acc[...] += lax.dot_general(lhs, lo_hot(place), NT, preferred_element_type=F32)
         return carry
 
-    lax.fori_loop(0, src_ref.shape[0] // 8, sort, 0)
+    lax.fori_loop(0, src_ref.shape[0] // STEP_ROWS, sort, 0)
     got = [acc[p * LIST_ROWS:(p + 1) * LIST_ROWS, :] for p in range(6)]
     ints = [g.astype(jnp.int32) for g in got[:3]]
     both = ints[0] + ints[1] * 256 + ints[2] * 65536
@@ -307,7 +314,7 @@
 
 
 def k2a_body(own_t_ref, src_ref, dst_ref, ew_ref, part_ref, lsrc_ref, ldst_ref, lpair_ref, lw_ref, num_ref,
-             pos, acc, table, wide, num_fast, src_a, dst_a, src_b, dst_b, sems, slot_sems, *bufs):
+             pos, acc, table, wide, src_a, dst_a, src_b, dst_b, slot_sems, *bufs):
     rows = part_ref.shape[0]
     sort_edges(src_ref, dst_ref, ew_ref, rows, rows // 2, pos, acc, lsrc_ref, ldst_ref, lpair_ref, lw_ref, num_ref)
 
@@ -317,13 +324,10 @@
         return carry
 
     lax.fori_loop(0, rows // LANES, widen, 0)
-    copy = pltpu.make_async_copy(num_ref, num_fast, sems.at[0])
-    copy.start()
     lists, slots = (lsrc_ref, ldst_ref), ((src_a, dst_a), (src_b, dst_b))
     start_slots(lists, slots, slot_sems)
     clear_rows(bufs)
-    copy.wait()
-    end = num_fast[0, 0]
+    end = number(num_ref, 0, 0)
     spread_weights(lw_ref, wide, *list_rows(0, end))
     slot_loop(lists, slots, slot_sems, wide, table, bufs, end)
 
@@ -336,8 +340,8 @@
 
 def k2b_body(part_ref, prev_ref, next_ref, lsrc_ref, ldst_ref, num_ref, lw_ref, w2_ref,
              hid_ref, pos_a_ref, pos_b_ref, tab_ref, table, wide, src_fast, dst_fast, sems, *bufs):
-    first = num_ref[0, 0]
-    end = first + num_ref[0, 1] + num_ref[0, 2]
+    first = number(num_ref, 0, 0)
+    end = first + number(num_ref, 0, 1) + number(num_ref, 0, 2)
     lists, fast = (lsrc_ref, ldst_ref), (src_fast, dst_fast)
     start_lists(lists, fast, sems, first, end)
     spread_weights(lw_ref, wide, *list_rows(first, end))
@@ -390,7 +394,7 @@
 def k4a_body(ldst_ref, lsrc_ref, num_ref, lw_ref, pos_a_ref, pos_b_ref, dt_ref, w2_ref, part_ref,
              table, wide, take_a, put_a, take_b, put_b, slot_sems, *bufs):
     rows = part_ref.shape[0]
-    lists, slots, end = (ldst_ref, lsrc_ref), ((take_a, put_a), (take_b, put_b)), num_ref[0, 0]
+    lists, slots, end = (ldst_ref, lsrc_ref), ((take_a, put_a), (take_b, put_b)), number(num_ref, 0, 0)
     start_slots(lists, slots, slot_sems)
     w2_all, group = stack_classes(w2_ref, rows // LANES)
     clear_rows(bufs)
@@ -417,10 +421,10 @@
              ((next_dst, next_src), next_w, next_late, next_a, 2, 1))
     spans = []
     for (lists, _, _, _, row, kind), fast, pool in zip(sides, fasts, pools):
-        first = num_ref[row, 0]
+        first = number(num_ref, row, 0)
         if kind == 2:
-            first = first + num_ref[row, 1]
-        spans.append((first, first + num_ref[row, kind]))
+            first = first + number(num_ref, row, 1)
+        spans.append((first, first + number(num_ref, row, kind)))
         start_lists(lists, fast, pool, *spans[-1])
     w2_all, group = stack_classes(w2_ref, rows // LANES)
     clear_rows(bufs)
@@ -549,10 +553,10 @@
     acc_o[...] = jnp.zeros_like(acc_o)
     late_rows = pos_late_ref.shape[0]
     late_ref[0:late_rows, :] = pos_late_ref[...]
-    steps = src_ref.shape[0] // 8
+    steps = src_ref.shape[0] // STEP_ROWS
 
     def own_forward(i, carry):
-        src = wide_row(src_ref, pl.multiple_of(i * 8, 8))
+        src = wide_row(src_ref, pl.multiple_of(i * STEP_ROWS, STEP_ROWS))
         vals[i] = pick_cols(ext_b[0:own_hi * CLASS_ROWS, :], 1, src, lo_hot(src))
         return carry
 
@@ -567,7 +571,7 @@
 
 
     def forward(i, carry):
-        first = pl.multiple_of(i * 8, 8)
+        first = pl.multiple_of(i * STEP_ROWS, STEP_ROWS)
         src, dst = wide_row(src_ref, first), wide_row(dst_ref, first)
         val = vals[i] + pick_cols(ext_b[own_hi * CLASS_ROWS:, :], 1, src, lo_hot(src), own_hi)
         val = val * wide_row(w_ref, first)
@@ -597,7 +601,7 @@
     dz_b[...] = stack_pieces(jnp.concatenate(d_log, axis=0))
 
     def backward(i, carry):
-        first = pl.multiple_of(i * 8, 8)
+        first = pl.multiple_of(i * STEP_ROWS, STEP_ROWS)
         src, dst = wide_row(src_ref, first), wide_row(dst_ref, first)
         val = pick_cols(dz_b[...], 3, dst, lo_hot(dst)) * wide_row(w_ref, first)
         vals[i] = val
@@ -616,7 +620,7 @@
         copies.append(copy)
 
     def own_backward(i, carry):
-        src = wide_row(src_ref, pl.multiple_of(i * 8, 8))
+        src = wide_row(src_ref, pl.multiple_of(i * STEP_ROWS, STEP_ROWS))
         acc_o[...] += add_cols(vals[i], src, lo_hot(src), own_hi)
         return carry
 
@@ -781,8 +785,8 @@
             out_shape=(arr(F32, rows, width),) + lists_in,
             in_specs=[vmem()] * 4, out_specs=(vmem(),) * 6,
             scratch_shapes=[scr(I32, edges // LANES, LANES), scr(F32, 6 * LIST_ROWS, LANES), scr(F32, 2 * rows, LANES),
-                            scr(F32, entries, LANES), fast_row, fast_row, fast_row, fast_row, fast_row,
-                            pltpu.SemaphoreType.DMA((1,)), dma(2)] + own_bufs,
+                            scr(F32, entries, LANES), fast_row, fast_row, fast_row, fast_row,
+                            dma(2)] + own_bufs,
             compiler_params=pltpu.CompilerParams(vmem_limit_bytes=OWN_VMEM), cost_estimate=busy, name="aggregate_own",
         )(own_t, src2, dst2, ew2)
 
@@ -790,7 +794,7 @@
             k2b_body,
             out_shape=(arr(BF16, rows, width), arr(BF16, EARLY_ROWS, width), arr(BF16, late_rows, width),
                        arr(F32, own_hi * CLASS_ROWS, LANES)),
-            in_specs=[vmem(), vmem(), vmem(), hbm(), hbm(), smem(), vmem(), vmem()], out_specs=(vmem(),) * 4,
+            in_specs=[vmem(), vmem(), vmem(), hbm(), hbm(), vmem(), vmem(), vmem()], out_specs=(vmem(),) * 4,
             scratch_shapes=[scr(F32, 4 * halo, LANES), scr(F32, entries, LANES), fast_list, fast_list, list_dma] + bufs,
             compiler_params=params(), name="aggregate_halo",
         )(part_own, from_prev, from_next, lsrc, ldst, num, lw, w2)
@@ -807,7 +811,7 @@
             in_specs=[vmem()] * 13, out_specs=(vmem(),) * 13,
             scratch_shapes=[scr(I32, 2, *listed), scr(I32, 2, 8, LANES), scr(BF16, all_hi * CLASS_ROWS, LANES),
                             scr(BF16, 2, 16, halo), scr(BF16, 2, 16, halo), scr(F32, 2, CLASS_ROWS, halo),
-                            scr(F32, 2, CLASS_ROWS, halo), scr(F32, edges // 1024, CLASS_ROWS, 1024),
+                            scr(F32, 2, CLASS_ROWS, halo), scr(F32, edges // (STEP_ROWS * LANES), CLASS_ROWS, STEP_ROWS * LANES),
                             scr(F32, own_hi * 24, LANES), scr(F32, 2 * halo // LANES * 24, LANES),
                             scr(F32, own_hi * 24, LANES), scr(F32, own_hi * 24, LANES), scr(BF16, 3 * own_hi * CLASS_ROWS, LANES),
                             scr(F32, 2, 8, LANES), scr(F32, PLANE + num_z - 2, 8, LANES),
@@ -820,7 +824,7 @@
         part_own = pl.pallas_call(
             k4a_body,
             out_shape=arr(F32, rows, width),
-            in_specs=[hbm(), hbm(), smem()] + [vmem()] * 5, out_specs=vmem(),
+            in_specs=[hbm(), hbm()] + [vmem()] * 6, out_specs=vmem(),
             scratch_shapes=[scr(F32, 2 * rows, LANES), scr(F32, entries, LANES), fast_row, fast_row, fast_row, fast_row,
                             dma(2)] + own_bufs,
             compiler_params=pltpu.CompilerParams(vmem_limit_bytes=OWN_VMEM), cost_estimate=busy, name="scatter_own",
@@ -830,7 +834,7 @@
         part = pl.pallas_call(
             k4b_body,
             out_shape=arr(F32, sum_rows_pad, width),
-            in_specs=[vmem(), smem(), vmem()] + [hbm(), hbm(), vmem()] * 2 + [vmem()] * 7, out_specs=vmem(),
+            in_specs=[vmem(), vmem(), vmem()] + [hbm(), hbm(), vmem()] * 2 + [vmem()] * 7, out_specs=vmem(),
             scratch_shapes=[scr(F32, 2 * rows, LANES), scr(F32, entries, LANES), scr(BF16, rows, width),
                             pltpu.SMEM((2 * halo,), I32), pltpu.SemaphoreType.DMA]
             + [fast_list] * 4 + [list_dma] * 2 + bufs,

time: 111 us -> 106 us (0.955)
  Pallas kernels: 95.5 us -> 90.1 us
    pallas_call x1, Pallas kernels: 26.1 us -> 23.3 us  [device_step(): pl.pallas_call(functools.partial(k3_body, num_dev), out_shape=(tab_b, arr...]
    pallas_call x1, Pallas kernels: 25.4 us -> 23.1 us  [device_step(): pl.pallas_call(functools.partial(k5_body, num_dev), out_shape=arr(F32, su...]
  transfers between devices with their start and end apart: 4 -> 4, of which waited for: 0 -> 0; matrix products, arithmetic and copies ran while one was open for 0% -> 0% of each run, Pallas kernels for 20% -> 21%
where the time goes in v7:
time: 106 us; the launch traced here: 105 us
  Pallas kernels  90.1 us (85%)
  starting transfers between devices  11.9 us (11%)
  local copies, waits for them, and re-layouts  1.76 us (2%)
    pallas_call x1, Pallas kernels, device_step(): pl.pallas_call(functools.partial(k3_body, num_dev), out_shape=(tab_b, arr...  23.3 us
    pallas_call x1, Pallas kernels, device_step(): pl.pallas_call(functools.partial(k5_body, num_dev), out_shape=arr(F32, su...  23.1 us
    pallas_call x1, Pallas kernels, device_step(): pl.pallas_call(k2a_body, out_shape=(arr(F32, rows, width),) + lists_in, i...  11.9 us
    pallas_call x1, Pallas kernels, device_step(): pl.pallas_call(k4b_body, out_shape=arr(F32, sum_rows_pad, width), in_spec...  10.4 us
    pallas_call x1, Pallas kernels, device_step(): pl.pallas_call(k4a_body, out_shape=arr(F32, rows, width), in_specs=[hbm()...  10.1 us
    ppermute x1, starting transfers between devices, device_step(): lax.ppermute(to_prev, GRAPH_AXIS, [(g, (g - 1) % num_dev) for g in range(...  5.98 us
    pallas_call x1, Pallas kernels, device_step(): pl.pallas_call(k2b_body, out_shape=(arr(BF16, rows, width), arr(BF16, EAR...  5.76 us
    ppermute x1, starting transfers between devices, device_step(): lax.ppermute(late, GRAPH_AXIS, [(g, (g - 1) % num_dev) for g in range(num...  5.33 us
  transfers between devices with their start and end apart: 4, of which 0 were waited for; matrix products, arithmetic and copies ran while one was open for 0% of the time, Pallas kernels for 21%

profile of v7, /device:TPU:0, one launch (start us, length us, event | category | flops | bytes accessed | tf_op | source)
XLA Modules:
  0.0 104.6 jit_solution(7614401784700097108)
XLA Ops:
  0.6 0.0 copy-start.1
  0.6 1.0 copy-done.1
  1.7 0.0 copy-start.5
  1.7 0.7 copy-done.5
  2.4 0.0 copy-start.2
  2.4 0.0 copy-start.3
  2.4 0.0 copy-start.4
  2.4 4.8 %transform.1 = (bf16[256,2048]{1,0:T(8,128)(2,1)S(1)}, bf16[1024,256]{1,0:T(8,128)(2,1)S(1)}, bf16[1024,256]{1,0:T(8,128)(2,1)S(1)}) custom-call(bf16[500,2048]{1,0:T(8,128)(2,1)} %bitcast.10, f32[500,256]{1,0:T(8,128)S(1)} %copy-done.1, s32[2,1024]{1,0:T(2,128)S(1)} %copy-done.5), custom_call_target="tpu_custom_call" | custom-call | tf_op jit(solution)/shard_map/transform/pallas_call | solution.py:769
  7.2 0.6 collective-permute-start
  7.8 6.0 %collective-permute-start.1 = (bf16[1024,256]{1,0:T(8,128)(2,1)S(1)}, bf16[1024,256]{1,0:T(8,128)(2,1)S(1)}, u32[]{:S(2)}, u32[]{:S(2)}) collective-permute-start(bf16[1024,256]{1,0:T(8,128)(2,1)S(1)} %get-tuple-element.39), channel_id=1, source_target_pairs={{0,31},{1,0},{2,1},{3,2},{4,3},{5,4},{6,5},{7,6},{8,7},{9,8},{10,9... | collective-permute-start | bytes 1572872 | tf_op jit(solution)/shard_map/ppermute | solution.py:778
  13.8 0.0 copy-done.2
  13.8 0.0 copy-done.3
  13.8 0.0 copy-done.4
  13.8 0.0 copy-start.6
  13.8 11.9 %aggregate_own.1 = (f32[2048,256]{1,0:T(8,128)S(1)}, s32[80,128]{1,0:T(8,128)S(1)}, s32[80,128]{1,0:T(8,128)S(1)}, s32[80,128]{1,0:T(8,128)S(1)}, f32[80,128]{1,0:T(8,128)S(1)}, /*index=5*/s32[8,128]{1,0:T(8,128)S(1)}) custom-call(bf16[256,2048]{1,0:T(8,128)(2,1)S(1)} %get-tuple-element.32.own_t_ref, s32[64,128]{1,0:T(8,128)S(1)} %bitcast.12, ...), custom_call_target="tpu_custom_call" | custom-call | flops 8000000000 | bytes 10000000 | tf_op jit(solution)/shard_map/aggregate_own/pallas_call | solution.py:783
  25.7 0.0 copy-start.7
  25.7 0.0 copy-start.8
  25.7 0.0 collective-permute-done.prev_ref
  25.7 0.0 collective-permute-done.1.next_ref
  25.7 0.0 copy-done.6
  25.8 5.8 %aggregate_halo.1 = (bf16[2048,256]{1,0:T(8,128)(2,1)S(1)}, bf16[768,256]{1,0:T(8,128)(2,1)S(1)}, bf16[1280,256]{1,0:T(8,128)(2,1)S(1)}, f32[128,128]{1,0:T(8,128)S(1)}) custom-call(f32[2048,256]{1,0:T(8,128)S(1)} %get-tuple-element.37.part_ref, bf16[1024,256]{1,0:T(8,128)(2,1)S(1)} %collective-permute-done.prev_ref, ...), custom_call_target="tpu_custom_call" | custom-call | tf_op jit(solution)/shard_map/aggregate_halo/pallas_call | solution.py:793
  31.5 0.0 copy-done.7
  31.5 0.0 copy-done.8
  31.5 23.3 %layer_two.1 = (bf16[128,128]{1,0:T(8,128)(2,1)S(1)}, f32[16,256]{1,0:T(8,128)S(1)}, bf16[1344,256]{1,0:T(8,128)(2,1)S(1)}, bf16[768,256]{1,0:T(8,128)(2,1)S(1)}...) custom-call(f32[128,128]{1,0:T(8,128)S(1)} %get-tuple-element.42.tab, ...), custom_call_target="tpu_custom_call" | custom-call | tf_op jit(solution)/shard_map/layer_two/pallas_call | solution.py:807
  54.8 0.1 collective-permute-start.2
  54.9 5.3 %collective-permute-start.3 = (bf16[1344,256]{1,0:T(8,128)(2,1)S(1)}, bf16[1344,256]{1,0:T(8,128)(2,1)S(1)}, u32[]{:S(2)}, u32[]{:S(2)}) collective-permute-start(bf16[1344,256]{1,0:T(8,128)(2,1)S(1)} %get-tuple-element.55), channel_id=1, source_target_pairs={{0,31},{1,0},{2,1},{3,2},{4,3},{5,4},{6,5},{7,6},{8,7},{9,8},{10,9... | collective-permute-start | bytes 2064392 | tf_op jit(solution)/shard_map/ppermute | solution.py:823
  60.2 0.0 copy-start
  60.2 10.1 %scatter_own.1.part_ref = f32[2048,256]{1,0:T(8,128)S(1)} custom-call(s32[80,128]{1,0:T(8,128)S(1)} %get-tuple-element.33.ldst_ref, s32[80,128]{1,0:T(8,128)S(1)} %get-tuple-element.34.lsrc_ref, s32[8,128]{1,0:T(8,128)S(1)} %get-tuple-element.35.num_ref, f32[80,128]{1,0:T(8,128)S(1)} %get-tuple-element.36.lw_ref, ...), custom_call_target="tpu_custom_call" | custom-call | flops 8000000000 | bytes 10000000 | tf_op jit(solution)/shard_map/scatter_own/pallas_call | solution.py:824
  70.3 0.0 collective-permute-done.2.prev_late
  70.3 0.0 collective-permute-done.3.next_late
  70.3 0.0 copy-done
  70.3 10.4 %scatter_peers.1.part_ref = f32[512,256]{1,0:T(8,128)S(1)} custom-call(f32[2048,256]{1,0:T(8,128)S(1)} %scatter_own.1.part_ref, s32[8,128]{1,0:T(8,128)S(1)} %get-tuple-element.46.num_ref, s32[2048]{0:T(1024)S(1)} %bitcast.23, s32[80,128]{1,0:T(8,128)S(1)} %get-tuple-element.48.prev_dst, s32[80,128]{1,0:T(8,128)S(1)} %get-tuple-element.49.prev_src, ...), custom_call_target="tpu_custom_call" | custom-call | tf_op jit(solution)/shard_map/scatter_peers/pallas_call | solution.py:834
  80.7 23.1 %sum_gradients.1.full_ref = f32[512,256]{1,0:T(8,128)S(1)} custom-call(f32[512,256]{1,0:T(8,128)S(1)} %scatter_peers.1.part_ref), custom_call_target="tpu_custom_call" | custom-call | tf_op jit(solution)/shard_map/sum_gradients/pallas_call | solution.py:848
  103.8 0.8 outputs.1
Async XLA Ops:
  0.6 1.0 copy-start.1
  1.7 0.7 copy-start.5
  2.4 11.4 %copy-start.2 = (s32[8192]{0:T(1024)S(1)}, s32[8192]{0:T(1024)}, u32[]{:S(2)}) copy-start(s32[8192]{0:T(1024)} %param.13) | copy-start | bytes 98308
  2.4 11.4 %copy-start.3 = (s32[8192]{0:T(1024)S(1)}, s32[8192]{0:T(1024)}, u32[]{:S(2)}) copy-start(s32[8192]{0:T(1024)} %param.14) | copy-start | bytes 98308
  2.4 11.4 %copy-start.4 = (f32[8192]{0:T(1024)S(1)}, f32[8192]{0:T(1024)}, u32[]{:S(2)}) copy-start(f32[8192]{0:T(1024)} %param.15) | copy-start | bytes 98308
  7.2 18.5 %collective-permute-start = (bf16[1024,256]{1,0:T(8,128)(2,1)S(1)}, bf16[1024,256]{1,0:T(8,128)(2,1)S(1)}, u32[]{:S(2)}, u32[]{:S(2)}) collective-permute-start(bf16[1024,256]{1,0:T(8,128)(2,1)S(1)} %get-tuple-element.38), channel_id=1, source_target_pairs={{0,1},{1,2},{2,3},{3,4},{4,5},{5,6},{6,7},{7,8},{8,9},{9,10},{10,1... | collective-permute-start | bytes 1572872 | tf_op jit(solution)/shard_map/ppermute | solution.py:777
  7.8 17.9 %collective-permute-start.1 = (bf16[1024,256]{1,0:T(8,128)(2,1)S(1)}, bf16[1024,256]{1,0:T(8,128)(2,1)S(1)}, u32[]{:S(2)}, u32[]{:S(2)}) collective-permute-start(bf16[1024,256]{1,0:T(8,128)(2,1)S(1)} %get-tuple-element.39), channel_id=1, source_target_pairs={{0,31},{1,0},{2,1},{3,2},{4,3},{5,4},{6,5},{7,6},{8,7},{9,8},{10,9... | collective-permute-start | bytes 1572872 | tf_op jit(solution)/shard_map/ppermute | solution.py:778
  13.8 12.0 %copy-start.6 = (f32[256,7]{0,1:T(8,128)S(1)}, f32[256,7]{0,1:T(8,128)}, u32[]{:S(2)}) copy-start(f32[256,7]{0,1:T(8,128)} %param.11) | copy-start | bytes 21508
  25.7 5.8 %copy-start.7 = (s32[2048]{0:T(1024)S(1)}, s32[2048]{0:T(1024)}, u32[]{:S(2)}) copy-start(s32[2048]{0:T(1024)} %param.16) | copy-start | bytes 24580
  25.7 5.8 %copy-start.8 = (s32[2048]{0:T(1024)S(1)}, s32[2048]{0:T(1024)}, u32[]{:S(2)}) copy-start(s32[2048]{0:T(1024)} %param.17) | copy-start | bytes 24580
  54.8 15.5 %collective-permute-start.2 = (bf16[1344,256]{1,0:T(8,128)(2,1)S(1)}, bf16[1344,256]{1,0:T(8,128)(2,1)S(1)}, u32[]{:S(2)}, u32[]{:S(2)}) collective-permute-start(bf16[1344,256]{1,0:T(8,128)(2,1)S(1)} %get-tuple-element.55), channel_id=1, source_target_pairs={{0,1},{1,2},{2,3},{3,4},{4,5},{5,6},{6,7},{7,8},{8,9},{9,10},{10,1... | collective-permute-start | bytes 2064392 | tf_op jit(solution)/shard_map/ppermute | solution.py:822
  54.9 15.4 %collective-permute-start.3 = (bf16[1344,256]{1,0:T(8,128)(2,1)S(1)}, bf16[1344,256]{1,0:T(8,128)(2,1)S(1)}, u32[]{:S(2)}, u32[]{:S(2)}) collective-permute-start(bf16[1344,256]{1,0:T(8,128)(2,1)S(1)} %get-tuple-element.55), channel_id=1, source_target_pairs={{0,31},{1,0},{2,1},{3,2},{4,3},{5,4},{6,5},{7,6},{8,7},{9,8},{10,9... | collective-permute-start | bytes 2064392 | tf_op jit(solution)/shard_map/ppermute | solution.py:823
  60.2 10.1 %copy-start = (bf16[2048,500]{0,1:T(8,128)(2,1)S(1)}, bf16[2048,500]{0,1:T(8,128)(2,1)}, u32[]{:S(2)}) copy-start(bf16[2048,500]{0,1:T(8,128)(2,1)} %param.9) | copy-start | bytes 6144004

commit v8 on v7

--- a/solution.py
+++ b/solution.py
@@ -452,16 +452,13 @@
     return jnp.broadcast_to(lax.shift_right_logical(idx, 7), (CLASS_ROWS, idx.shape[1]))
 
 
-def pick_cols(table_b, pieces, idx, hot, first=0):
-    cols = jnp.dot(table_b, hot, preferred_element_type=F32)
-    rows = table_b.shape[0] // pieces
+def pick_cols(table_b, idx, hot, first=0):
+    pieces = table_b.shape[1] // LANES
+    cols = jnp.dot(table_b, jnp.concatenate([hot] * pieces, axis=0), preferred_element_type=F32)
     hi = hi_of(idx) - first
     out = jnp.zeros(hi.shape, F32)
-    for h in range(rows // CLASS_ROWS):
-        part = cols[h * CLASS_ROWS:(h + 1) * CLASS_ROWS]
-        for p in range(1, pieces):
-            part = part + cols[p * rows + h * CLASS_ROWS:p * rows + (h + 1) * CLASS_ROWS]
-        out = out + jnp.where(hi == h, part, 0.0)
+    for h in range(table_b.shape[0] // CLASS_ROWS):
+        out = out + jnp.where(hi == h, cols[h * CLASS_ROWS:(h + 1) * CLASS_ROWS], 0.0)
     return out
 
 
@@ -487,7 +484,7 @@
 
 
 def stack_pieces(val):
-    return jnp.concatenate(three_pieces(val), axis=0).astype(BF16)
+    return jnp.concatenate(three_pieces(val), axis=1).astype(BF16)
 
 
 def k3_body(num_dev, tab_ref, send_ref, src_ref, dst_ref, w_ref, lab_ref, mask_ref, hid_ref, pos_ref, pos_late_ref,
@@ -529,7 +526,7 @@
     hot_send = [lo_hot(send_ref[r:r + 1, :]) for r in range(2)]
     copies = []
     for r in (1, 0):
-        val = pick_cols(own_b, 1, send_ref[r:r + 1, :], hot_send[r])
+        val = pick_cols(own_b, send_ref[r:r + 1, :], hot_send[r])
         fwd_send[r] = jnp.concatenate([val, jnp.zeros_like(val)], axis=0).astype(BF16)
         copy = remote(fwd_send.at[r], fwd_recv.at[1 - r], sems, r, nxt if r == 1 else prv)
         copy.start()
@@ -557,7 +554,7 @@
 
     def own_forward(i, carry):
         src = wide_row(src_ref, pl.multiple_of(i * STEP_ROWS, STEP_ROWS))
-        vals[i] = pick_cols(ext_b[0:own_hi * CLASS_ROWS, :], 1, src, lo_hot(src))
+        vals[i] = pick_cols(ext_b[0:own_hi * CLASS_ROWS, :], src, lo_hot(src))
         return carry
 
     lax.fori_loop(0, steps, own_forward, 0)
@@ -573,7 +570,7 @@
     def forward(i, carry):
         first = pl.multiple_of(i * STEP_ROWS, STEP_ROWS)
         src, dst = wide_row(src_ref, first), wide_row(dst_ref, first)
-        val = vals[i] + pick_cols(ext_b[own_hi * CLASS_ROWS:, :], 1, src, lo_hot(src), own_hi)
+        val = vals[i] + pick_cols(ext_b[own_hi * CLASS_ROWS:, :], src, lo_hot(src), own_hi)
         val = val * wide_row(w_ref, first)
         acc_z[...] += add_cols(val, dst, lo_hot(dst), own_hi)
         return carry
@@ -603,7 +600,7 @@
     def backward(i, carry):
         first = pl.multiple_of(i * STEP_ROWS, STEP_ROWS)
         src, dst = wide_row(src_ref, first), wide_row(dst_ref, first)
-        val = pick_cols(dz_b[...], 3, dst, lo_hot(dst)) * wide_row(w_ref, first)
+        val = pick_cols(dz_b[...], dst, lo_hot(dst)) * wide_row(w_ref, first)
         vals[i] = val
         acc_s[...] += add_cols(val, src, lo_hot(src), 2 * halo_hi, own_hi)
         return carry
@@ -813,7 +810,7 @@
                             scr(BF16, 2, 16, halo), scr(BF16, 2, 16, halo), scr(F32, 2, CLASS_ROWS, halo),
                             scr(F32, 2, CLASS_ROWS, halo), scr(F32, edges // (STEP_ROWS * LANES), CLASS_ROWS, STEP_ROWS * LANES),
                             scr(F32, own_hi * 24, LANES), scr(F32, 2 * halo // LANES * 24, LANES),
-                            scr(F32, own_hi * 24, LANES), scr(F32, own_hi * 24, LANES), scr(BF16, 3 * own_hi * CLASS_ROWS, LANES),
+                            scr(F32, own_hi * 24, LANES), scr(F32, own_hi * 24, LANES), scr(BF16, own_hi * CLASS_ROWS, 3 * LANES),
                             scr(F32, 2, 8, LANES), scr(F32, PLANE + num_z - 2, 8, LANES),
                             dma(4), dma(PLANE + num_z - 2), dma(6), dma(6)],
             compiler_params=params(1), name="layer_two",

time: 106 us -> 105 us (level); the launches traced: 105 us -> 106 us
  Pallas kernels: 90.1 us -> 91.6 us
    pallas_call x1, Pallas kernels: 11.9 us -> 16.1 us  [device_step(): pl.pallas_call(k2a_body, out_shape=(arr(F32, rows, width),) + lists_in, i...]
    pallas_call x1, Pallas kernels: 10.1 us -> 14.3 us  [device_step(): pl.pallas_call(k4a_body, out_shape=arr(F32, rows, width), in_specs=[hbm()...]
    pallas_call x1, Pallas kernels: 23.1 us -> 19.4 us  [device_step(): pl.pallas_call(functools.partial(k5_body, num_dev), out_shape=arr(F32, su...]
    pallas_call x1, Pallas kernels: 23.3 us -> 20.4 us  [device_step(): pl.pallas_call(functools.partial(k3_body, num_dev), out_shape=(tab_b, arr...]
  transfers between devices with their start and end apart: 4 -> 4, of which waited for: 0 -> 0; matrix products, arithmetic and copies ran while one was open for 0% -> 0% of each run, Pallas kernels for 21% -> 29%
where the time goes in v8:
time: 105 us; the launch traced here: 106 us
  Pallas kernels  91.6 us (87%)
  starting transfers between devices  11.9 us (11%)
  local copies, waits for them, and re-layouts  1.76 us (2%)
    pallas_call x1, Pallas kernels, device_step(): pl.pallas_call(functools.partial(k3_body, num_dev), out_shape=(tab_b, arr...  20.4 us
    pallas_call x1, Pallas kernels, device_step(): pl.pallas_call(functools.partial(k5_body, num_dev), out_shape=arr(F32, su...  19.4 us
    pallas_call x1, Pallas kernels, device_step(): pl.pallas_call(k2a_body, out_shape=(arr(F32, rows, width),) + lists_in, i...  16.1 us
    pallas_call x1, Pallas kernels, device_step(): pl.pallas_call(k4a_body, out_shape=arr(F32, rows, width), in_specs=[hbm()...  14.3 us
    pallas_call x1, Pallas kernels, device_step(): pl.pallas_call(k4b_body, out_shape=arr(F32, sum_rows_pad, width), in_spec...  9.55 us
    pallas_call x1, Pallas kernels, device_step(): pl.pallas_call(k2b_body, out_shape=(arr(BF16, rows, width), arr(BF16, EAR...  6.14 us
    ppermute x1, starting transfers between devices, device_step(): lax.ppermute(to_prev, GRAPH_AXIS, [(g, (g - 1) % num_dev) for g in range(...  5.98 us
    ppermute x1, starting transfers between devices, device_step(): lax.ppermute(late, GRAPH_AXIS, [(g, (g - 1) % num_dev) for g in range(num...  5.33 us
  transfers between devices with their start and end apart: 4, of which 0 were waited for; matrix products, arithmetic and copies ran while one was open for 0% of the time, Pallas kernels for 29%

profile of v8, /device:TPU:0, one launch (start us, length us, event | category | flops | bytes accessed | tf_op | source)
XLA Modules:
  0.0 106.1 jit_solution(3095634384950435785)
XLA Ops:
  0.6 0.0 copy-start.1
  0.6 1.0 copy-done.1
  1.7 0.0 copy-start.5
  1.7 0.7 copy-done.5
  2.4 0.0 copy-start.2
  2.4 0.0 copy-start.3
  2.4 0.0 copy-start.4
  2.4 4.8 %transform.1 = (bf16[256,2048]{1,0:T(8,128)(2,1)S(1)}, bf16[1024,256]{1,0:T(8,128)(2,1)S(1)}, bf16[1024,256]{1,0:T(8,128)(2,1)S(1)}) custom-call(bf16[500,2048]{1,0:T(8,128)(2,1)} %bitcast.10, f32[500,256]{1,0:T(8,128)S(1)} %copy-done.1, s32[2,1024]{1,0:T(2,128)S(1)} %copy-done.5), custom_call_target="tpu_custom_call" | custom-call | tf_op jit(solution)/shard_map/transform/pallas_call | solution.py:766
  7.2 0.6 collective-permute-start
  7.8 6.0 %collective-permute-start.1 = (bf16[1024,256]{1,0:T(8,128)(2,1)S(1)}, bf16[1024,256]{1,0:T(8,128)(2,1)S(1)}, u32[]{:S(2)}, u32[]{:S(2)}) collective-permute-start(bf16[1024,256]{1,0:T(8,128)(2,1)S(1)} %get-tuple-element.39), channel_id=1, source_target_pairs={{0,31},{1,0},{2,1},{3,2},{4,3},{5,4},{6,5},{7,6},{8,7},{9,8},{10,9... | collective-permute-start | bytes 1572872 | tf_op jit(solution)/shard_map/ppermute | solution.py:775
  13.8 0.0 copy-done.2
  13.8 0.0 copy-done.3
  13.8 0.0 copy-done.4
  13.8 0.0 copy-start.6
  13.8 16.1 %aggregate_own.1 = (f32[2048,256]{1,0:T(8,128)S(1)}, s32[80,128]{1,0:T(8,128)S(1)}, s32[80,128]{1,0:T(8,128)S(1)}, s32[80,128]{1,0:T(8,128)S(1)}, f32[80,128]{1,0:T(8,128)S(1)}, /*index=5*/s32[8,128]{1,0:T(8,128)S(1)}) custom-call(bf16[256,2048]{1,0:T(8,128)(2,1)S(1)} %get-tuple-element.32.own_t_ref, s32[64,128]{1,0:T(8,128)S(1)} %bitcast.12, ...), custom_call_target="tpu_custom_call" | custom-call | flops 8000000000 | bytes 10000000 | tf_op jit(solution)/shard_map/aggregate_own/pallas_call | solution.py:780
  29.9 0.0 copy-start.7
  29.9 0.0 copy-start.8
  29.9 0.0 collective-permute-done.prev_ref
  29.9 0.0 collective-permute-done.1.next_ref
  29.9 0.0 copy-done.6
  30.0 6.1 %aggregate_halo.1 = (bf16[2048,256]{1,0:T(8,128)(2,1)S(1)}, bf16[768,256]{1,0:T(8,128)(2,1)S(1)}, bf16[1280,256]{1,0:T(8,128)(2,1)S(1)}, f32[128,128]{1,0:T(8,128)S(1)}) custom-call(f32[2048,256]{1,0:T(8,128)S(1)} %get-tuple-element.37.part_ref, bf16[1024,256]{1,0:T(8,128)(2,1)S(1)} %collective-permute-done.prev_ref, ...), custom_call_target="tpu_custom_call" | custom-call | tf_op jit(solution)/shard_map/aggregate_halo/pallas_call | solution.py:790
  36.1 0.0 copy-done.7
  36.1 0.0 copy-done.8
  36.1 20.4 %layer_two.1 = (bf16[128,128]{1,0:T(8,128)(2,1)S(1)}, f32[16,256]{1,0:T(8,128)S(1)}, bf16[1344,256]{1,0:T(8,128)(2,1)S(1)}, bf16[768,256]{1,0:T(8,128)(2,1)S(1)}...) custom-call(f32[128,128]{1,0:T(8,128)S(1)} %get-tuple-element.42.tab, ...), custom_call_target="tpu_custom_call" | custom-call | tf_op jit(solution)/shard_map/layer_two/pallas_call | solution.py:804
  56.5 0.1 collective-permute-start.2
  56.6 5.3 %collective-permute-start.3 = (bf16[1344,256]{1,0:T(8,128)(2,1)S(1)}, bf16[1344,256]{1,0:T(8,128)(2,1)S(1)}, u32[]{:S(2)}, u32[]{:S(2)}) collective-permute-start(bf16[1344,256]{1,0:T(8,128)(2,1)S(1)} %get-tuple-element.55), channel_id=1, source_target_pairs={{0,31},{1,0},{2,1},{3,2},{4,3},{5,4},{6,5},{7,6},{8,7},{9,8},{10,9... | collective-permute-start | bytes 2064392 | tf_op jit(solution)/shard_map/ppermute | solution.py:820
  61.9 0.0 copy-start
  61.9 14.3 %scatter_own.1.part_ref = f32[2048,256]{1,0:T(8,128)S(1)} custom-call(s32[80,128]{1,0:T(8,128)S(1)} %get-tuple-element.33.ldst_ref, s32[80,128]{1,0:T(8,128)S(1)} %get-tuple-element.34.lsrc_ref, s32[8,128]{1,0:T(8,128)S(1)} %get-tuple-element.35.num_ref, f32[80,128]{1,0:T(8,128)S(1)} %get-tuple-element.36.lw_ref, ...), custom_call_target="tpu_custom_call" | custom-call | flops 8000000000 | bytes 10000000 | tf_op jit(solution)/shard_map/scatter_own/pallas_call | solution.py:821
  76.2 0.0 collective-permute-done.2.prev_late
  76.2 0.0 collective-permute-done.3.next_late
  76.2 0.0 copy-done
  76.2 9.6 %scatter_peers.1.part_ref = f32[512,256]{1,0:T(8,128)S(1)} custom-call(f32[2048,256]{1,0:T(8,128)S(1)} %scatter_own.1.part_ref, s32[8,128]{1,0:T(8,128)S(1)} %get-tuple-element.46.num_ref, s32[2048]{0:T(1024)S(1)} %bitcast.23, s32[80,128]{1,0:T(8,128)S(1)} %get-tuple-element.48.prev_dst, s32[80,128]{1,0:T(8,128)S(1)} %get-tuple-element.49.prev_src, ...), custom_call_target="tpu_custom_call" | custom-call | tf_op jit(solution)/shard_map/scatter_peers/pallas_call | solution.py:831
  85.8 19.4 %sum_gradients.1.full_ref = f32[512,256]{1,0:T(8,128)S(1)} custom-call(f32[512,256]{1,0:T(8,128)S(1)} %scatter_peers.1.part_ref), custom_call_target="tpu_custom_call" | custom-call | tf_op jit(solution)/shard_map/sum_gradients/pallas_call | solution.py:845
  105.2 0.8 outputs.1
Async XLA Ops:
  0.6 1.0 copy-start.1
  1.7 0.7 copy-start.5
  2.4 11.4 %copy-start.2 = (s32[8192]{0:T(1024)S(1)}, s32[8192]{0:T(1024)}, u32[]{:S(2)}) copy-start(s32[8192]{0:T(1024)} %param.13) | copy-start | bytes 98308
  2.4 11.4 %copy-start.3 = (s32[8192]{0:T(1024)S(1)}, s32[8192]{0:T(1024)}, u32[]{:S(2)}) copy-start(s32[8192]{0:T(1024)} %param.14) | copy-start | bytes 98308
  2.4 11.4 %copy-start.4 = (f32[8192]{0:T(1024)S(1)}, f32[8192]{0:T(1024)}, u32[]{:S(2)}) copy-start(f32[8192]{0:T(1024)} %param.15) | copy-start | bytes 98308
  7.2 22.7 %collective-permute-start = (bf16[1024,256]{1,0:T(8,128)(2,1)S(1)}, bf16[1024,256]{1,0:T(8,128)(2,1)S(1)}, u32[]{:S(2)}, u32[]{:S(2)}) collective-permute-start(bf16[1024,256]{1,0:T(8,128)(2,1)S(1)} %get-tuple-element.38), channel_id=1, source_target_pairs={{0,1},{1,2},{2,3},{3,4},{4,5},{5,6},{6,7},{7,8},{8,9},{9,10},{10,1... | collective-permute-start | bytes 1572872 | tf_op jit(solution)/shard_map/ppermute | solution.py:774
  7.8 22.1 %collective-permute-start.1 = (bf16[1024,256]{1,0:T(8,128)(2,1)S(1)}, bf16[1024,256]{1,0:T(8,128)(2,1)S(1)}, u32[]{:S(2)}, u32[]{:S(2)}) collective-permute-start(bf16[1024,256]{1,0:T(8,128)(2,1)S(1)} %get-tuple-element.39), channel_id=1, source_target_pairs={{0,31},{1,0},{2,1},{3,2},{4,3},{5,4},{6,5},{7,6},{8,7},{9,8},{10,9... | collective-permute-start | bytes 1572872 | tf_op jit(solution)/shard_map/ppermute | solution.py:775
  13.8 16.2 %copy-start.6 = (f32[256,7]{0,1:T(8,128)S(1)}, f32[256,7]{0,1:T(8,128)}, u32[]{:S(2)}) copy-start(f32[256,7]{0,1:T(8,128)} %param.11) | copy-start | bytes 21508
  29.9 6.2 %copy-start.7 = (s32[2048]{0:T(1024)S(1)}, s32[2048]{0:T(1024)}, u32[]{:S(2)}) copy-start(s32[2048]{0:T(1024)} %param.16) | copy-start | bytes 24580
  29.9 6.2 %copy-start.8 = (s32[2048]{0:T(1024)S(1)}, s32[2048]{0:T(1024)}, u32[]{:S(2)}) copy-start(s32[2048]{0:T(1024)} %param.17) | copy-start | bytes 24580
  56.5 19.7 %collective-permute-start.2 = (bf16[1344,256]{1,0:T(8,128)(2,1)S(1)}, bf16[1344,256]{1,0:T(8,128)(2,1)S(1)}, u32[]{:S(2)}, u32[]{:S(2)}) collective-permute-start(bf16[1344,256]{1,0:T(8,128)(2,1)S(1)} %get-tuple-element.55), channel_id=1, source_target_pairs={{0,1},{1,2},{2,3},{3,4},{4,5},{5,6},{6,7},{7,8},{8,9},{9,10},{10,1... | collective-permute-start | bytes 2064392 | tf_op jit(solution)/shard_map/ppermute | solution.py:819
  56.6 19.6 %collective-permute-start.3 = (bf16[1344,256]{1,0:T(8,128)(2,1)S(1)}, bf16[1344,256]{1,0:T(8,128)(2,1)S(1)}, u32[]{:S(2)}, u32[]{:S(2)}) collective-permute-start(bf16[1344,256]{1,0:T(8,128)(2,1)S(1)} %get-tuple-element.55), channel_id=1, source_target_pairs={{0,31},{1,0},{2,1},{3,2},{4,3},{5,4},{6,5},{7,6},{8,7},{9,8},{10,9... | collective-permute-start | bytes 2064392 | tf_op jit(solution)/shard_map/ppermute | solution.py:820
  61.9 14.3 %copy-start = (bf16[2048,500]{0,1:T(8,128)(2,1)S(1)}, bf16[2048,500]{0,1:T(8,128)(2,1)}, u32[]{:S(2)}) copy-start(bf16[2048,500]{0,1:T(8,128)(2,1)} %param.9) | copy-start | bytes 6144004
